TPU v7x, 512 devices: a whole 4x4x16 slice. The times are simulated.
512 devices in a mesh: gz: 8 (over x, y_lo), xy: 64 (over z, y_hi, core).
Axes of the slice: x: 4, y: 4 (y_hi: 2, y_lo: 2; y = y_hi * 2 + y_lo), z: 16, core: 2. Of those that a mesh axis runs over, the one named last changes fastest.
Arguments:
- fixed: float32 [64, 1024, 1024], P('gz', 'xy'), may hold values from -6 to 6
- moving: float32 [64, 1024, 1024], P('gz', 'xy'), may hold values from -9 to 9
Outputs:
- update: float32 [3, 64, 1024, 1024], P(None, 'gz', 'xy')
All inputs are finite; a program needn't handle non-finite values.
Results may differ from a plain program's by a relative error of at most 0.00016.
Values sent between devices are 32-bit elements; how exact they have to be, the bound alone decides.
No kernel may reach another device: no remote copies, remote signals or barrier semaphores. Data moves between devices by JAX's collectives and lax.ppermute only.
A program may use at most 64 MiB of HBM per device.

v0:
```python
import functools

import jax
import jax.numpy as jnp
from jax import lax
from jax.sharding import Mesh
from jax.sharding import PartitionSpec as P

RADIUS = 4
SPACING = 8
XY = ("xy_0", "xy_1", "xy_2")
GZ = ("gz_0", "gz_1")
GZ_XY = ("gz_0", "gz_1", "xy_0", "xy_1", "xy_2")


HIGH = lax.Precision.HIGHEST
EPS = 1e-05


def from_behind(block, axis, distance):
    devices = range(lax.axis_size(axis))
    route = [(i - distance, i) for i in devices if i - distance in devices]
    return lax.ppermute(block, axis, route)


def extended(block, sides, width):
    for axis, dim in sides:
        count = lax.axis_size(axis)
        forward = [(i, i + 1) for i in range(count - 1)]
        backward = [(target, source) for source, target in forward]
        low = lax.ppermute(
            lax.slice_in_dim(block, block.shape[dim] - width, None, axis=dim), axis, forward
        )
        high = lax.ppermute(lax.slice_in_dim(block, 0, width, axis=dim), axis, backward)
        block = jnp.concatenate([low, block, high], axis=dim)
    return block


def one_axis_at_a_time(x, axes):
    return functools.reduce(lax.psum, axes, x)


def basis(index, knot):
    span = index // SPACING
    frac = (index - span * SPACING).astype(jnp.float32) / SPACING
    offset = knot - span
    other = 1.0 - frac
    first = other * other * other / 6.0
    second = (3.0 * frac**3 - 6.0 * frac**2 + 4.0) / 6.0
    third = (-3.0 * frac**3 + 3.0 * frac**2 + 3.0 * frac + 1.0) / 6.0
    fourth = frac**3 / 6.0
    zero = jnp.zeros_like(frac)
    return jnp.where(
        offset == 0,
        first,
        jnp.where(
            offset == 1, second, jnp.where(offset == 2, third, jnp.where(offset == 3, fourth, zero))
        ),
    )


def square_total(index):
    span = index // SPACING
    total = basis(index, span) ** 2
    for step in range(1, 4):
        total = total + basis(index, span + step) ** 2
    return total


def fit_matrix(index, knot):
    value = basis(index, knot)
    return value * value * value / square_total(index)


def knot_mass(knot, extent):
    spans = extent // SPACING
    within = jnp.arange(SPACING)
    offsets = jnp.arange(4)
    energy = jnp.sum(basis(within[None, :], offsets[:, None]) ** 2, axis=1)
    start = knot[:, None] - offsets[None, :]
    valid = (start >= 0) & (start <= spans - 1)
    return jnp.sum(jnp.where(valid, energy[None, :], jnp.zeros_like(energy)[None, :]), axis=1)


def window_sum(padded, shape):
    depth, rows, width = shape
    span = 2 * RADIUS + 1
    acc = padded[0:depth]
    for step in range(1, span):
        acc = acc + padded[step : step + depth]
    out = acc[:, 0:rows]
    for step in range(1, span):
        out = out + acc[:, step : step + rows]
    res = out[:, :, 0:width]
    for step in range(1, span):
        res = res + out[:, :, step : step + width]
    return res


def cc_force(fpad, mpad, shape):
    depth, rows, width = shape
    count = float((2 * RADIUS + 1) ** 3)
    sum_f = window_sum(fpad, shape)
    sum_m = window_sum(mpad, shape)
    sum_ff = window_sum(fpad * fpad, shape)
    sum_mm = window_sum(mpad * mpad, shape)
    sum_fm = window_sum(fpad * mpad, shape)
    r = RADIUS
    centre_f = fpad[r : r + depth, r : r + rows, r : r + width]
    centre_m = mpad[r : r + depth, r : r + rows, r : r + width]
    grad_z = (
        mpad[r + 1 : r + 1 + depth, r : r + rows, r : r + width]
        - mpad[r - 1 : r - 1 + depth, r : r + rows, r : r + width]
    ) * 0.5
    grad_y = (
        mpad[r : r + depth, r + 1 : r + 1 + rows, r : r + width]
        - mpad[r : r + depth, r - 1 : r - 1 + rows, r : r + width]
    ) * 0.5
    grad_x = (
        mpad[r : r + depth, r : r + rows, r + 1 : r + 1 + width]
        - mpad[r : r + depth, r : r + rows, r - 1 : r - 1 + width]
    ) * 0.5
    mean_f = sum_f / count
    mean_m = sum_m / count
    cov = sum_fm / count - mean_f * mean_m
    var_f = sum_ff / count - mean_f * mean_f
    var_m = sum_mm / count - mean_m * mean_m
    factor = 2.0 * cov / (var_f * var_m + EPS)
    resid = centre_f - mean_f - cov / (var_m + EPS) * (centre_m - mean_m)
    common = factor * resid
    return jnp.stack([common * grad_z, common * grad_y, common * grad_x])


def shifted_pads(block, offset):
    knots = block.shape[0]
    rest = ((0, 0),) * (block.ndim - 1)
    lower = ((0, offset),) + rest
    upper = ((offset, 0),) + rest
    return (lower, upper, knots)


def fold_rows(block, span, devices):
    reach = min((span + 2) // span, devices - 1)
    total = block
    for dist in range(1, reach + 1):
        offset = dist * span
        lower, upper, knots = shifted_pads(block, offset)
        below = from_behind(block, XY, dist)
        above = from_behind(block, XY, -dist)
        total = total + jnp.pad(below[offset:], lower) + jnp.pad(above[: knots - offset], upper)
    return total


def fold_planes(block, span, devices):
    reach = min((span + 2) // span, devices - 1)
    total = block
    for dist in range(1, reach + 1):
        offset = dist * span
        lower, upper, knots = shifted_pads(block, offset)
        below = from_behind(block, GZ, dist)
        above = from_behind(block, GZ, -dist)
        total = total + jnp.pad(below[offset:], lower) + jnp.pad(above[: knots - offset], upper)
    return total


def shards(fixed, moving):
    depth, rows, width = fixed.shape
    slab = lax.axis_index(GZ)
    strip = lax.axis_index(XY)
    slabs_all = lax.axis_size(GZ)
    strips_all = lax.axis_size(XY)
    span_z = depth // SPACING
    span_y = rows // SPACING
    knots_z = span_z + 3
    knots_y = span_y + 3
    knots_x = width // SPACING + 3
    stacked = jnp.stack([fixed, moving])
    rimmed = extended(stacked, ((GZ, 1), (XY, 2)), RADIUS)
    rimmed = jnp.pad(rimmed, ((0, 0), (0, 0), (0, 0), (RADIUS, RADIUS)))
    force = cc_force(rimmed[0], rimmed[1], (depth, rows, width))
    vox_x = jnp.arange(width)
    ctl_x = jnp.arange(knots_x)
    fit_x = fit_matrix(vox_x[:, None], ctl_x[None, :])
    reduced = jnp.dot(force.reshape(-1, width), fit_x, precision=HIGH).reshape(
        3, depth, rows, knots_x
    )
    vox_z = slab * depth + jnp.arange(depth)
    vox_y = strip * rows + jnp.arange(rows)
    ctl_z = slab * span_z + jnp.arange(knots_z)
    ctl_y = strip * span_y + jnp.arange(knots_y)
    own_fit_y = fit_matrix(vox_y[None, :], ctl_y[:, None])
    own_fit_z = fit_matrix(vox_z[None, :], ctl_z[:, None])
    row_data = reduced.transpose(2, 0, 1, 3).reshape(rows, -1)
    row_terms = jnp.dot(own_fit_y, row_data, precision=HIGH).reshape(knots_y, 3, depth, knots_x)
    row_block = fold_rows(row_terms, span_y, strips_all)
    plane_data = row_block.transpose(2, 0, 1, 3).reshape(depth, -1)
    plane_terms = jnp.dot(own_fit_z, plane_data, precision=HIGH).reshape(
        knots_z, knots_y, 3, knots_x
    )
    numer = fold_planes(plane_terms, span_z, slabs_all)
    mass_z = knot_mass(ctl_z, depth * slabs_all)
    mass_y = knot_mass(ctl_y, rows * strips_all)
    mass_x = knot_mass(ctl_x, width)
    coef = numer / (
        mass_z[:, None, None, None] * mass_y[None, :, None, None] * mass_x[None, None, None, :]
    )
    eval_x = basis(vox_x[:, None], ctl_x[None, :])
    eval_y = basis(vox_y[:, None], ctl_y[None, :])
    eval_z = basis(vox_z[:, None], ctl_z[None, :])
    field = jnp.dot(coef.reshape(-1, knots_x), eval_x.T, precision=HIGH).reshape(
        knots_z, knots_y, 3, width
    )
    field = jnp.einsum("yb,abkx->aykx", eval_y, field, precision=HIGH)
    field = jnp.einsum("za,aykx->kzyx", eval_z, field, precision=HIGH)
    partial_power = jnp.sum(field * field)
    total_power = one_axis_at_a_time(partial_power, GZ_XY)
    power = total_power / (field.size * slabs_all * strips_all)
    return field / (jnp.sqrt(power) + 1e-06)


def solution(mesh):
    torus = Mesh(mesh.devices.reshape(4, 2, 16, 2, 2), ("gz_0", "gz_1", "xy_0", "xy_1", "xy_2"))
    placed = (P(GZ, XY, None), P(GZ, XY, None))
    return jax.shard_map(
        shards, mesh=torus, in_specs=placed, out_specs=P(None, GZ, XY, None), check_vma=False
    )
```

profile of v0, /device:TPU:1, one launch (start us, length us, event | category | flops | bytes accessed | tf_op | source)
XLA Modules:
  0.0 181.4 jit_solution(6793122535438666444)
XLA Ops:
  1.4 4.1 %collective-permute-start = (f32[2,4,16,1024]{3,2,1,0:T(8,128)S(1)}, f32[2,4,16,1024]{3,2,1,0:T(8,128)S(1)}, u32[]{:S(2)}, u32[]{:S(2)}) collective-permute-start(f32[2,4,16,1024]{3,2,1,0:T(8,128)S(1)} %get-tuple-element.18), channel_id=1, source_target_pairs={{0,64},{64,128},{128,192},{192,256},{256,320},{320,384},{384,448},... | collective-permute-start | bytes 1572872 | tf_op jit(solution)/shard_map/ppermute | solution.py:31
  7.1 17.2 %collective-permute-done = f32[2,4,16,1024]{3,2,1,0:T(8,128)S(1)} collective-permute-done((f32[2,4,16,1024]{3,2,1,0:T(8,128)S(1)}, f32[2,4,16,1024]{3,2,1,0:T(8,128)S(1)}, u32[]{:S(2)}, u32[]{:S(2)}) %collective-permute-start) | collective-permute-done | bytes 524320 | tf_op jit(solution)/shard_map/ppermute | solution.py:31
  24.6 8.8 %collective-permute-start.2 = (f32[2,16,4,1024]{3,2,1,0:T(4,128)S(1)}, f32[2,16,4,1024]{3,2,1,0:T(4,128)S(1)}, u32[]{:S(2)}, u32[]{:S(2)}) collective-permute-start(f32[2,16,4,1024]{3,2,1,0:T(4,128)S(1)} %get-tuple-element.16), channel_id=1, source_target_pairs={{0,1},{1,2},{2,3},{3,4},{4,5},{5,6},{6,7},{7,8},{8,9},{9,10},{10,1... | collective-permute-start | bytes 1572872 | tf_op jit(solution)/shard_map/ppermute | solution.py:31
  33.4 1.9 %collective-permute-start.3 = (f32[2,16,4,1024]{3,2,1,0:T(4,128)S(1)}, f32[2,16,4,1024]{3,2,1,0:T(4,128)S(1)}, u32[]{:S(2)}, u32[]{:S(2)}) collective-permute-start(f32[2,16,4,1024]{3,2,1,0:T(4,128)S(1)} %get-tuple-element.17), channel_id=1, source_target_pairs={{1,0},{2,1},{3,2},{4,3},{5,4},{6,5},{7,6},{8,7},{9,8},{10,9},{11,1... | collective-permute-start | bytes 1572872 | tf_op jit(solution)/shard_map/ppermute | solution.py:34
  35.7 9.4 %collective-permute-done.2 = f32[2,16,4,1024]{3,2,1,0:T(4,128)S(1)} collective-permute-done((f32[2,16,4,1024]{3,2,1,0:T(4,128)S(1)}, f32[2,16,4,1024]{3,2,1,0:T(4,128)S(1)}, u32[]{:S(2)}, u32[]{:S(2)}) %collective-permute-start.2) | collective-permute-done | bytes 524320 | tf_op jit(solution)/shard_map/ppermute | solution.py:31
  45.4 3.9 %select_maximum_fusion = f32[2,16,24,1032]{3,2,1,0:T(8,128)S(1)} fusion(f32[2,16,4,1024]{3,2,1,0:T(4,128)S(1)} %collective-permute-done.3, f32[2,16,4,1024]{3,2,1,0:T(4,128)S(1)} %collective-permute-done.2, f32[2,4,16,1024]{3,2,1,0:T(8,128)S(1)} %collective-permute-done.1, f32[2,4,16,1024]{3,2,1,0:T(8,128)S(1)} %collective-permute-done, ...), kind=kLoop, calls=%fused_computation.2 | loop fusion | flops 11096064 | bytes 6316032 | tf_op jit(solution)/shard_map/concatenate | solution.py:35
  53.2 6.3 %fusion.32 = (f32[1,8,16,1024]{3,2,1,0:T(8,128)S(1)}, f32[8,16,1024]{2,1,0:T(8,128)S(1)}) fusion(f32[16,24,1032]{2,1,0:T(8,128)S(1)} %get-tuple-element.13, f32[16,24,1032]{2,1,0:T(8,128)S(1)} %get-tuple-element.12, f32[8,16,1032]{2,1,0:T(8,128)S(1)} %slice_add_fusion.40, f32[8,16,1032]{2,1,0:T(8,128)S(1)} %slice_add_fusion.48, ...), kind=kLoop, calls=%fused_computation.129 | loop fusion | flops 8519680 | bytes 26738688 | tf_op jit(solution)/shard_map/stack | solution.py:131
  60.2 1.5 fusion.7
  62.9 5.6 %collective-permute-start.4 = (f32[5,3,8,131]{3,0,2,1:T(8,128)S(1)}, f32[5,3,8,131]{3,0,2,1:T(8,128)S(1)}, u32[]{:S(2)}, u32[]{:S(2)}) collective-permute-start(f32[5,3,8,131]{3,0,2,1:T(8,128)S(1)} %fusion.47), channel_id=1, source_target_pairs={{0,1},{1,2},{2,3},{3,4},{4,5},{5,6},{6,7},{7,8},{8,9},{9,10},{10,1... | collective-permute-start | bytes 188648 | tf_op jit(solution)/shard_map/ppermute | solution.py:23
  68.5 1.9 %collective-permute-start.5 = (f32[5,3,8,131]{3,0,2,1:T(8,128)S(1)}, f32[5,3,8,131]{3,0,2,1:T(8,128)S(1)}, u32[]{:S(2)}, u32[]{:S(2)}) collective-permute-start(f32[5,3,8,131]{3,0,2,1:T(8,128)S(1)} %fusion.47), channel_id=1, source_target_pairs={{1,0},{2,1},{3,2},{4,3},{5,4},{6,5},{7,6},{8,7},{9,8},{10,9},{11,1... | collective-permute-start | bytes 188648 | tf_op jit(solution)/shard_map/ppermute | solution.py:23
  70.4 2.0 %collective-permute-start.6 = (f32[5,3,8,131]{3,0,2,1:T(8,128)S(1)}, f32[5,3,8,131]{3,0,2,1:T(8,128)S(1)}, u32[]{:S(2)}, u32[]{:S(2)}) collective-permute-start(f32[5,3,8,131]{3,0,2,1:T(8,128)S(1)} %fusion.47), channel_id=1, source_target_pairs={{0,2},{1,3},{2,4},{3,5},{4,6},{5,7},{6,8},{7,9},{8,10},{9,11},{10,... | collective-permute-start | bytes 188648 | tf_op jit(solution)/shard_map/ppermute | solution.py:23
  73.8 3.2 %collective-permute-done.5 = f32[5,3,8,131]{3,0,2,1:T(8,128)S(1)} collective-permute-done((f32[5,3,8,131]{3,0,2,1:T(8,128)S(1)}, f32[5,3,8,131]{3,0,2,1:T(8,128)S(1)}, u32[]{:S(2)}, u32[]{:S(2)}) %collective-permute-start.5) | collective-permute-done | bytes 62912 | tf_op jit(solution)/shard_map/ppermute | solution.py:23
  77.1 4.6 %collective-permute-done.7 = f32[5,3,8,131]{3,0,2,1:T(8,128)S(1)} collective-permute-done((f32[5,3,8,131]{3,0,2,1:T(8,128)S(1)}, f32[5,3,8,131]{3,0,2,1:T(8,128)S(1)}, u32[]{:S(2)}, u32[]{:S(2)}) %collective-permute-start.7) | collective-permute-done | bytes 62912 | tf_op jit(solution)/shard_map/ppermute | solution.py:23
  82.5 3.6 %collective-permute-start.8 = (f32[4,5,3,131]{3,0,2,1:T(4,128)S(1)}, f32[4,5,3,131]{3,0,2,1:T(4,128)S(1)}, u32[]{:S(2)}, u32[]{:S(2)}) collective-permute-start(f32[4,5,3,131]{3,0,2,1:T(4,128)S(1)} %fusion.70), channel_id=1, source_target_pairs={{0,64},{64,128},{128,192},{192,256},{256,320},{320,384},{384,448},... | collective-permute-start | bytes 94328 | tf_op jit(solution)/shard_map/ppermute | solution.py:23
  86.2 3.5 %collective-permute-start.10 = (f32[4,5,3,131]{3,0,2,1:T(4,128)S(1)}, f32[4,5,3,131]{3,0,2,1:T(4,128)S(1)}, u32[]{:S(2)}, u32[]{:S(2)}) collective-permute-start(f32[4,5,3,131]{3,0,2,1:T(4,128)S(1)} %fusion.70), channel_id=1, source_target_pairs={{0,128},{64,192},{128,256},{192,320},{256,384},{320,448},{1,129},{... | collective-permute-start | bytes 94328 | tf_op jit(solution)/shard_map/ppermute | solution.py:23
  91.0 6.1 %collective-permute-start.12 = (f32[4,5,3,131]{3,0,2,1:T(4,128)S(1)}, f32[4,5,3,131]{3,0,2,1:T(4,128)S(1)}, u32[]{:S(2)}, u32[]{:S(2)}) collective-permute-start(f32[4,5,3,131]{3,0,2,1:T(4,128)S(1)} %fusion.70), channel_id=1, source_target_pairs={{0,192},{64,256},{128,320},{192,384},{256,448},{1,193},{65,257},{1... | collective-permute-start | bytes 94328 | tf_op jit(solution)/shard_map/ppermute | solution.py:23
  99.9 3.1 %collective-permute-done.13 = f32[4,5,3,131]{3,0,2,1:T(4,128)S(1)} collective-permute-done((f32[4,5,3,131]{3,0,2,1:T(4,128)S(1)}, f32[4,5,3,131]{3,0,2,1:T(4,128)S(1)}, u32[]{:S(2)}, u32[]{:S(2)}) %collective-permute-start.13) | collective-permute-done | bytes 31472 | tf_op jit(solution)/shard_map/ppermute | solution.py:23
  105.4 2.9 %multiply_reduce_fusion = (f32[]{:T(128)}, f32[16,3,1024,8]{2,3,1,0:T(8,128)S(1)}) fusion(f32[8]{0:T(128)S(1)} %broadcast_multiply_fusion.4, f32[8]{0:T(128)S(1)} %get-tuple-element.24, f32[8]{0:T(128)S(1)} %get-tuple-element.25, f32[8]{0:T(128)S(1)} %get-tuple-element.22, s32[8]{0:T(128)S(1)} %and_select_fusion.2, s32[4]{0:T(128)S(1)} %iota_add_fusion.3, ...), kind=kOutput, calls=%fused_computation.17 | convolution fusion | flops 19661088 | bytes 2359476 | tf_op jit(solution)/shard_map/za,aykx->kzyx/dot_general | solution.py:214
  108.3 10.0 %psum.35 = f32[]{:T(128)} all-reduce(f32[]{:T(128)} %get-tuple-element.20), channel_id=1, replica_groups=mesh['gz_0'=4,'gz_1'=2,'xy_0'=16,'xy_1'=2,'xy_2'=2] {'gz_0'}, use_global_device_ids=true, to_apply=%region_5.6 | all-reduce | flops 1 | bytes 8 | tf_op jit(solution)/shard_map/psum | solution.py:40
  118.3 4.4 %psum.36 = f32[]{:T(128)} all-reduce(f32[]{:T(128)} %psum.35), channel_id=1, replica_groups=mesh['gz_0'=4,'gz_1'=2,'xy_0'=16,'xy_1'=2,'xy_2'=2] {'gz_1'}, use_global_device_ids=true, to_apply=%region_6.7 | all-reduce | flops 1 | bytes 8 | tf_op jit(solution)/shard_map/psum | solution.py:40
  122.7 32.3 %psum.37 = f32[]{:T(128)} all-reduce(f32[]{:T(128)} %psum.36), channel_id=1, replica_groups=mesh['gz_0'=4,'gz_1'=2,'xy_0'=16,'xy_1'=2,'xy_2'=2] {'xy_0'}, use_global_device_ids=true, to_apply=%region_7.8 | all-reduce | flops 1 | bytes 8 | tf_op jit(solution)/shard_map/psum | solution.py:40
  155.0 5.9 %psum.38 = f32[]{:T(128)} all-reduce(f32[]{:T(128)} %psum.37), channel_id=1, replica_groups=mesh['gz_0'=4,'gz_1'=2,'xy_0'=16,'xy_1'=2,'xy_2'=2] {'xy_1'}, use_global_device_ids=true, to_apply=%region_8.9 | all-reduce | flops 1 | bytes 8 | tf_op jit(solution)/shard_map/psum | solution.py:40
  160.9 17.6 %psum.39 = f32[]{:T(128)} all-reduce(f32[]{:T(128)} %psum.38), channel_id=1, replica_groups=mesh['gz_0'=4,'gz_1'=2,'xy_0'=16,'xy_1'=2,'xy_2'=2] {'xy_2'}, use_global_device_ids=true, to_apply=%region_9.10 | all-reduce | flops 1 | bytes 8 | tf_op jit(solution)/shard_map/psum | solution.py:40
  179.3 2.1 %copy.16 = f32[3,8,16,1024]{3,2,1,0:T(8,128)} copy(f32[3,8,16,1024]{3,1,0,2:T(8,128)S(1)} %divide_bitcast_fusion) | data formatting | bytes 3145728 | tf_op jit(solution)/shard_map/div | solution.py:218
  (75 shorter events, 18.4 us)
Async XLA Ops:
  0.0 24.3 %copy-start = (f32[8,16,1024]{2,1,0:T(8,128)S(1)}, f32[8,16,1024]{2,1,0:T(8,128)}, u32[]{:S(2)}) copy-start(f32[8,16,1024]{2,1,0:T(8,128)} %param.2) | copy-start | bytes 1572868
  0.0 24.3 %copy-start.1 = (f32[8,16,1024]{2,1,0:T(8,128)S(1)}, f32[8,16,1024]{2,1,0:T(8,128)}, u32[]{:S(2)}) copy-start(f32[8,16,1024]{2,1,0:T(8,128)} %param.3) | copy-start | bytes 1572868
  1.4 23.0 %collective-permute-start = (f32[2,4,16,1024]{3,2,1,0:T(8,128)S(1)}, f32[2,4,16,1024]{3,2,1,0:T(8,128)S(1)}, u32[]{:S(2)}, u32[]{:S(2)}) collective-permute-start(f32[2,4,16,1024]{3,2,1,0:T(8,128)S(1)} %get-tuple-element.18), channel_id=1, source_target_pairs={{0,64},{64,128},{128,192},{192,256},{256,320},{320,384},{384,448},... | collective-permute-start | bytes 1572872 | tf_op jit(solution)/shard_map/ppermute | solution.py:31
  5.4 18.9 %collective-permute-start.1 = (f32[2,4,16,1024]{3,2,1,0:T(8,128)S(1)}, f32[2,4,16,1024]{3,2,1,0:T(8,128)S(1)}, u32[]{:S(2)}, u32[]{:S(2)}) collective-permute-start(f32[2,4,16,1024]{3,2,1,0:T(8,128)S(1)} %get-tuple-element.19), channel_id=1, source_target_pairs={{64,0},{128,64},{192,128},{256,192},{320,256},{384,320},{448,384},... | collective-permute-start | bytes 1572872 | tf_op jit(solution)/shard_map/ppermute | solution.py:34
  24.6 20.6 %collective-permute-start.2 = (f32[2,16,4,1024]{3,2,1,0:T(4,128)S(1)}, f32[2,16,4,1024]{3,2,1,0:T(4,128)S(1)}, u32[]{:S(2)}, u32[]{:S(2)}) collective-permute-start(f32[2,16,4,1024]{3,2,1,0:T(4,128)S(1)} %get-tuple-element.16), channel_id=1, source_target_pairs={{0,1},{1,2},{2,3},{3,4},{4,5},{5,6},{6,7},{7,8},{8,9},{9,10},{10,1... | collective-permute-start | bytes 1572872 | tf_op jit(solution)/shard_map/ppermute | solution.py:31
  33.4 12.0 %collective-permute-start.3 = (f32[2,16,4,1024]{3,2,1,0:T(4,128)S(1)}, f32[2,16,4,1024]{3,2,1,0:T(4,128)S(1)}, u32[]{:S(2)}, u32[]{:S(2)}) collective-permute-start(f32[2,16,4,1024]{3,2,1,0:T(4,128)S(1)} %get-tuple-element.17), channel_id=1, source_target_pairs={{1,0},{2,1},{3,2},{4,3},{5,4},{6,5},{7,6},{8,7},{9,8},{10,9},{11,1... | collective-permute-start | bytes 1572872 | tf_op jit(solution)/shard_map/ppermute | solution.py:34
  62.9 10.9 %collective-permute-start.4 = (f32[5,3,8,131]{3,0,2,1:T(8,128)S(1)}, f32[5,3,8,131]{3,0,2,1:T(8,128)S(1)}, u32[]{:S(2)}, u32[]{:S(2)}) collective-permute-start(f32[5,3,8,131]{3,0,2,1:T(8,128)S(1)} %fusion.47), channel_id=1, source_target_pairs={{0,1},{1,2},{2,3},{3,4},{4,5},{5,6},{6,7},{7,8},{8,9},{9,10},{10,1... | collective-permute-start | bytes 188648 | tf_op jit(solution)/shard_map/ppermute | solution.py:23
  68.5 8.5 %collective-permute-start.5 = (f32[5,3,8,131]{3,0,2,1:T(8,128)S(1)}, f32[5,3,8,131]{3,0,2,1:T(8,128)S(1)}, u32[]{:S(2)}, u32[]{:S(2)}) collective-permute-start(f32[5,3,8,131]{3,0,2,1:T(8,128)S(1)} %fusion.47), channel_id=1, source_target_pairs={{1,0},{2,1},{3,2},{4,3},{5,4},{6,5},{7,6},{8,7},{9,8},{10,9},{11,1... | collective-permute-start | bytes 188648 | tf_op jit(solution)/shard_map/ppermute | solution.py:23
  70.4 6.6 %collective-permute-start.6 = (f32[5,3,8,131]{3,0,2,1:T(8,128)S(1)}, f32[5,3,8,131]{3,0,2,1:T(8,128)S(1)}, u32[]{:S(2)}, u32[]{:S(2)}) collective-permute-start(f32[5,3,8,131]{3,0,2,1:T(8,128)S(1)} %fusion.47), channel_id=1, source_target_pairs={{0,2},{1,3},{2,4},{3,5},{4,6},{5,7},{6,8},{7,9},{8,10},{9,11},{10,... | collective-permute-start | bytes 188648 | tf_op jit(solution)/shard_map/ppermute | solution.py:23
  72.5 9.2 %collective-permute-start.7 = (f32[5,3,8,131]{3,0,2,1:T(8,128)S(1)}, f32[5,3,8,131]{3,0,2,1:T(8,128)S(1)}, u32[]{:S(2)}, u32[]{:S(2)}) collective-permute-start(f32[5,3,8,131]{3,0,2,1:T(8,128)S(1)} %fusion.47), channel_id=1, source_target_pairs={{2,0},{3,1},{4,2},{5,3},{6,4},{7,5},{8,6},{9,7},{10,8},{11,9},{12,... | collective-permute-start | bytes 188648 | tf_op jit(solution)/shard_map/ppermute | solution.py:23
  82.5 15.9 %collective-permute-start.8 = (f32[4,5,3,131]{3,0,2,1:T(4,128)S(1)}, f32[4,5,3,131]{3,0,2,1:T(4,128)S(1)}, u32[]{:S(2)}, u32[]{:S(2)}) collective-permute-start(f32[4,5,3,131]{3,0,2,1:T(4,128)S(1)} %fusion.70), channel_id=1, source_target_pairs={{0,64},{64,128},{128,192},{192,256},{256,320},{320,384},{384,448},... | collective-permute-start | bytes 94328 | tf_op jit(solution)/shard_map/ppermute | solution.py:23
  86.2 13.6 %collective-permute-start.10 = (f32[4,5,3,131]{3,0,2,1:T(4,128)S(1)}, f32[4,5,3,131]{3,0,2,1:T(4,128)S(1)}, u32[]{:S(2)}, u32[]{:S(2)}) collective-permute-start(f32[4,5,3,131]{3,0,2,1:T(4,128)S(1)} %fusion.70), channel_id=1, source_target_pairs={{0,128},{64,192},{128,256},{192,320},{256,384},{320,448},{1,129},{... | collective-permute-start | bytes 94328 | tf_op jit(solution)/shard_map/ppermute | solution.py:23
  89.7 10.1 %collective-permute-start.11 = (f32[4,5,3,131]{3,0,2,1:T(4,128)S(1)}, f32[4,5,3,131]{3,0,2,1:T(4,128)S(1)}, u32[]{:S(2)}, u32[]{:S(2)}) collective-permute-start(f32[4,5,3,131]{3,0,2,1:T(4,128)S(1)} %fusion.70), channel_id=1, source_target_pairs={{128,0},{192,64},{256,128},{320,192},{384,256},{448,320},{129,1},{... | collective-permute-start | bytes 94328 | tf_op jit(solution)/shard_map/ppermute | solution.py:23
  91.0 8.9 %collective-permute-start.12 = (f32[4,5,3,131]{3,0,2,1:T(4,128)S(1)}, f32[4,5,3,131]{3,0,2,1:T(4,128)S(1)}, u32[]{:S(2)}, u32[]{:S(2)}) collective-permute-start(f32[4,5,3,131]{3,0,2,1:T(4,128)S(1)} %fusion.70), channel_id=1, source_target_pairs={{0,192},{64,256},{128,320},{192,384},{256,448},{1,193},{65,257},{1... | collective-permute-start | bytes 94328 | tf_op jit(solution)/shard_map/ppermute | solution.py:23
  97.1 5.9 %collective-permute-start.13 = (f32[4,5,3,131]{3,0,2,1:T(4,128)S(1)}, f32[4,5,3,131]{3,0,2,1:T(4,128)S(1)}, u32[]{:S(2)}, u32[]{:S(2)}) collective-permute-start(f32[4,5,3,131]{3,0,2,1:T(4,128)S(1)} %fusion.70), channel_id=1, source_target_pairs={{192,0},{256,64},{320,128},{384,192},{448,256},{193,1},{257,65},{3... | collective-permute-start | bytes 94328 | tf_op jit(solution)/shard_map/ppermute | solution.py:23
  98.4 5.2 %collective-permute-start.9 = (f32[4,5,3,131]{3,0,2,1:T(4,128)S(1)}, f32[4,5,3,131]{3,0,2,1:T(4,128)S(1)}, u32[]{:S(2)}, u32[]{:S(2)}) collective-permute-start(f32[4,5,3,131]{3,0,2,1:T(4,128)S(1)} %fusion.70), channel_id=1, source_target_pairs={{64,0},{128,64},{192,128},{256,192},{320,256},{384,320},{448,384},... | collective-permute-start | bytes 94328 | tf_op jit(solution)/shard_map/ppermute | solution.py:23
where the time goes:
time: 182 us; the launch traced here: 181 us
  blocking collectives  70.1 us (39%)
  starting transfers between devices  44 us (24%)
  waiting for transfers between devices  38.4 us (21%)
  other arithmetic  17.3 us (10%)
  matrix products  6.87 us (4%)
  local copies, waits for them, and re-layouts  3.53 us (2%)
    psum x5, blocking collectives, one_axis_at_a_time(): return functools.reduce(lax.psum, axes, x)  70.1 us
    ppermute x10, starting transfers between devices, from_behind(): return lax.ppermute(block, axis, route)  28 us
    ppermute x2, waiting for transfers between devices, extended(): lax.ppermute(lax.slice_in_dim(block, block.shape[dim] - width, None, axis...  26.6 us
    ppermute x2, starting transfers between devices, extended(): lax.ppermute(lax.slice_in_dim(block, block.shape[dim] - width, None, axis...  12.9 us
    ppermute x10, waiting for transfers between devices, from_behind(): return lax.ppermute(block, axis, route)  11.4 us
    another operation x2, other arithmetic, cc_force(): return jnp.stack([common * grad_z, common * grad_y, common * grad_x])  6.92 us
    concatenate x1, other arithmetic, extended(): block = jnp.concatenate([low, block, high], axis=dim)  3.86 us
  transfers between devices with their start and end apart: 14, of which 7 were waited for; matrix products, arithmetic and copies ran while one was open for 1% of the time, Pallas kernels for 0%

commit v1 on v0

v1 whole, which is shorter than its diff:
```python
import functools

import jax
import jax.numpy as jnp
import numpy as np
from jax import lax
from jax.experimental import pallas as pl
from jax.experimental.pallas import tpu as pltpu
from jax.sharding import Mesh
from jax.sharding import PartitionSpec as P

RADIUS = 4
SPACING = 8
EPS = 1e-05
COUNT = float((2 * RADIUS + 1) ** 3)
XY = ("xy_0", "xy_1", "xy_2")
GZ = ("gz_0", "gz_1")
PLANE = ("gz_0", "gz_1", "xy_1", "xy_2")
SLABS, STRIPS, STACKS = 8, 4, 16
MEMBERS = SLABS * STRIPS
DEPTH, ROWS, WIDTH = 8, 16, 1024
COLS = WIDTH // MEMBERS
WIDE = COLS + 2 * RADIUS
LANES = 128
KZ = SLABS + 3
KY = STRIPS * ROWS // SPACING + 3
F32 = jnp.float32
BF16 = jnp.bfloat16


def np_basis(index, knot):
    span = index // SPACING
    t = (index - span * SPACING) / SPACING
    j = knot - span
    out = np.where(j == 0, (1 - t) ** 3 / 6, 0.0)
    out = np.where(j == 1, (3 * t**3 - 6 * t**2 + 4) / 6, out)
    out = np.where(j == 2, (-3 * t**3 + 3 * t**2 + 3 * t + 1) / 6, out)
    return np.where(j == 3, t**3 / 6, out)


def np_fit(index, knot):
    value = np_basis(index, knot)
    span = index // SPACING
    total = sum(np_basis(index, span + step) ** 2 for step in range(4))
    return value**3 / total


def np_mass(knots, extent):
    spans = extent // SPACING
    within = np.arange(SPACING)
    energy = [np.sum(np_basis(within, np.full(SPACING, j)) ** 2) for j in range(4)]
    return np.array(
        [sum(energy[j] for j in range(4) if 0 <= c - j <= spans - 1) for c in range(knots)]
    )


def tables():
    z8, y16 = np.arange(DEPTH), np.arange(ROWS)
    fit_z = np_fit(z8[None, :], np.arange(4)[:, None])
    fit_y = np_fit(np.arange(STRIPS * ROWS)[None, :], np.arange(16)[:, None])
    fit_zy = np.einsum("az,bqy->abqyz", fit_z, fit_y.reshape(16, STRIPS, ROWS))
    fit_zy[:, KY:] = 0.0
    fit_zy = fit_zy.reshape(64, STRIPS * LANES)
    fit_x = np_fit(np.arange(COLS)[None, :], np.arange(8)[:, None])
    fit_x = np.kron(np.eye(3), fit_x)
    knots_x = WIDTH // SPACING + 3
    mass_x = np_mass(knots_x, WIDTH)
    full_x = np_basis(np.arange(WIDTH)[None, :], np.arange(knots_x)[:, None]) / mass_x[:, None]
    wide_x = np.zeros((MEMBERS, 8, WIDTH))
    for member in range(MEMBERS):
        wide_x[member, :7] = full_x[4 * member : 4 * member + 7]
    wide_x = wide_x.reshape(MEMBERS * 8, WIDTH)
    gram_x = wide_x @ wide_x.T
    eval_z = np_basis(np.arange(SLABS * DEPTH)[:, None], np.arange(KZ)[None, :])
    eval_y = np_basis(np.arange(STRIPS * ROWS)[:, None], np.arange(KY)[None, :])
    gram_zy = np.zeros((LANES, LANES))
    gram_zy[: KZ * KY, : KZ * KY] = np.kron(eval_z.T @ eval_z, eval_y.T @ eval_y)
    mass_z = np_mass(KZ, SLABS * DEPTH)
    mass_y = np_mass(STACKS * 8 + 3, STACKS * STRIPS * ROWS)
    inverse = np.zeros((STACKS, LANES))
    for stack in range(STACKS):
        inverse[stack, : KZ * KY] = (
            1.0 / (mass_z[:, None] * mass_y[None, 8 * stack : 8 * stack + KY])
        ).reshape(-1)
    ez = eval_z.reshape(SLABS, DEPTH, KZ)
    ey = eval_y.reshape(STRIPS, ROWS, KY)
    lane = np.arange(LANES)
    low = np.where((lane < KZ * KY) & (lane % KY < 3), 1.0, 0.0)
    high = np.where((lane < KZ * KY) & (lane % KY >= 8), 1.0, 0.0)
    ez_l = np.zeros((SLABS, DEPTH, LANES))
    ey_l = np.zeros((STRIPS, ROWS, LANES))
    ez_l[..., : KZ * KY] = np.repeat(ez, KY, axis=2)
    ey_l[..., : KZ * KY] = np.tile(ey, (1, 1, KZ))
    f = lambda v: np.asarray(v, np.float32)
    return dict(
        fit_zy=f(fit_zy), fit_x=f(fit_x), wide_x=f(wide_x), gram_x=f(gram_x), gram_zy=f(gram_zy),
        inverse=f(inverse), ez=f(ez_l), ey=f(ey_l), low=f(low), high=f(high),
    )


def split(x):
    hi = x.astype(BF16)
    return hi, (x - hi.astype(F32)).astype(BF16)


def dot(a, b, dims):
    ah, al = split(a)
    bh, bl = split(b)
    d = lambda u, v: lax.dot_general(u, v, (dims, ((), ())), preferred_element_type=F32)
    return d(ah, bh) + d(ah, bl) + d(al, bh)


NN = ((1,), (0,))
NT = ((1,), (1,))


def pack_kernel(f_ref, m_ref, o_ref, s_ref, b_ref):
    zero = jnp.zeros((RADIUS, LANES), F32)
    for image, ref in enumerate((f_ref, m_ref)):
        s_ref[image, 0:RADIUS, :] = zero
        s_ref[image, RADIUS + WIDTH : 2 * RADIUS + WIDTH, :] = zero
        for block in range(WIDTH // LANES):
            buf = b_ref.at[image, block]
            buf[...] = ref[:, block * LANES : (block + 1) * LANES]
            rows = [buf[pl.ds(y, DEPTH, stride=ROWS), :] for y in range(ROWS)]
            tile = jnp.concatenate(rows, axis=0).T
            s_ref[image, RADIUS + block * LANES : RADIUS + (block + 1) * LANES, :] = tile
    for image in range(2):
        for member in range(MEMBERS):
            o_ref[member, image] = s_ref[image, member * COLS : member * COLS + WIDE, :]


def rim_kernel(r_ref, up_ref, down_ref):
    for half in range(2):
        for image in range(2):
            slabs = range(4 * half, 4 * half + 4)
            up_ref[half, image] = jnp.concatenate(
                [r_ref[STRIPS * g + STRIPS - 1, image, :, 96:128] for g in slabs], axis=1
            )
            down_ref[half, image] = jnp.concatenate(
                [r_ref[STRIPS * g, image, :, 0:32] for g in slabs], axis=1
            )


def force_kernel(r_ref, below_ref, above_ref, fz_ref, fx_ref, o_ref, pre, suf, rim, sums, fr, acc, accp):
    lane = lax.broadcasted_iota(jnp.int32, (COLS, LANES), 1)
    z = lane & 7
    y = lane >> 3
    lane_w = lax.broadcasted_iota(jnp.int32, (WIDE, LANES), 1)
    roll = pltpu.roll

    zeros = jnp.zeros((COLS, LANES), F32)
    for q in range(STRIPS + 1):
        for field in range(5):
            suf[0, q, field] = zeros
            pre[SLABS, q, field] = zeros
    for g in range(SLABS):
        for image in range(2):
            b = below_ref[g // 4, image]
            a = above_ref[g // 4, image]
            at = (g % 4) * 32
            b = roll(b, (96 - at) % LANES, 1) if (96 - at) % LANES else b
            a = roll(a, (LANES - at) % LANES, 1) if at else a
            rim[g, image] = jnp.where(lane_w >= 96, b, jnp.where(lane_w < 32, a, 0.0))

    def window_x(v):
        s = v + roll(v, WIDE - 1, 0)
        s = s + roll(s, WIDE - 2, 0)
        s = s + roll(s, WIDE - 4, 0)
        return s[0:COLS] + v[8 : 8 + COLS]

    def images(g, q):
        if q < STRIPS:
            return r_ref[g * STRIPS + q, 0], r_ref[g * STRIPS + q, 1]
        return rim[g, 0], rim[g, 1]

    def phase_a(g, carry):
        for q in range(STRIPS + 1):
            f, m = images(g, q)
            for field, v in enumerate((f, m, f * f, m * m, f * m)):
                w = window_x(v)
                p = w + jnp.where(z >= 1, roll(w, 1, 1), 0.0)
                p = p + jnp.where(z >= 2, roll(p, 2, 1), 0.0)
                p = p + jnp.where(z >= 4, roll(p, 4, 1), 0.0)
                s = w + jnp.where(z < 7, roll(w, LANES - 1, 1), 0.0)
                s = s + jnp.where(z < 6, roll(s, LANES - 2, 1), 0.0)
                s = s + jnp.where(z < 4, roll(s, LANES - 4, 1), 0.0)
                pre[g, q, field] = p
                suf[g + 1, q, field] = s
        return carry

    lax.fori_loop(0, SLABS, phase_a, 0)

    for a in range(KZ):
        acc[a] = jnp.zeros((16, 96), F32)

    def shift_y(d, here, after):
        return roll(jnp.where(y >= d, here, after), LANES - 8 * d, 1)

    def phase_b(g, carry):
        n = STRIPS + 1
        for field in range(5):
            w = []
            for q in range(n):
                t0 = suf[g, q, field] + pre[g, q, field]
                t1 = suf[g + 1, q, field] + pre[g + 1, q, field]
                w.append(jnp.where(z < 4, roll(t0, LANES - 4, 1), roll(t1, 4, 1)))
            s = [w[q] + shift_y(1, w[q], w[(q + 1) % n]) for q in range(n)]
            s = [s[q] + shift_y(2, s[q], s[(q + 1) % n]) for q in range(n)]
            s = [s[q] + shift_y(4, s[q], s[(q + 1) % n]) for q in range(n)]
            t = [s[q] + shift_y(8, w[q], w[(q + 1) % n]) for q in range(n)]
            for q in range(STRIPS):
                sums[field, q] = roll(jnp.where(y < 12, t[q], t[(q - 1) % n]), 32, 1)

        centre = lambda g, q: images(g, q)[1][RADIUS : RADIUS + COLS]
        mid = [centre(g, q) for q in range(n)]
        down = jnp.maximum(g - 1, 0)
        up = jnp.minimum(g + 1, SLABS - 1)
        for q in range(STRIPS):
            f, m = images(g, q)
            fc = f[RADIUS : RADIUS + COLS]
            mc = mid[q]
            grad_x = (m[RADIUS + 1 : RADIUS + 1 + COLS] - m[RADIUS - 1 : RADIUS - 1 + COLS]) * 0.5
            nxt = roll(jnp.where(y >= 1, mc, mid[(q + 1) % n]), LANES - 8, 1)
            prv = roll(jnp.where(y < 15, mc, mid[(q - 1) % n]), 8, 1)
            grad_y = (nxt - prv) * 0.5
            m_up = jnp.where(g < SLABS - 1, centre(up, q), 0.0)
            m_down = jnp.where(g > 0, centre(down, q), 0.0)
            nxt = jnp.where(z < 7, roll(mc, LANES - 1, 1), roll(m_up, 7, 1))
            prv = jnp.where(z > 0, roll(mc, 1, 1), roll(m_down, LANES - 7, 1))
            grad_z = (nxt - prv) * 0.5
            inv = 1.0 / COUNT
            mean_f = sums[0, q] * inv
            mean_m = sums[1, q] * inv
            cov = sums[4, q] * inv - mean_f * mean_m
            var_f = sums[2, q] * inv - mean_f * mean_f
            var_m = sums[3, q] * inv - mean_m * mean_m
            factor = 2.0 * cov / (var_f * var_m + EPS)
            resid = fc - mean_f - cov / (var_m + EPS) * (mc - mean_m)
            common = factor * resid
            at = slice(q * LANES, (q + 1) * LANES)
            fr[0:32, at] = common * grad_z
            fr[32:64, at] = common * grad_y
            fr[64:96, at] = common * grad_x
        part = dot(fz_ref[...], fr[...], NT)
        for a in range(4):
            acc[g + a] += part[16 * a : 16 * a + 16]
        return carry

    lax.fori_loop(0, SLABS, phase_b, 0)

    accp[...] = jnp.zeros((LANES, 96), F32)
    for a in range(KZ):
        accp[a * KY : (a + 1) * KY, :] = acc[a, 0:KY, :]
    o_ref[...] = dot(fx_ref[...], accp[...], NT)


def fold_kernel(p_ref, below_ref, above_ref, low_ref, high_ref, o_ref):
    total = p_ref[...]
    total += low_ref[...] * pltpu.roll(below_ref[...], LANES - 8, 1)
    total += high_ref[...] * pltpu.roll(above_ref[...], 8, 1)
    for member in range(MEMBERS):
        o_ref[member] = total


def power_kernel(g_ref, inv_ref, gx_ref, gzy_ref, o_ref):
    total = jnp.zeros((8, LANES), F32)
    for k in range(3):
        n = jnp.concatenate([g_ref[p, 8 * k : 8 * k + 8, :] for p in range(MEMBERS)], axis=0)
        n = n * inv_ref[...]
        t = dot(gx_ref[...], n, NN)
        u = dot(n, gzy_ref[...], NN)
        total += jnp.sum((t * u).reshape(MEMBERS, 8, LANES), axis=0)
    total = jnp.full((8, LANES), jnp.sum(total), F32)
    for stack in range(STACKS):
        o_ref[stack] = total


def field_kernel(size, g_ref, e_ref, w_ref, p_ref, o_ref):
    power = p_ref[0]
    for stack in range(1, STACKS):
        power = power + p_ref[stack]
    scale = 1.0 / (jnp.sqrt(power / size) + 1e-6)
    e = e_ref[...]
    for k in range(3):
        n = jnp.concatenate([g_ref[p, 8 * k : 8 * k + 8, :] for p in range(MEMBERS)], axis=0)
        h = dot(e, n, NT) * scale[0:1, 0:1]
        o_ref[k * LANES : (k + 1) * LANES, :] = dot(h, w_ref[...], NN)


def call(kernel, shapes, *args, scratch=()):
    return pl.pallas_call(
        kernel,
        out_shape=shapes,
        scratch_shapes=list(scratch),
        compiler_params=pltpu.CompilerParams(vmem_limit_bytes=48 << 20),
    )(*args)


def shards(fixed, moving):
    tab = tables()
    sds = lambda *shape: jax.ShapeDtypeStruct(shape, F32)
    stack = lax.axis_index("xy_0")
    slab = lax.axis_index(GZ)
    strip = lax.axis_index(("xy_1", "xy_2"))
    upward = [(i, i + 1) for i in range(STACKS - 1)]
    downward = [(i + 1, i) for i in range(STACKS - 1)]

    inverse = lax.dynamic_slice_in_dim(tab["inverse"], stack, 1, 0)
    ez = lax.dynamic_index_in_dim(tab["ez"], slab, 0, keepdims=False)
    ey = lax.dynamic_index_in_dim(tab["ey"], strip, 0, keepdims=False)
    evals = (ez[:, None, :] * ey[None, :, :]).reshape(LANES, LANES) * inverse

    flat = (DEPTH * ROWS, WIDTH)
    chunks = call(
        pack_kernel,
        sds(MEMBERS, 2, WIDE, LANES),
        fixed.reshape(flat),
        moving.reshape(flat),
        scratch=[
            pltpu.VMEM((2, WIDTH + 2 * RADIUS, LANES), F32),
            pltpu.VMEM((2, WIDTH // LANES, LANES, LANES), F32),
        ],
    )
    blocks = lax.all_to_all(chunks, PLANE, 0, 0)
    up, down = call(rim_kernel, (sds(2, 2, WIDE, LANES), sds(2, 2, WIDE, LANES)), blocks)
    below = lax.ppermute(up, "xy_0", upward)
    above = lax.ppermute(down, "xy_0", downward)
    part = call(
        force_kernel,
        sds(24, LANES),
        blocks,
        below,
        above,
        tab["fit_zy"],
        tab["fit_x"],
        scratch=[
            pltpu.VMEM((SLABS + 1, STRIPS + 1, 5, COLS, LANES), F32),
            pltpu.VMEM((SLABS + 1, STRIPS + 1, 5, COLS, LANES), F32),
            pltpu.VMEM((SLABS, 2, WIDE, LANES), F32),
            pltpu.VMEM((5, STRIPS, COLS, LANES), F32),
            pltpu.VMEM((96, STRIPS * LANES), F32),
            pltpu.VMEM((KZ, 16, 96), F32),
            pltpu.VMEM((LANES, 96), F32),
        ],
    )
    below = lax.ppermute(part, "xy_0", upward)
    above = lax.ppermute(part, "xy_0", downward)
    copies = call(
        fold_kernel,
        sds(MEMBERS, 24, LANES),
        part,
        below,
        above,
        tab["low"][None],
        tab["high"][None],
    )
    numer = lax.all_to_all(copies, PLANE, 0, 0)
    power = call(
        power_kernel, sds(STACKS, 8, LANES), numer, inverse, tab["gram_x"], tab["gram_zy"]
    )
    powers = lax.all_to_all(power, "xy_0", 0, 0)
    size = float(3 * SLABS * DEPTH * STACKS * STRIPS * ROWS * WIDTH)
    field = call(
        functools.partial(field_kernel, size),
        sds(3 * LANES, WIDTH),
        numer,
        evals,
        tab["wide_x"],
        powers,
    )
    return field.reshape(3, DEPTH, ROWS, WIDTH)


def solution(mesh):
    torus = Mesh(mesh.devices.reshape(4, 2, 16, 2, 2), ("gz_0", "gz_1", "xy_0", "xy_1", "xy_2"))
    placed = (P(GZ, XY, None), P(GZ, XY, None))
    return jax.shard_map(
        shards, mesh=torus, in_specs=placed, out_specs=P(None, GZ, XY, None), check_vma=False
    )
```

time: 182 us -> 148 us (0.81)
  Pallas kernels: 0 us -> 57.6 us
  blocking collectives: 70.1 us -> 29.5 us
  other arithmetic: 17.3 us -> 0.02 us
  starting transfers between devices: 44 us -> 28 us
  waiting for transfers between devices: 38.4 us -> 28.3 us
  matrix products: 6.87 us -> 0 us
    psum x5 -> x0, blocking collectives: 70.1 us -> none  [one_axis_at_a_time(): return functools.reduce(lax.psum, axes, x)]
    pallas_call x0 -> x6, Pallas kernels: none -> 57.6 us  [call(): pl.pallas_call(kernel, out_shape=shapes, scratch_shapes=list(scratch), co...]
    ppermute x14 -> x4, starting transfers between devices: 44 us -> 8.77 us  [the longest x1 3.72 us: shards(): below = lax.ppermute(part, 'xy_0', upward)]
    all_to_all x0 -> x1, blocking collectives: none -> 29.5 us  [shards(): blocks = lax.all_to_all(chunks, PLANE, 0, 0)]
    ppermute x14 -> x4, waiting for transfers between devices: 38.4 us -> 8.91 us  [the longest x1 4.84 us: shards(): above = lax.ppermute(part, 'xy_0', downward)]
    all_to_all x0 -> x2, waiting for transfers between devices: none -> 19.4 us  [the longest x1 11.6 us: shards(): powers = lax.all_to_all(power, 'xy_0', 0, 0)]
    all_to_all x0 -> x2, starting transfers between devices: none -> 19.2 us  [the longest x1 13.1 us: shards(): powers = lax.all_to_all(power, 'xy_0', 0, 0)]
    another operation x3 -> x0, other arithmetic: 8.27 us -> none  [the longest x2 6.92 us: cc_force(): return jnp.stack([common * grad_z, common * grad_y, common * grad_x])]
  transfers between devices with their start and end apart: 14 -> 6, of which waited for: 7 -> 4; matrix products, arithmetic and copies ran while one was open for 1% -> 1% of each run, Pallas kernels for 0% -> 0%
where the time goes in v1:
time: 148 us
  Pallas kernels  57.6 us (39%)
  blocking collectives  29.5 us (20%)
  waiting for transfers between devices  28.3 us (19%)
  starting transfers between devices  28 us (19%)
  local copies, waits for them, and re-layouts  4.2 us (3%)
    pallas_call x6, Pallas kernels, call(): pl.pallas_call(kernel, out_shape=shapes, scratch_shapes=list(scratch), co...  57.6 us
    all_to_all x1, blocking collectives, shards(): blocks = lax.all_to_all(chunks, PLANE, 0, 0)  29.5 us
    all_to_all x1, starting transfers between devices, shards(): powers = lax.all_to_all(power, 'xy_0', 0, 0)  13.1 us
    all_to_all x1, waiting for transfers between devices, shards(): powers = lax.all_to_all(power, 'xy_0', 0, 0)  11.6 us
    all_to_all x1, waiting for transfers between devices, shards(): numer = lax.all_to_all(copies, PLANE, 0, 0)  7.79 us
    all_to_all x1, starting transfers between devices, shards(): numer = lax.all_to_all(copies, PLANE, 0, 0)  6.19 us
    ppermute x1, waiting for transfers between devices, shards(): above = lax.ppermute(part, 'xy_0', downward)  4.84 us
    ppermute x1, waiting for transfers between devices, shards(): above = lax.ppermute(down, 'xy_0', downward)  4.06 us
  transfers between devices with their start and end apart: 6, of which 4 were waited for; matrix products, arithmetic and copies ran while one was open for 1% of the time, Pallas kernels for 0%

profile of v1, /device:TPU:1, one launch (start us, length us, event | category | flops | bytes accessed | tf_op | source)
XLA Modules:
  0.0 147.8 jit_solution(14140291274114169440)
XLA Ops:
  0.0 1.0 copy-done.1
  1.0 1.0 copy-done.2
  2.1 0.5 shard_map.118
  2.6 29.5 %all_to_all.15.r_ref = f32[32,2,40,128]{3,2,1,0:T(8,128)S(1)} all-to-all(f32[32,2,40,128]{3,2,1,0:T(8,128)S(1)} %shard_map.118), channel_id=1, replica_groups=mesh['gz_0'=4,'gz_1'=2,'xy_0'=16,'xy_1'=2,'xy_2'=2] {'gz_0','gz_1','xy_1..., dimensions={0} | all-to-all | bytes 2621440 | tf_op jit(solution)/shard_map/all_to_all | solution.py:325
  32.2 0.2 shard_map.119
  32.4 2.3 %collective-permute-start = (f32[2,2,40,128]{3,2,1,0:T(8,128)S(1)}, f32[2,2,40,128]{3,2,1,0:T(8,128)S(1)}, u32[]{:S(2)}, u32[]{:S(2)}) collective-permute-start(f32[2,2,40,128]{3,2,1,0:T(8,128)S(1)} %get-tuple-element.7), channel_id=1, source_target_pairs={{0,4},{4,8},{8,12},{12,16},{16,20},{20,24},{24,28},{28,32},{32,36}... | collective-permute-start | bytes 245768 | tf_op jit(solution)/shard_map/ppermute | solution.py:327
  34.7 0.0 copy-start.3
  34.7 1.4 collective-permute-start.1
  36.2 0.0 collective-permute-done.below_ref
  36.2 4.1 %collective-permute-done.1.above_ref = f32[2,2,40,128]{3,2,1,0:T(8,128)S(1)} collective-permute-done((f32[2,2,40,128]{3,2,1,0:T(8,128)S(1)}, f32[2,2,40,128]{3,2,1,0:T(8,128)S(1)}, u32[]{:S(2)}, u32[]{:S(2)}) %collective-permute-start.1) | collective-permute-done | bytes 81952 | tf_op jit(solution)/shard_map/ppermute | solution.py:328
  40.2 52.1 %shard_map.120.p_ref = f32[24,128]{1,0:T(8,128)S(1)} custom-call(f32[32,2,40,128]{3,2,1,0:T(8,128)S(1)} %all_to_all.15.r_ref, f32[2,2,40,128]{3,2,1,0:T(8,128)S(1)} %collective-permute-done.below_ref, f32[2,2,40,128]{3,2,1,0:T(8,128)S(1)} %collective-permute-done.1.above_ref, f32[64,512]{1,0:T(8,128)S(1)} %copy-done.4, f32[24,96]{1,0:T(8,128)S(1)} %copy-done.6), custom_call_target="tpu_custom_call" | custom-call | tf_op jit(solution)/shard_map/pallas_call | solution.py:292
  92.3 3.7 %collective-permute-start.2 = (f32[24,128]{1,0:T(8,128)S(1)}, f32[24,128]{1,0:T(8,128)S(1)}, u32[]{:S(2)}, u32[]{:S(2)}) collective-permute-start(f32[24,128]{1,0:T(8,128)S(1)} %shard_map.120.p_ref), channel_id=1, source_target_pairs={{0,4},{4,8},{8,12},{12,16},{16,20},{20,24},{24,28},{28,32},{32,36}... | collective-permute-start | bytes 36872 | tf_op jit(solution)/shard_map/ppermute | solution.py:347
  96.0 1.3 collective-permute-start.3
  97.3 4.8 %collective-permute-done.3.above_ref = f32[24,128]{1,0:T(8,128)S(1)} collective-permute-done((f32[24,128]{1,0:T(8,128)S(1)}, f32[24,128]{1,0:T(8,128)S(1)}, u32[]{:S(2)}, u32[]{:S(2)}) %collective-permute-start.3) | collective-permute-done | bytes 12320 | tf_op jit(solution)/shard_map/ppermute | solution.py:348
  102.2 0.8 shard_map.121
  103.0 6.2 %all-to-all-start.1 = ((f32[32,24,128]{2,1,0:T(8,128)}), f32[32,24,128]{2,1,0:T(8,128)S(1)}, u32[]{:S(2)}, u32[]{:S(2)}) async-start(f32[32,24,128]{2,1,0:T(8,128)} %shard_map.121), calls=%async_computation.1 | async-start | bytes 786432 | tf_op jit(solution)/shard_map/all_to_all | solution.py:358
  109.2 0.7 constant_dynamic-slice_fusion
  109.9 0.7 dynamic-slice_bitcast_fusion.1
  110.6 0.7 dynamic-slice_bitcast_fusion
  111.3 7.8 %all-to-all-done.1.g_ref = f32[32,24,128]{2,1,0:T(8,128)S(1)} async-done(((f32[32,24,128]{2,1,0:T(8,128)}), f32[32,24,128]{2,1,0:T(8,128)S(1)}, u32[]{:S(2)}, u32[]{:S(2)}) %all-to-all-start.1) | async-done | bytes 393248 | tf_op jit(solution)/shard_map/all_to_all | solution.py:358
  119.1 1.4 shard_map.122
  120.5 13.1 %all-to-all-start.2 = ((f32[16,8,128]{2,1,0:T(8,128)}), f32[16,8,128]{2,1,0:T(8,128)S(1)}, u32[]{:S(2)}, u32[]{:S(2)}) async-start(f32[16,8,128]{2,1,0:T(8,128)} %shard_map.122), calls=%async_computation.2 | async-start | bytes 131072 | tf_op jit(solution)/shard_map/all_to_all | solution.py:362
  133.6 11.6 %all-to-all-done.2.p_ref = f32[16,8,128]{2,1,0:T(8,128)S(1)} async-done(((f32[16,8,128]{2,1,0:T(8,128)}), f32[16,8,128]{2,1,0:T(8,128)S(1)}, u32[]{:S(2)}, u32[]{:S(2)}) %all-to-all-start.2) | async-done | bytes 65568 | tf_op jit(solution)/shard_map/all_to_all | solution.py:362
  145.2 2.6 %shard_map.123 = f32[384,1024]{1,0:T(8,128)} custom-call(f32[32,24,128]{2,1,0:T(8,128)S(1)} %all-to-all-done.1.g_ref, f32[128,128]{1,0:T(8,128)S(1)} %bitcast_multiply_fusion.e_ref, f32[256,1024]{1,0:T(8,128)S(1)} %copy-done, f32[16,8,128]{2,1,0:T(8,128)S(1)} %all-to-all-done.2.p_ref), custom_call_target="tpu_custom_call" | custom-call | tf_op jit(solution)/shard_map/pallas_call | solution.py:292
  (18 shorter events, 0.1 us)
Async XLA Ops:
  0.0 1.0 copy-start.1
  1.0 1.0 copy-start.2
  32.2 8.1 %copy-start.4 = (f32[64,512]{1,0:T(8,128)S(1)}, f32[64,512]{1,0:T(8,128)}, u32[]{:S(2)}) copy-start(f32[64,512]{1,0:T(8,128)} %constant.60.clone.fz_ref) | copy-start | bytes 393220
  32.2 8.1 %copy-start.6 = (f32[24,96]{1,0:T(8,128)S(1)}, f32[24,96]{1,0:T(8,128)}, u32[]{:S(2)}) copy-start(f32[24,96]{1,0:T(8,128)} %constant.61.clone.fx_ref) | copy-start | bytes 27652
  32.2 70.0 %copy-start.7 = (f32[1,128]{1,0:T(1,128)S(1)}, f32[1,128]{1,0:T(1,128)}, u32[]{:S(2)}) copy-start(f32[1,128]{1,0:T(1,128)} %constant.62.clone.low_ref) | copy-start | bytes 1540
  32.2 70.0 %copy-start.8 = (f32[1,128]{1,0:T(1,128)S(1)}, f32[1,128]{1,0:T(1,128)}, u32[]{:S(2)}) copy-start(f32[1,128]{1,0:T(1,128)} %constant.63.clone.high_ref) | copy-start | bytes 1540
  32.4 3.8 %collective-permute-start = (f32[2,2,40,128]{3,2,1,0:T(8,128)S(1)}, f32[2,2,40,128]{3,2,1,0:T(8,128)S(1)}, u32[]{:S(2)}, u32[]{:S(2)}) collective-permute-start(f32[2,2,40,128]{3,2,1,0:T(8,128)S(1)} %get-tuple-element.7), channel_id=1, source_target_pairs={{0,4},{4,8},{8,12},{12,16},{16,20},{20,24},{24,28},{28,32},{32,36}... | collective-permute-start | bytes 245768 | tf_op jit(solution)/shard_map/ppermute | solution.py:327
  34.7 84.4 %copy-start.3 = (f32[256,256]{1,0:T(8,128)S(1)}, f32[256,256]{1,0:T(8,128)}, u32[]{:S(2)}) copy-start(f32[256,256]{1,0:T(8,128)} %constant.64.clone.gx_ref) | copy-start | bytes 786436
  34.7 84.4 %copy-start.5 = (f32[128,128]{1,0:T(8,128)S(1)}, f32[128,128]{1,0:T(8,128)}, u32[]{:S(2)}) copy-start(f32[128,128]{1,0:T(8,128)} %constant.65.clone.gzy_ref) | copy-start | bytes 196612
  34.7 5.5 %collective-permute-start.1 = (f32[2,2,40,128]{3,2,1,0:T(8,128)S(1)}, f32[2,2,40,128]{3,2,1,0:T(8,128)S(1)}, u32[]{:S(2)}, u32[]{:S(2)}) collective-permute-start(f32[2,2,40,128]{3,2,1,0:T(8,128)S(1)} %get-tuple-element.8), channel_id=1, source_target_pairs={{4,0},{8,4},{12,8},{16,12},{20,16},{24,20},{28,24},{32,28},{36,32}... | collective-permute-start | bytes 245768 | tf_op jit(solution)/shard_map/ppermute | solution.py:328
  92.3 52.9 %copy-start = (f32[256,1024]{1,0:T(8,128)S(1)}, f32[256,1024]{1,0:T(8,128)}, u32[]{:S(2)}) copy-start(f32[256,1024]{1,0:T(8,128)} %constant.66.clone.w_ref) | copy-start | bytes 3145732
  92.3 5.0 %collective-permute-start.2 = (f32[24,128]{1,0:T(8,128)S(1)}, f32[24,128]{1,0:T(8,128)S(1)}, u32[]{:S(2)}, u32[]{:S(2)}) collective-permute-start(f32[24,128]{1,0:T(8,128)S(1)} %shard_map.120.p_ref), channel_id=1, source_target_pairs={{0,4},{4,8},{8,12},{12,16},{16,20},{20,24},{24,28},{28,32},{32,36}... | collective-permute-start | bytes 36872 | tf_op jit(solution)/shard_map/ppermute | solution.py:347
  96.0 6.1 %collective-permute-start.3 = (f32[24,128]{1,0:T(8,128)S(1)}, f32[24,128]{1,0:T(8,128)S(1)}, u32[]{:S(2)}, u32[]{:S(2)}) collective-permute-start(f32[24,128]{1,0:T(8,128)S(1)} %shard_map.120.p_ref), channel_id=1, source_target_pairs={{4,0},{8,4},{12,8},{16,12},{20,16},{24,20},{28,24},{32,28},{36,32}... | collective-permute-start | bytes 36872 | tf_op jit(solution)/shard_map/ppermute | solution.py:348
  103.0 16.1 %all-to-all-start.1 = ((f32[32,24,128]{2,1,0:T(8,128)}), f32[32,24,128]{2,1,0:T(8,128)S(1)}, u32[]{:S(2)}, u32[]{:S(2)}) async-start(f32[32,24,128]{2,1,0:T(8,128)} %shard_map.121), calls=%async_computation.1 | async-start | bytes 786432 | tf_op jit(solution)/shard_map/all_to_all | solution.py:358
  120.5 24.7 %all-to-all-start.2 = ((f32[16,8,128]{2,1,0:T(8,128)}), f32[16,8,128]{2,1,0:T(8,128)S(1)}, u32[]{:S(2)}, u32[]{:S(2)}) async-start(f32[16,8,128]{2,1,0:T(8,128)} %shard_map.122), calls=%async_computation.2 | async-start | bytes 131072 | tf_op jit(solution)/shard_map/all_to_all | solution.py:362

commit v2 on v1

--- a/solution.py
+++ b/solution.py
@@ -57,12 +57,16 @@
 def tables():
     z8, y16 = np.arange(DEPTH), np.arange(ROWS)
     fit_z = np_fit(z8[None, :], np.arange(4)[:, None])
-    fit_y = np_fit(np.arange(STRIPS * ROWS)[None, :], np.arange(16)[:, None])
-    fit_zy = np.einsum("az,bqy->abqyz", fit_z, fit_y.reshape(16, STRIPS, ROWS))
-    fit_zy[:, KY:] = 0.0
-    fit_zy = fit_zy.reshape(64, STRIPS * LANES)
+    fit_y = np_fit(y16[None, :], np.arange(8)[:, None])
+    fit_zy = np.einsum("az,by->abyz", fit_z, fit_y).reshape(32, LANES).astype(np.float32)
     fit_x = np_fit(np.arange(COLS)[None, :], np.arange(8)[:, None])
-    fit_x = np.kron(np.eye(3), fit_x)
+    fit_x = np.einsum("qr,kj,cx->qkcjrx", np.eye(STRIPS), np.eye(3), fit_x).reshape(96, 3 * LANES)
+    place = np.zeros((STRIPS, 16, 8, LANES))
+    for q in range(STRIPS):
+        for a in range(KZ):
+            for b in range(5):
+                place[q, a, b, KY * a + 2 * q + b] = 1.0
+    place = place.reshape(STRIPS, LANES, LANES)
     knots_x = WIDTH // SPACING + 3
     mass_x = np_mass(knots_x, WIDTH)
     full_x = np_basis(np.arange(WIDTH)[None, :], np.arange(knots_x)[:, None]) / mass_x[:, None]
@@ -92,8 +96,11 @@
     ez_l[..., : KZ * KY] = np.repeat(ez, KY, axis=2)
     ey_l[..., : KZ * KY] = np.tile(ey, (1, 1, KZ))
     f = lambda v: np.asarray(v, np.float32)
+    high_zy = fit_zy.astype(jnp.bfloat16)
+    low_zy = (fit_zy - high_zy.astype(np.float32)).astype(jnp.bfloat16)
+    fit_zy = np.block([[high_zy, high_zy], [low_zy, np.zeros_like(low_zy)]])
     return dict(
-        fit_zy=f(fit_zy), fit_x=f(fit_x), wide_x=f(wide_x), gram_x=f(gram_x), gram_zy=f(gram_zy),
+        fit_zy=fit_zy, place=f(place), fit_x=f(fit_x), wide_x=f(wide_x), gram_x=f(gram_x), gram_zy=f(gram_zy),
         inverse=f(inverse), ez=f(ez_l), ey=f(ey_l), low=f(low), high=f(high),
     )
 
@@ -142,117 +149,131 @@
             )
 
 
-def force_kernel(r_ref, below_ref, above_ref, fz_ref, fx_ref, o_ref, pre, suf, rim, sums, fr, acc, accp):
-    lane = lax.broadcasted_iota(jnp.int32, (COLS, LANES), 1)
-    z = lane & 7
-    y = lane >> 3
-    lane_w = lax.broadcasted_iota(jnp.int32, (WIDE, LANES), 1)
+def force_kernel(
+    r_ref, below_ref, above_ref, fz_ref, fx_ref, place_ref, o_ref, stack, rim_t, turned, mid, fr, acc
+):
     roll = pltpu.roll
-
-    zeros = jnp.zeros((COLS, LANES), F32)
-    for q in range(STRIPS + 1):
-        for field in range(5):
-            suf[0, q, field] = zeros
-            pre[SLABS, q, field] = zeros
-    for g in range(SLABS):
-        for image in range(2):
-            b = below_ref[g // 4, image]
-            a = above_ref[g // 4, image]
-            at = (g % 4) * 32
-            b = roll(b, (96 - at) % LANES, 1) if (96 - at) % LANES else b
-            a = roll(a, (LANES - at) % LANES, 1) if at else a
-            rim[g, image] = jnp.where(lane_w >= 96, b, jnp.where(lane_w < 32, a, 0.0))
 
     def window_x(v):
         s = v + roll(v, WIDE - 1, 0)
         s = s + roll(s, WIDE - 2, 0)
         s = s + roll(s, WIDE - 4, 0)
-        return s[0:COLS] + v[8 : 8 + COLS]
-
-    def images(g, q):
-        if q < STRIPS:
-            return r_ref[g * STRIPS + q, 0], r_ref[g * STRIPS + q, 1]
-        return rim[g, 0], rim[g, 1]
-
-    def phase_a(g, carry):
-        for q in range(STRIPS + 1):
-            f, m = images(g, q)
-            for field, v in enumerate((f, m, f * f, m * m, f * m)):
-                w = window_x(v)
-                p = w + jnp.where(z >= 1, roll(w, 1, 1), 0.0)
-                p = p + jnp.where(z >= 2, roll(p, 2, 1), 0.0)
-                p = p + jnp.where(z >= 4, roll(p, 4, 1), 0.0)
-                s = w + jnp.where(z < 7, roll(w, LANES - 1, 1), 0.0)
-                s = s + jnp.where(z < 6, roll(s, LANES - 2, 1), 0.0)
-                s = s + jnp.where(z < 4, roll(s, LANES - 4, 1), 0.0)
-                pre[g, q, field] = p
-                suf[g + 1, q, field] = s
+        return s[0:COLS] + v[2 * RADIUS : 2 * RADIUS + COLS]
+
+    def windows(f, m):
+        return [window_x(v) for v in (f, m, f * f, m * m, f * m)]
+
+    for half in range(2):
+        for at, ref in ((0, below_ref), (96, above_ref)):
+            values = windows(ref[half, 0], ref[half, 1])
+            values.append(ref[half, 1, RADIUS : RADIUS + COLS, :])
+            for item, v in enumerate(values):
+                stack[item, at : at + COLS, :] = v
+        for item in range(6):
+            stack[item, 32:96, :] = jnp.zeros((64, LANES), F32)
+            rim_t[half, item] = stack[item].T
+
+    def phase_x(g, carry):
+        for q in range(STRIPS):
+            i = g * STRIPS + q
+            values = windows(r_ref[i, 0], r_ref[i, 1])
+            values.append(r_ref[i, 0, RADIUS : RADIUS + COLS, :])
+            values.append(r_ref[i, 1, RADIUS : RADIUS + COLS, :])
+            values.append(
+                (
+                    r_ref[i, 1, RADIUS + 1 : RADIUS + 1 + COLS, :]
+                    - r_ref[i, 1, RADIUS - 1 : RADIUS - 1 + COLS, :]
+                )
+                * 0.5
+            )
+            for item, v in enumerate(values):
+                stack[item, q * COLS : (q + 1) * COLS, :] = v
+        for item in range(8):
+            turned[item, g] = stack[item].T
         return carry
 
-    lax.fori_loop(0, SLABS, phase_a, 0)
-
-    for a in range(KZ):
-        acc[a] = jnp.zeros((16, 96), F32)
-
-    def shift_y(d, here, after):
-        return roll(jnp.where(y >= d, here, after), LANES - 8 * d, 1)
-
-    def phase_b(g, carry):
-        n = STRIPS + 1
+    lax.fori_loop(0, SLABS, phase_x, 0)
+
+    lane = lax.broadcasted_iota(jnp.int32, (8, LANES), 1)
+    first, last = lane < COLS, lane >= LANES - COLS
+    row = lambda y: pl.ds(y * 8, 8) if not isinstance(y, int) else slice(y * 8, y * 8 + 8)
+
+    def phase_y(g, carry):
+        half = g // 4
+        base = (g % 4) * 4
+        near = lambda item, i: rim_t[half, item, row(base + i), :]
         for field in range(5):
-            w = []
-            for q in range(n):
-                t0 = suf[g, q, field] + pre[g, q, field]
-                t1 = suf[g + 1, q, field] + pre[g + 1, q, field]
-                w.append(jnp.where(z < 4, roll(t0, LANES - 4, 1), roll(t1, 4, 1)))
-            s = [w[q] + shift_y(1, w[q], w[(q + 1) % n]) for q in range(n)]
-            s = [s[q] + shift_y(2, s[q], s[(q + 1) % n]) for q in range(n)]
-            s = [s[q] + shift_y(4, s[q], s[(q + 1) % n]) for q in range(n)]
-            t = [s[q] + shift_y(8, w[q], w[(q + 1) % n]) for q in range(n)]
-            for q in range(STRIPS):
-                sums[field, q] = roll(jnp.where(y < 12, t[q], t[(q - 1) % n]), 32, 1)
-
-        centre = lambda g, q: images(g, q)[1][RADIUS : RADIUS + COLS]
-        mid = [centre(g, q) for q in range(n)]
-        down = jnp.maximum(g - 1, 0)
-        up = jnp.minimum(g + 1, SLABS - 1)
-        for q in range(STRIPS):
-            f, m = images(g, q)
-            fc = f[RADIUS : RADIUS + COLS]
-            mc = mid[q]
-            grad_x = (m[RADIUS + 1 : RADIUS + 1 + COLS] - m[RADIUS - 1 : RADIUS - 1 + COLS]) * 0.5
-            nxt = roll(jnp.where(y >= 1, mc, mid[(q + 1) % n]), LANES - 8, 1)
-            prv = roll(jnp.where(y < 15, mc, mid[(q - 1) % n]), 8, 1)
-            grad_y = (nxt - prv) * 0.5
-            m_up = jnp.where(g < SLABS - 1, centre(up, q), 0.0)
-            m_down = jnp.where(g > 0, centre(down, q), 0.0)
-            nxt = jnp.where(z < 7, roll(mc, LANES - 1, 1), roll(m_up, 7, 1))
-            prv = jnp.where(z > 0, roll(mc, 1, 1), roll(m_down, LANES - 7, 1))
-            grad_z = (nxt - prv) * 0.5
-            inv = 1.0 / COUNT
-            mean_f = sums[0, q] * inv
-            mean_m = sums[1, q] * inv
-            cov = sums[4, q] * inv - mean_f * mean_m
-            var_f = sums[2, q] * inv - mean_f * mean_f
-            var_m = sums[3, q] * inv - mean_m * mean_m
+            v = [turned[field, g, row(y), :] for y in range(ROWS)]
+            lower = [jnp.where(first, near(field, i), roll(v[12 + i], COLS, 1)) for i in range(4)]
+            upper = [jnp.where(last, near(field, i), roll(v[i], LANES - COLS, 1)) for i in range(4)]
+            v = lower + v + upper
+            s = [v[i] + v[i + 1] for i in range(23)]
+            s = [s[i] + s[i + 2] for i in range(21)]
+            for y in range(ROWS):
+                turned[field, g, row(y), :] = (s[y] + s[y + 4]) + v[y + 8]
+        m0 = turned[6, g, row(0), :]
+        m15 = turned[6, g, row(15), :]
+        mid[g, row(0), :] = jnp.where(first, near(5, 3), roll(m15, COLS, 1))
+        mid[g, row(17), :] = jnp.where(last, near(5, 0), roll(m0, LANES - COLS, 1))
+        mid[g, 8 : 8 + LANES, :] = turned[6, g]
+        return carry
+
+    lax.fori_loop(0, SLABS, phase_y, 0)
+
+    z = lax.broadcasted_iota(jnp.int32, (8, LANES), 0)
+    zero = jnp.zeros((8, LANES), F32)
+
+    def window_z(v):
+        v = [zero] + v + [zero]
+
+        def ahead(u, d):
+            r = [roll(x, 8 - d, 0) for x in u] + [zero]
+            return [x + jnp.where(z < 8 - d, r[i], r[i + 1]) for i, x in enumerate(u)]
+
+        s = ahead(ahead(ahead(v, 1), 2), 4)
+        t = [s[i] + v[i + 1] for i in range(SLABS + 1)]
+        return [roll(jnp.where(z >= 4, t[g], t[g + 1]), 4, 0) for g in range(SLABS)]
+
+    inv = 1.0 / COUNT
+
+    def phase_z(y, carry):
+        sums = [window_z([turned[field, g, row(y), :] for g in range(SLABS)]) for field in range(5)]
+        m = [mid[g, row(y + 1), :] for g in range(SLABS)]
+        fore = [roll(v, 7, 0) for v in m] + [zero]
+        back = [zero] + [roll(v, 1, 0) for v in m]
+        for g in range(SLABS):
+            grad_z = (
+                jnp.where(z < 7, fore[g], fore[g + 1]) - jnp.where(z > 0, back[g + 1], back[g])
+            ) * 0.5
+            grad_y = (mid[g, row(y + 2), :] - mid[g, row(y), :]) * 0.5
+            grad_x = turned[7, g, row(y), :]
+            mean_f = sums[0][g] * inv
+            mean_m = sums[1][g] * inv
+            cov = sums[4][g] * inv - mean_f * mean_m
+            var_f = sums[2][g] * inv - mean_f * mean_f
+            var_m = sums[3][g] * inv - mean_m * mean_m
             factor = 2.0 * cov / (var_f * var_m + EPS)
-            resid = fc - mean_f - cov / (var_m + EPS) * (mc - mean_m)
+            resid = turned[5, g, row(y), :] - mean_f - cov / (var_m + EPS) * (m[g] - mean_m)
             common = factor * resid
-            at = slice(q * LANES, (q + 1) * LANES)
-            fr[0:32, at] = common * grad_z
-            fr[32:64, at] = common * grad_y
-            fr[64:96, at] = common * grad_x
-        part = dot(fz_ref[...], fr[...], NT)
+            for k, grad in enumerate((grad_z, grad_y, grad_x)):
+                fr[g, row(y), k * LANES : (k + 1) * LANES] = common * grad
+        return carry
+
+    lax.fori_loop(0, ROWS, phase_z, 0)
+
+    acc[...] = jnp.zeros((16, 8, 3 * LANES), F32)
+    for g in range(SLABS):
+        hi, lo = split(fr[g])
+        part = lax.dot_general(
+            fz_ref[...], jnp.concatenate([hi, lo], axis=0), (NN, ((), ())), preferred_element_type=F32
+        )
         for a in range(4):
-            acc[g + a] += part[16 * a : 16 * a + 16]
-        return carry
-
-    lax.fori_loop(0, SLABS, phase_b, 0)
-
-    accp[...] = jnp.zeros((LANES, 96), F32)
-    for a in range(KZ):
-        accp[a * KY : (a + 1) * KY, :] = acc[a, 0:KY, :]
-    o_ref[...] = dot(fx_ref[...], accp[...], NT)
+            acc[g + a] += part[8 * a : 8 * a + 8] + part[32 + 8 * a : 40 + 8 * a]
+    wide = dot(fx_ref[...], acc[...].reshape(LANES, 3 * LANES), NT)
+    total = dot(wide[0:24], place_ref[0], NN)
+    for q in range(1, STRIPS):
+        total += dot(wide[24 * q : 24 * q + 24], place_ref[q], NN)
+    o_ref[...] = total
 
 
 def fold_kernel(p_ref, below_ref, above_ref, low_ref, high_ref, o_ref):
@@ -334,14 +355,14 @@
         above,
         tab["fit_zy"],
         tab["fit_x"],
+        tab["place"],
         scratch=[
-            pltpu.VMEM((SLABS + 1, STRIPS + 1, 5, COLS, LANES), F32),
-            pltpu.VMEM((SLABS + 1, STRIPS + 1, 5, COLS, LANES), F32),
-            pltpu.VMEM((SLABS, 2, WIDE, LANES), F32),
-            pltpu.VMEM((5, STRIPS, COLS, LANES), F32),
-            pltpu.VMEM((96, STRIPS * LANES), F32),
-            pltpu.VMEM((KZ, 16, 96), F32),
-            pltpu.VMEM((LANES, 96), F32),
+            pltpu.VMEM((8, LANES, LANES), F32),
+            pltpu.VMEM((2, 6, LANES, LANES), F32),
+            pltpu.VMEM((8, SLABS, LANES, LANES), F32),
+            pltpu.VMEM((SLABS, LANES + 16, LANES), F32),
+            pltpu.VMEM((SLABS, LANES, 3 * LANES), F32),
+            pltpu.VMEM((16, 8, 3 * LANES), F32),
         ],
     )
     below = lax.ppermute(part, "xy_0", upward)

time: 148 us -> 102 us (0.69)
  Pallas kernels: 57.6 us -> 11.7 us
    pallas_call x6, Pallas kernels: 57.6 us -> 11.7 us  [call(): pl.pallas_call(kernel, out_shape=shapes, scratch_shapes=list(scratch), co...]
  transfers between devices with their start and end apart: 6 -> 6, of which waited for: 4 -> 4; matrix products, arithmetic and copies ran while one was open for 1% -> 2% of each run, Pallas kernels for 0% -> 0%
where the time goes in v2:
time: 102 us
  blocking collectives  29.5 us (29%)
  waiting for transfers between devices  28.3 us (28%)
  starting transfers between devices  28 us (27%)
  Pallas kernels  11.7 us (11%)
  local copies, waits for them, and re-layouts  4.2 us (4%)
    all_to_all x1, blocking collectives, shards(): blocks = lax.all_to_all(chunks, PLANE, 0, 0)  29.5 us
    all_to_all x1, starting transfers between devices, shards(): powers = lax.all_to_all(power, 'xy_0', 0, 0)  13.1 us
    pallas_call x6, Pallas kernels, call(): pl.pallas_call(kernel, out_shape=shapes, scratch_shapes=list(scratch), co...  11.7 us
    all_to_all x1, waiting for transfers between devices, shards(): powers = lax.all_to_all(power, 'xy_0', 0, 0)  11.6 us
    all_to_all x1, waiting for transfers between devices, shards(): numer = lax.all_to_all(copies, PLANE, 0, 0)  7.8 us
    all_to_all x1, starting transfers between devices, shards(): numer = lax.all_to_all(copies, PLANE, 0, 0)  6.18 us
    ppermute x1, waiting for transfers between devices, shards(): above = lax.ppermute(part, 'xy_0', downward)  4.84 us
    ppermute x1, waiting for transfers between devices, shards(): above = lax.ppermute(down, 'xy_0', downward)  4.06 us
  transfers between devices with their start and end apart: 6, of which 4 were waited for; matrix products, arithmetic and copies ran while one was open for 2% of the time, Pallas kernels for 0%

profile of v2, /device:TPU:1, one launch (start us, length us, event | category | flops | bytes accessed | tf_op | source)
XLA Modules:
  0.0 101.9 jit_solution(16523211762726530245)
XLA Ops:
  0.0 1.0 %copy-done.1 = f32[8,16,1024]{2,1,0:T(8,128)S(1)} copy-done((f32[8,16,1024]{2,1,0:T(8,128)S(1)}, f32[8,16,1024]{2,1,0:T(8,128)}, u32[]{:S(2)}) %copy-start.1) | copy-done | bytes 524312
  1.0 1.0 %copy-done.2 = f32[8,16,1024]{2,1,0:T(8,128)S(1)} copy-done((f32[8,16,1024]{2,1,0:T(8,128)S(1)}, f32[8,16,1024]{2,1,0:T(8,128)}, u32[]{:S(2)}) %copy-start.2) | copy-done | bytes 524312
  2.1 0.5 shard_map.127
  2.6 29.5 %all_to_all.15.r_ref = f32[32,2,40,128]{3,2,1,0:T(8,128)S(1)} all-to-all(f32[32,2,40,128]{3,2,1,0:T(8,128)S(1)} %shard_map.127), channel_id=1, replica_groups=mesh['gz_0'=4,'gz_1'=2,'xy_0'=16,'xy_1'=2,'xy_2'=2] {'gz_0','gz_1','xy_1..., dimensions={0} | all-to-all | bytes 2621440 | tf_op jit(solution)/shard_map/all_to_all | solution.py:346
  32.2 0.0 copy-start.9
  32.2 0.2 shard_map.128
  32.4 2.3 %collective-permute-start = (f32[2,2,40,128]{3,2,1,0:T(8,128)S(1)}, f32[2,2,40,128]{3,2,1,0:T(8,128)S(1)}, u32[]{:S(2)}, u32[]{:S(2)}) collective-permute-start(f32[2,2,40,128]{3,2,1,0:T(8,128)S(1)} %get-tuple-element.7), channel_id=1, source_target_pairs={{0,4},{4,8},{8,12},{12,16},{16,20},{20,24},{24,28},{28,32},{32,36}... | collective-permute-start | bytes 245768 | tf_op jit(solution)/shard_map/ppermute | solution.py:348
  34.7 1.4 %collective-permute-start.1 = (f32[2,2,40,128]{3,2,1,0:T(8,128)S(1)}, f32[2,2,40,128]{3,2,1,0:T(8,128)S(1)}, u32[]{:S(2)}, u32[]{:S(2)}) collective-permute-start(f32[2,2,40,128]{3,2,1,0:T(8,128)S(1)} %get-tuple-element.8), channel_id=1, source_target_pairs={{4,0},{8,4},{12,8},{16,12},{20,16},{24,20},{28,24},{32,28},{36,32}... | collective-permute-start | bytes 245768 | tf_op jit(solution)/shard_map/ppermute | solution.py:349
  36.2 0.0 collective-permute-done.below_ref
  36.2 4.1 %collective-permute-done.1.above_ref = f32[2,2,40,128]{3,2,1,0:T(8,128)S(1)} collective-permute-done((f32[2,2,40,128]{3,2,1,0:T(8,128)S(1)}, f32[2,2,40,128]{3,2,1,0:T(8,128)S(1)}, u32[]{:S(2)}, u32[]{:S(2)}) %collective-permute-start.1) | collective-permute-done | bytes 81952 | tf_op jit(solution)/shard_map/ppermute | solution.py:349
  40.3 6.2 %shard_map.129.p_ref = f32[24,128]{1,0:T(8,128)S(1)} custom-call(f32[32,2,40,128]{3,2,1,0:T(8,128)S(1)} %all_to_all.15.r_ref, f32[2,2,40,128]{3,2,1,0:T(8,128)S(1)} %collective-permute-done.below_ref, f32[2,2,40,128]{3,2,1,0:T(8,128)S(1)} %collective-permute-done.1.above_ref, bf16[64,256]{1,0:T(8,128)(2,1)S(1)} %copy-done.7, f32[96,384]{1,0:T(8,128)S(1)} %copy-done.5, ...), custom_call_target="tpu_custom_call" | custom-call | tf_op jit(solution)/shard_map/pallas_call | solution.py:313
  46.4 3.7 %collective-permute-start.2 = (f32[24,128]{1,0:T(8,128)S(1)}, f32[24,128]{1,0:T(8,128)S(1)}, u32[]{:S(2)}, u32[]{:S(2)}) collective-permute-start(f32[24,128]{1,0:T(8,128)S(1)} %shard_map.129.p_ref), channel_id=1, source_target_pairs={{0,4},{4,8},{8,12},{12,16},{16,20},{20,24},{24,28},{28,32},{32,36}... | collective-permute-start | bytes 36872 | tf_op jit(solution)/shard_map/ppermute | solution.py:368
  50.1 1.3 %collective-permute-start.3 = (f32[24,128]{1,0:T(8,128)S(1)}, f32[24,128]{1,0:T(8,128)S(1)}, u32[]{:S(2)}, u32[]{:S(2)}) collective-permute-start(f32[24,128]{1,0:T(8,128)S(1)} %shard_map.129.p_ref), channel_id=1, source_target_pairs={{4,0},{8,4},{12,8},{16,12},{20,16},{24,20},{28,24},{32,28},{36,32}... | collective-permute-start | bytes 36872 | tf_op jit(solution)/shard_map/ppermute | solution.py:369
  51.4 4.8 %collective-permute-done.3.above_ref = f32[24,128]{1,0:T(8,128)S(1)} collective-permute-done((f32[24,128]{1,0:T(8,128)S(1)}, f32[24,128]{1,0:T(8,128)S(1)}, u32[]{:S(2)}, u32[]{:S(2)}) %collective-permute-start.3) | collective-permute-done | bytes 12320 | tf_op jit(solution)/shard_map/ppermute | solution.py:369
  56.3 0.8 shard_map.130
  57.1 6.2 %all-to-all-start.1 = ((f32[32,24,128]{2,1,0:T(8,128)}), f32[32,24,128]{2,1,0:T(8,128)S(1)}, u32[]{:S(2)}, u32[]{:S(2)}) async-start(f32[32,24,128]{2,1,0:T(8,128)} %shard_map.130), calls=%async_computation.1 | async-start | bytes 786432 | tf_op jit(solution)/shard_map/all_to_all | solution.py:379
  63.3 0.7 constant_dynamic-slice_fusion
  64.0 0.7 dynamic-slice_bitcast_fusion.1
  64.7 0.7 dynamic-slice_bitcast_fusion
  65.4 7.8 %all-to-all-done.1.g_ref = f32[32,24,128]{2,1,0:T(8,128)S(1)} async-done(((f32[32,24,128]{2,1,0:T(8,128)}), f32[32,24,128]{2,1,0:T(8,128)S(1)}, u32[]{:S(2)}, u32[]{:S(2)}) %all-to-all-start.1) | async-done | bytes 393248 | tf_op jit(solution)/shard_map/all_to_all | solution.py:379
  73.2 1.4 %shard_map.131 = f32[16,8,128]{2,1,0:T(8,128)} custom-call(f32[32,24,128]{2,1,0:T(8,128)S(1)} %all-to-all-done.1.g_ref, f32[1,128]{1,0:T(1,128)S(1)} %get-tuple-element.9.inv_ref, f32[256,256]{1,0:T(8,128)S(1)} %copy-done.3, f32[128,128]{1,0:T(8,128)S(1)} %copy-done.6), custom_call_target="tpu_custom_call" | custom-call | tf_op jit(solution)/shard_map/pallas_call | solution.py:313
  74.6 13.1 %all-to-all-start.2 = ((f32[16,8,128]{2,1,0:T(8,128)}), f32[16,8,128]{2,1,0:T(8,128)S(1)}, u32[]{:S(2)}, u32[]{:S(2)}) async-start(f32[16,8,128]{2,1,0:T(8,128)} %shard_map.131), calls=%async_computation.2 | async-start | bytes 131072 | tf_op jit(solution)/shard_map/all_to_all | solution.py:383
  87.7 11.6 %all-to-all-done.2.p_ref = f32[16,8,128]{2,1,0:T(8,128)S(1)} async-done(((f32[16,8,128]{2,1,0:T(8,128)}), f32[16,8,128]{2,1,0:T(8,128)S(1)}, u32[]{:S(2)}, u32[]{:S(2)}) %all-to-all-start.2) | async-done | bytes 65568 | tf_op jit(solution)/shard_map/all_to_all | solution.py:383
  99.3 2.6 %shard_map.132 = f32[384,1024]{1,0:T(8,128)} custom-call(f32[32,24,128]{2,1,0:T(8,128)S(1)} %all-to-all-done.1.g_ref, f32[128,128]{1,0:T(8,128)S(1)} %bitcast_multiply_fusion.e_ref, f32[256,1024]{1,0:T(8,128)S(1)} %copy-done, f32[16,8,128]{2,1,0:T(8,128)S(1)} %all-to-all-done.2.p_ref), custom_call_target="tpu_custom_call" | custom-call | tf_op jit(solution)/shard_map/pallas_call | solution.py:313
  (20 shorter events, 0.1 us)
Async XLA Ops:
  0.0 1.0 %copy-start.1 = (f32[8,16,1024]{2,1,0:T(8,128)S(1)}, f32[8,16,1024]{2,1,0:T(8,128)}, u32[]{:S(2)}) copy-start(f32[8,16,1024]{2,1,0:T(8,128)} %param.13) | copy-start | bytes 1572868
  1.0 1.0 %copy-start.2 = (f32[8,16,1024]{2,1,0:T(8,128)S(1)}, f32[8,16,1024]{2,1,0:T(8,128)}, u32[]{:S(2)}) copy-start(f32[8,16,1024]{2,1,0:T(8,128)} %param.14) | copy-start | bytes 1572868
  32.2 8.1 %copy-start.4 = (f32[4,128,128]{2,1,0:T(8,128)S(1)}, f32[4,128,128]{2,1,0:T(8,128)}, u32[]{:S(2)}) copy-start(f32[4,128,128]{2,1,0:T(8,128)} %constant.64.clone.place_ref) | copy-start | bytes 786436
  32.2 8.1 %copy-start.5 = (f32[96,384]{1,0:T(8,128)S(1)}, f32[96,384]{1,0:T(8,128)}, u32[]{:S(2)}) copy-start(f32[96,384]{1,0:T(8,128)} %constant.63.clone.fx_ref) | copy-start | bytes 442372
  32.2 8.1 %copy-start.7 = (bf16[64,256]{1,0:T(8,128)(2,1)S(1)}, bf16[64,256]{1,0:T(8,128)(2,1)}, u32[]{:S(2)}) copy-start(bf16[64,256]{1,0:T(8,128)(2,1)} %constant.62.clone.fz_ref) | copy-start | bytes 98308
  32.2 24.1 %copy-start.8 = (f32[1,128]{1,0:T(1,128)S(1)}, f32[1,128]{1,0:T(1,128)}, u32[]{:S(2)}) copy-start(f32[1,128]{1,0:T(1,128)} %constant.65.clone.low_ref) | copy-start | bytes 1540
  32.2 24.1 %copy-start.9 = (f32[1,128]{1,0:T(1,128)S(1)}, f32[1,128]{1,0:T(1,128)}, u32[]{:S(2)}) copy-start(f32[1,128]{1,0:T(1,128)} %constant.66.clone.high_ref) | copy-start | bytes 1540
  32.4 3.8 %collective-permute-start = (f32[2,2,40,128]{3,2,1,0:T(8,128)S(1)}, f32[2,2,40,128]{3,2,1,0:T(8,128)S(1)}, u32[]{:S(2)}, u32[]{:S(2)}) collective-permute-start(f32[2,2,40,128]{3,2,1,0:T(8,128)S(1)} %get-tuple-element.7), channel_id=1, source_target_pairs={{0,4},{4,8},{8,12},{12,16},{16,20},{20,24},{24,28},{28,32},{32,36}... | collective-permute-start | bytes 245768 | tf_op jit(solution)/shard_map/ppermute | solution.py:348
  34.7 38.5 %copy-start.3 = (f32[256,256]{1,0:T(8,128)S(1)}, f32[256,256]{1,0:T(8,128)}, u32[]{:S(2)}) copy-start(f32[256,256]{1,0:T(8,128)} %constant.67.clone.gx_ref) | copy-start | bytes 786436
  34.7 38.5 %copy-start.6 = (f32[128,128]{1,0:T(8,128)S(1)}, f32[128,128]{1,0:T(8,128)}, u32[]{:S(2)}) copy-start(f32[128,128]{1,0:T(8,128)} %constant.68.clone.gzy_ref) | copy-start | bytes 196612
  34.7 5.5 %collective-permute-start.1 = (f32[2,2,40,128]{3,2,1,0:T(8,128)S(1)}, f32[2,2,40,128]{3,2,1,0:T(8,128)S(1)}, u32[]{:S(2)}, u32[]{:S(2)}) collective-permute-start(f32[2,2,40,128]{3,2,1,0:T(8,128)S(1)} %get-tuple-element.8), channel_id=1, source_target_pairs={{4,0},{8,4},{12,8},{16,12},{20,16},{24,20},{28,24},{32,28},{36,32}... | collective-permute-start | bytes 245768 | tf_op jit(solution)/shard_map/ppermute | solution.py:349
  46.4 52.8 %copy-start = (f32[256,1024]{1,0:T(8,128)S(1)}, f32[256,1024]{1,0:T(8,128)}, u32[]{:S(2)}) copy-start(f32[256,1024]{1,0:T(8,128)} %constant.69.clone.w_ref) | copy-start | bytes 3145732
  46.4 5.0 %collective-permute-start.2 = (f32[24,128]{1,0:T(8,128)S(1)}, f32[24,128]{1,0:T(8,128)S(1)}, u32[]{:S(2)}, u32[]{:S(2)}) collective-permute-start(f32[24,128]{1,0:T(8,128)S(1)} %shard_map.129.p_ref), channel_id=1, source_target_pairs={{0,4},{4,8},{8,12},{12,16},{16,20},{20,24},{24,28},{28,32},{32,36}... | collective-permute-start | bytes 36872 | tf_op jit(solution)/shard_map/ppermute | solution.py:368
  50.1 6.1 %collective-permute-start.3 = (f32[24,128]{1,0:T(8,128)S(1)}, f32[24,128]{1,0:T(8,128)S(1)}, u32[]{:S(2)}, u32[]{:S(2)}) collective-permute-start(f32[24,128]{1,0:T(8,128)S(1)} %shard_map.129.p_ref), channel_id=1, source_target_pairs={{4,0},{8,4},{12,8},{16,12},{20,16},{24,20},{28,24},{32,28},{36,32}... | collective-permute-start | bytes 36872 | tf_op jit(solution)/shard_map/ppermute | solution.py:369
  57.1 16.1 %all-to-all-start.1 = ((f32[32,24,128]{2,1,0:T(8,128)}), f32[32,24,128]{2,1,0:T(8,128)S(1)}, u32[]{:S(2)}, u32[]{:S(2)}) async-start(f32[32,24,128]{2,1,0:T(8,128)} %shard_map.130), calls=%async_computation.1 | async-start | bytes 786432 | tf_op jit(solution)/shard_map/all_to_all | solution.py:379
  74.6 24.7 %all-to-all-start.2 = ((f32[16,8,128]{2,1,0:T(8,128)}), f32[16,8,128]{2,1,0:T(8,128)S(1)}, u32[]{:S(2)}, u32[]{:S(2)}) async-start(f32[16,8,128]{2,1,0:T(8,128)} %shard_map.131), calls=%async_computation.2 | async-start | bytes 131072 | tf_op jit(solution)/shard_map/all_to_all | solution.py:383

commit v3 on v2

--- a/solution.py
+++ b/solution.py
@@ -16,10 +16,19 @@
 XY = ("xy_0", "xy_1", "xy_2")
 GZ = ("gz_0", "gz_1")
 PLANE = ("gz_0", "gz_1", "xy_1", "xy_2")
+
+
+def member_of(slab, strip):
+    place = {"gz_0": slab // 2, "gz_1": slab % 2, "xy_1": strip // 2, "xy_2": strip % 2}
+    size = {"gz_0": 4, "gz_1": 2, "xy_1": 2, "xy_2": 2}
+    return functools.reduce(lambda total, axis: total * size[axis] + place[axis], PLANE, 0)
+
+
 SLABS, STRIPS, STACKS = 8, 4, 16
 MEMBERS = SLABS * STRIPS
 DEPTH, ROWS, WIDTH = 8, 16, 1024
 COLS = WIDTH // MEMBERS
+FROM_MIDDLE = sorted(range(STACKS), key=lambda i: abs(2 * i - STACKS))
 WIDE = COLS + 2 * RADIUS
 LANES = 128
 KZ = SLABS + 3
@@ -121,18 +130,25 @@
 NT = ((1,), (1,))
 
 
-def pack_kernel(f_ref, m_ref, o_ref, s_ref, b_ref):
+def pack_kernel(f_ref, m_ref, o_ref, s_ref, b_ref, t_ref, sem):
+    copies = [
+        pltpu.make_async_copy(ref, b_ref.at[image], sem.at[image])
+        for image, ref in enumerate((f_ref, m_ref))
+    ]
+    for copy in copies:
+        copy.start()
     zero = jnp.zeros((RADIUS, LANES), F32)
-    for image, ref in enumerate((f_ref, m_ref)):
+    for image in range(2):
         s_ref[image, 0:RADIUS, :] = zero
         s_ref[image, RADIUS + WIDTH : 2 * RADIUS + WIDTH, :] = zero
+    for image in range(2):
+        copies[image].wait()
         for block in range(WIDTH // LANES):
-            buf = b_ref.at[image, block]
-            buf[...] = ref[:, block * LANES : (block + 1) * LANES]
+            buf = t_ref.at[image, block]
+            buf[...] = b_ref[image, :, block * LANES : (block + 1) * LANES]
             rows = [buf[pl.ds(y, DEPTH, stride=ROWS), :] for y in range(ROWS)]
             tile = jnp.concatenate(rows, axis=0).T
             s_ref[image, RADIUS + block * LANES : RADIUS + (block + 1) * LANES, :] = tile
-    for image in range(2):
         for member in range(MEMBERS):
             o_ref[member, image] = s_ref[image, member * COLS : member * COLS + WIDE, :]
 
@@ -142,40 +158,29 @@
         for image in range(2):
             slabs = range(4 * half, 4 * half + 4)
             up_ref[half, image] = jnp.concatenate(
-                [r_ref[STRIPS * g + STRIPS - 1, image, :, 96:128] for g in slabs], axis=1
+                [r_ref[member_of(g, STRIPS - 1), image, :, 96:128] for g in slabs], axis=1
             )
             down_ref[half, image] = jnp.concatenate(
-                [r_ref[STRIPS * g, image, :, 0:32] for g in slabs], axis=1
+                [r_ref[member_of(g, 0), image, :, 0:32] for g in slabs], axis=1
             )
 
 
-def force_kernel(
-    r_ref, below_ref, above_ref, fz_ref, fx_ref, place_ref, o_ref, stack, rim_t, turned, mid, fr, acc
-):
+def window_x(v):
     roll = pltpu.roll
-
-    def window_x(v):
-        s = v + roll(v, WIDE - 1, 0)
-        s = s + roll(s, WIDE - 2, 0)
-        s = s + roll(s, WIDE - 4, 0)
-        return s[0:COLS] + v[2 * RADIUS : 2 * RADIUS + COLS]
-
-    def windows(f, m):
-        return [window_x(v) for v in (f, m, f * f, m * m, f * m)]
-
-    for half in range(2):
-        for at, ref in ((0, below_ref), (96, above_ref)):
-            values = windows(ref[half, 0], ref[half, 1])
-            values.append(ref[half, 1, RADIUS : RADIUS + COLS, :])
-            for item, v in enumerate(values):
-                stack[item, at : at + COLS, :] = v
-        for item in range(6):
-            stack[item, 32:96, :] = jnp.zeros((64, LANES), F32)
-            rim_t[half, item] = stack[item].T
-
+    s = v + roll(v, WIDE - 1, 0)
+    s = s + roll(s, WIDE - 2, 0)
+    s = s + roll(s, WIDE - 4, 0)
+    return s[0:COLS] + v[2 * RADIUS : 2 * RADIUS + COLS]
+
+
+def windows(f, m):
+    return [window_x(v) for v in (f, m, f * f, m * m, f * m)]
+
+
+def columns_kernel(r_ref, turned, stack):
     def phase_x(g, carry):
         for q in range(STRIPS):
-            i = g * STRIPS + q
+            i = member_of(g, q)
             values = windows(r_ref[i, 0], r_ref[i, 1])
             values.append(r_ref[i, 0, RADIUS : RADIUS + COLS, :])
             values.append(r_ref[i, 1, RADIUS : RADIUS + COLS, :])
@@ -194,6 +199,22 @@
 
     lax.fori_loop(0, SLABS, phase_x, 0)
 
+
+def force_kernel(
+    turned, below_ref, above_ref, fz_ref, fx_ref, place_ref, o_ref, stack, rim_t, summed, mid, fr, acc
+):
+    roll = pltpu.roll
+
+    for half in range(2):
+        for at, ref in ((0, below_ref), (96, above_ref)):
+            values = windows(ref[half, 0], ref[half, 1])
+            values.append(ref[half, 1, RADIUS : RADIUS + COLS, :])
+            for item, v in enumerate(values):
+                stack[item, at : at + COLS, :] = v
+        for item in range(6):
+            stack[item, 32:96, :] = jnp.zeros((64, LANES), F32)
+            rim_t[half, item] = stack[item].T
+
     lane = lax.broadcasted_iota(jnp.int32, (8, LANES), 1)
     first, last = lane < COLS, lane >= LANES - COLS
     row = lambda y: pl.ds(y * 8, 8) if not isinstance(y, int) else slice(y * 8, y * 8 + 8)
@@ -210,7 +231,7 @@
             s = [v[i] + v[i + 1] for i in range(23)]
             s = [s[i] + s[i + 2] for i in range(21)]
             for y in range(ROWS):
-                turned[field, g, row(y), :] = (s[y] + s[y + 4]) + v[y + 8]
+                summed[field, g, row(y), :] = (s[y] + s[y + 4]) + v[y + 8]
         m0 = turned[6, g, row(0), :]
         m15 = turned[6, g, row(15), :]
         mid[g, row(0), :] = jnp.where(first, near(5, 3), roll(m15, COLS, 1))
@@ -237,7 +258,7 @@
     inv = 1.0 / COUNT
 
     def phase_z(y, carry):
-        sums = [window_z([turned[field, g, row(y), :] for g in range(SLABS)]) for field in range(5)]
+        sums = [window_z([summed[field, g, row(y), :] for g in range(SLABS)]) for field in range(5)]
         m = [mid[g, row(y + 1), :] for g in range(SLABS)]
         fore = [roll(v, 7, 0) for v in m] + [zero]
         back = [zero] + [roll(v, 1, 0) for v in m]
@@ -284,37 +305,51 @@
         o_ref[member] = total
 
 
+def gathered(g_ref, k):
+    return jnp.concatenate([g_ref[p, 8 * k : 8 * k + 8, :] for p in range(MEMBERS)], axis=0)
+
+
 def power_kernel(g_ref, inv_ref, gx_ref, gzy_ref, o_ref):
+    parts = [gathered(g_ref, k) * inv_ref[...] for k in range(3)]
+    t = dot(gx_ref[...], jnp.concatenate(parts, axis=1), NN)
+    u = dot(jnp.concatenate(parts, axis=0), gzy_ref[...], NN)
     total = jnp.zeros((8, LANES), F32)
+    size = 8 * MEMBERS
     for k in range(3):
-        n = jnp.concatenate([g_ref[p, 8 * k : 8 * k + 8, :] for p in range(MEMBERS)], axis=0)
-        n = n * inv_ref[...]
-        t = dot(gx_ref[...], n, NN)
-        u = dot(n, gzy_ref[...], NN)
-        total += jnp.sum((t * u).reshape(MEMBERS, 8, LANES), axis=0)
+        product = t[:, k * LANES : (k + 1) * LANES] * u[k * size : (k + 1) * size]
+        total += jnp.sum(product.reshape(MEMBERS, 8, LANES), axis=0)
     total = jnp.full((8, LANES), jnp.sum(total), F32)
     for stack in range(STACKS):
         o_ref[stack] = total
 
 
-def field_kernel(size, g_ref, e_ref, w_ref, p_ref, o_ref):
+def field_kernel(g_ref, ez_ref, ey_ref, inv_ref, w_ref, o_ref):
+    ey = ey_ref[...]
+    rows = [ez_ref[z : z + 1] * ey for z in range(DEPTH)]
+    e = jnp.concatenate(rows, axis=0) * inv_ref[...]
+    h = dot(e, jnp.concatenate([gathered(g_ref, k) for k in range(3)], axis=0), NT)
+    size = 8 * MEMBERS
+    h = jnp.concatenate([h[:, k * size : (k + 1) * size] for k in range(3)], axis=0)
+    o_ref[...] = dot(h, w_ref[...], NN)
+
+
+def scale_kernel(size, f_ref, p_ref, o_ref):
     power = p_ref[0]
     for stack in range(1, STACKS):
         power = power + p_ref[stack]
     scale = 1.0 / (jnp.sqrt(power / size) + 1e-6)
-    e = e_ref[...]
-    for k in range(3):
-        n = jnp.concatenate([g_ref[p, 8 * k : 8 * k + 8, :] for p in range(MEMBERS)], axis=0)
-        h = dot(e, n, NT) * scale[0:1, 0:1]
-        o_ref[k * LANES : (k + 1) * LANES, :] = dot(h, w_ref[...], NN)
-
-
-def call(kernel, shapes, *args, scratch=()):
+    o_ref[...] = f_ref[...] * scale[0:1, 0:1]
+
+
+def call(kernel, shapes, *args, scratch=(), flops=0, **kw):
+    if flops:
+        kw["cost_estimate"] = pl.CostEstimate(flops=flops, transcendentals=0, bytes_accessed=1 << 20)
     return pl.pallas_call(
         kernel,
         out_shape=shapes,
         scratch_shapes=list(scratch),
-        compiler_params=pltpu.CompilerParams(vmem_limit_bytes=48 << 20),
+        compiler_params=pltpu.CompilerParams(vmem_limit_bytes=40 << 20),
+        **kw,
     )(*args)
 
 
@@ -330,36 +365,45 @@
     inverse = lax.dynamic_slice_in_dim(tab["inverse"], stack, 1, 0)
     ez = lax.dynamic_index_in_dim(tab["ez"], slab, 0, keepdims=False)
     ey = lax.dynamic_index_in_dim(tab["ey"], strip, 0, keepdims=False)
-    evals = (ez[:, None, :] * ey[None, :, :]).reshape(LANES, LANES) * inverse
 
     flat = (DEPTH * ROWS, WIDTH)
     chunks = call(
         pack_kernel,
         sds(MEMBERS, 2, WIDE, LANES),
-        fixed.reshape(flat),
-        moving.reshape(flat),
+        pltpu.with_memory_space_constraint(fixed.reshape(flat), pltpu.HBM),
+        pltpu.with_memory_space_constraint(moving.reshape(flat), pltpu.HBM),
         scratch=[
             pltpu.VMEM((2, WIDTH + 2 * RADIUS, LANES), F32),
+            pltpu.VMEM((2, LANES, WIDTH), F32),
             pltpu.VMEM((2, WIDTH // LANES, LANES, LANES), F32),
+            pltpu.SemaphoreType.DMA((2,)),
         ],
+        in_specs=[pl.BlockSpec(memory_space=pltpu.HBM)] * 2,
     )
     blocks = lax.all_to_all(chunks, PLANE, 0, 0)
     up, down = call(rim_kernel, (sds(2, 2, WIDE, LANES), sds(2, 2, WIDE, LANES)), blocks)
     below = lax.ppermute(up, "xy_0", upward)
     above = lax.ppermute(down, "xy_0", downward)
+    turned = call(
+        columns_kernel,
+        sds(8, SLABS, LANES, LANES),
+        blocks,
+        scratch=[pltpu.VMEM((8, LANES, LANES), F32)],
+        flops=1 << 31,
+    )
     part = call(
         force_kernel,
         sds(24, LANES),
-        blocks,
+        turned,
         below,
         above,
         tab["fit_zy"],
         tab["fit_x"],
         tab["place"],
         scratch=[
-            pltpu.VMEM((8, LANES, LANES), F32),
+            pltpu.VMEM((6, LANES, LANES), F32),
             pltpu.VMEM((2, 6, LANES, LANES), F32),
-            pltpu.VMEM((8, SLABS, LANES, LANES), F32),
+            pltpu.VMEM((5, SLABS, LANES, LANES), F32),
             pltpu.VMEM((SLABS, LANES + 16, LANES), F32),
             pltpu.VMEM((SLABS, LANES, 3 * LANES), F32),
             pltpu.VMEM((16, 8, 3 * LANES), F32),
@@ -380,15 +424,30 @@
     power = call(
         power_kernel, sds(STACKS, 8, LANES), numer, inverse, tab["gram_x"], tab["gram_zy"]
     )
-    powers = lax.all_to_all(power, "xy_0", 0, 0)
+    powers = lax.all_to_all(power, "xy_0", 0, 0, axis_index_groups=[FROM_MIDDLE])
     size = float(3 * SLABS * DEPTH * STACKS * STRIPS * ROWS * WIDTH)
     field = call(
-        functools.partial(field_kernel, size),
+        field_kernel,
         sds(3 * LANES, WIDTH),
         numer,
-        evals,
+        ez,
+        ey,
+        inverse,
         tab["wide_x"],
+        flops=1 << 31,
+    )
+    block = (LANES, WIDTH)
+    field = call(
+        functools.partial(scale_kernel, size),
+        sds(3 * LANES, WIDTH),
+        field,
         powers,
+        grid=(3,),
+        in_specs=[
+            pl.BlockSpec(block, lambda i: (i, 0)),
+            pl.BlockSpec((STACKS, 8, LANES), lambda i: (0, 0, 0)),
+        ],
+        out_specs=pl.BlockSpec(block, lambda i: (i, 0)),
     )
     return field.reshape(3, DEPTH, ROWS, WIDTH)
 

time: 102 us -> 92.7 us (0.909)
  waiting for transfers between devices: 28.3 us -> 16.6 us
  starting transfers between devices: 28 us -> 30.5 us
  local copies, waits for them, and re-layouts: 4.2 us -> 2.14 us
  Pallas kernels: 11.7 us -> 13.1 us
    all_to_all x1, waiting for transfers between devices: 11.6 us -> 1.35 us  [shards(): lax.all_to_all(power, 'xy_0', 0, 0, axis_index_groups=[FROM_MIDDLE])]
    all_to_all x1, starting transfers between devices: 13.1 us -> 15.6 us  [shards(): lax.all_to_all(power, 'xy_0', 0, 0, axis_index_groups=[FROM_MIDDLE])]
    ppermute x1, waiting for transfers between devices: 4.06 us -> 1.97 us  [shards(): above = lax.ppermute(down, 'xy_0', downward)]
    unnamed x20 -> x16, local copies, waits for them, and re-layouts: 2.12 us -> 0.05 us
    pallas_call x6 -> x8, Pallas kernels: 11.7 us -> 13.1 us  [call(): pl.pallas_call(kernel, out_shape=shapes, scratch_shapes=list(scratch), co...]
    mul x2 -> x0, local copies, waits for them, and re-layouts: 1.38 us -> none  [shards(): evals = (ez[:, None, :] * ey[None, :, :]).reshape(LANES, LANES) * inverse]
    squeeze x0 -> x2, local copies, waits for them, and re-layouts: none -> 1.38 us  [the longest x1 0.7 us: shards(): ey = lax.dynamic_index_in_dim(tab['ey'], strip, 0, keepdims=False)]
  transfers between devices with their start and end apart: 6 -> 6, of which waited for: 4 -> 4; matrix products, arithmetic and copies ran while one was open for 2% -> 2% of each run, Pallas kernels for 0% -> 3%
where the time goes in v3:
time: 92.7 us; the launch traced here: 92.1 us
  starting transfers between devices  30.5 us (33%)
  blocking collectives  29.5 us (32%)
  waiting for transfers between devices  16.6 us (18%)
  Pallas kernels  13.1 us (14%)
  local copies, waits for them, and re-layouts  2.14 us (2%)
    all_to_all x1, blocking collectives, shards(): blocks = lax.all_to_all(chunks, PLANE, 0, 0)  29.5 us
    all_to_all x1, starting transfers between devices, shards(): lax.all_to_all(power, 'xy_0', 0, 0, axis_index_groups=[FROM_MIDDLE])  15.6 us
    pallas_call x8, Pallas kernels, call(): pl.pallas_call(kernel, out_shape=shapes, scratch_shapes=list(scratch), co...  13.1 us
    all_to_all x1, waiting for transfers between devices, shards(): numer = lax.all_to_all(copies, PLANE, 0, 0)  8.48 us
    all_to_all x1, starting transfers between devices, shards(): numer = lax.all_to_all(copies, PLANE, 0, 0)  6.18 us
    ppermute x1, waiting for transfers between devices, shards(): above = lax.ppermute(part, 'xy_0', downward)  4.84 us
    ppermute x1, starting transfers between devices, shards(): below = lax.ppermute(part, 'xy_0', upward)  3.68 us
    ppermute x1, starting transfers between devices, shards(): below = lax.ppermute(up, 'xy_0', upward)  2.33 us
  transfers between devices with their start and end apart: 6, of which 4 were waited for; matrix products, arithmetic and copies ran while one was open for 2% of the time, Pallas kernels for 3%

profile of v3, /device:TPU:1, one launch (start us, length us, event | category | flops | bytes accessed | tf_op | source)
XLA Modules:
  0.0 92.1 jit_solution(9797024970067625073)
XLA Ops:
  0.0 1.7 %shard_map.127 = f32[32,2,40,128]{3,2,1,0:T(8,128)S(1)} custom-call(f32[128,1024]{1,0:T(8,128)} %bitcast.7, f32[128,1024]{1,0:T(8,128)} %bitcast.8), custom_call_target="tpu_custom_call" | custom-call | tf_op jit(solution)/shard_map/pallas_call | solution.py:347
  1.7 29.5 %all_to_all.15.r_ref = f32[32,2,40,128]{3,2,1,0:T(8,128)S(1)} all-to-all(f32[32,2,40,128]{3,2,1,0:T(8,128)S(1)} %shard_map.127), channel_id=1, replica_groups=mesh['gz_0'=4,'gz_1'=2,'xy_0'=16,'xy_1'=2,'xy_2'=2] {'gz_0','gz_1','xy_1..., dimensions={0} | all-to-all | bytes 2621440 | tf_op jit(solution)/shard_map/all_to_all | solution.py:383
  31.2 0.2 shard_map.129
  31.4 2.3 %collective-permute-start = (f32[2,2,40,128]{3,2,1,0:T(8,128)S(1)}, f32[2,2,40,128]{3,2,1,0:T(8,128)S(1)}, u32[]{:S(2)}, u32[]{:S(2)}) collective-permute-start(f32[2,2,40,128]{3,2,1,0:T(8,128)S(1)} %get-tuple-element.7), channel_id=1, source_target_pairs={{0,4},{4,8},{8,12},{12,16},{16,20},{20,24},{24,28},{28,32},{32,36}... | collective-permute-start | bytes 245768 | tf_op jit(solution)/shard_map/ppermute | solution.py:385
  33.8 0.0 copy-start
  33.8 0.0 copy-start.4
  33.8 1.4 %collective-permute-start.1 = (f32[2,2,40,128]{3,2,1,0:T(8,128)S(1)}, f32[2,2,40,128]{3,2,1,0:T(8,128)S(1)}, u32[]{:S(2)}, u32[]{:S(2)}) collective-permute-start(f32[2,2,40,128]{3,2,1,0:T(8,128)S(1)} %get-tuple-element.8), channel_id=1, source_target_pairs={{4,0},{8,4},{12,8},{16,12},{20,16},{24,20},{28,24},{32,28},{36,32}... | collective-permute-start | bytes 245768 | tf_op jit(solution)/shard_map/ppermute | solution.py:386
  35.2 2.0 %shard_map.128.turned = f32[8,8,128,128]{3,2,1,0:T(8,128)S(1)} custom-call(f32[32,2,40,128]{3,2,1,0:T(8,128)S(1)} %all_to_all.15.r_ref), custom_call_target="tpu_custom_call" | custom-call | flops 2147483648 | bytes 1048576 | tf_op jit(solution)/shard_map/pallas_call | solution.py:347
  37.3 2.0 %collective-permute-done.1.above_ref = f32[2,2,40,128]{3,2,1,0:T(8,128)S(1)} collective-permute-done((f32[2,2,40,128]{3,2,1,0:T(8,128)S(1)}, f32[2,2,40,128]{3,2,1,0:T(8,128)S(1)}, u32[]{:S(2)}, u32[]{:S(2)}) %collective-permute-start.1) | collective-permute-done | bytes 81952 | tf_op jit(solution)/shard_map/ppermute | solution.py:386
  39.3 4.2 %shard_map.130.p_ref = f32[24,128]{1,0:T(8,128)S(1)} custom-call(f32[8,8,128,128]{3,2,1,0:T(8,128)S(1)} %shard_map.128.turned, f32[2,2,40,128]{3,2,1,0:T(8,128)S(1)} %collective-permute-done.below_ref, f32[2,2,40,128]{3,2,1,0:T(8,128)S(1)} %collective-permute-done.1.above_ref, bf16[64,256]{1,0:T(8,128)(2,1)S(1)} %copy-done.4, f32[96,384]{1,0:T(8,128)S(1)} %copy-done.2, ...), custom_call_target="tpu_custom_call" | custom-call | tf_op jit(solution)/shard_map/pallas_call | solution.py:347
  43.5 3.7 %collective-permute-start.2 = (f32[24,128]{1,0:T(8,128)S(1)}, f32[24,128]{1,0:T(8,128)S(1)}, u32[]{:S(2)}, u32[]{:S(2)}) collective-permute-start(f32[24,128]{1,0:T(8,128)S(1)} %shard_map.130.p_ref), channel_id=1, source_target_pairs={{0,4},{4,8},{8,12},{12,16},{16,20},{20,24},{24,28},{28,32},{32,36}... | collective-permute-start | bytes 36872 | tf_op jit(solution)/shard_map/ppermute | solution.py:412
  47.2 1.3 %collective-permute-start.3 = (f32[24,128]{1,0:T(8,128)S(1)}, f32[24,128]{1,0:T(8,128)S(1)}, u32[]{:S(2)}, u32[]{:S(2)}) collective-permute-start(f32[24,128]{1,0:T(8,128)S(1)} %shard_map.130.p_ref), channel_id=1, source_target_pairs={{4,0},{8,4},{12,8},{16,12},{20,16},{24,20},{28,24},{32,28},{36,32}... | collective-permute-start | bytes 36872 | tf_op jit(solution)/shard_map/ppermute | solution.py:413
  48.5 4.8 %collective-permute-done.3.above_ref = f32[24,128]{1,0:T(8,128)S(1)} collective-permute-done((f32[24,128]{1,0:T(8,128)S(1)}, f32[24,128]{1,0:T(8,128)S(1)}, u32[]{:S(2)}, u32[]{:S(2)}) %collective-permute-start.3) | collective-permute-done | bytes 12320 | tf_op jit(solution)/shard_map/ppermute | solution.py:413
  53.4 0.8 shard_map.131
  54.2 6.2 %all-to-all-start.1 = ((f32[32,24,128]{2,1,0:T(8,128)}), f32[32,24,128]{2,1,0:T(8,128)S(1)}, u32[]{:S(2)}, u32[]{:S(2)}) async-start(f32[32,24,128]{2,1,0:T(8,128)} %shard_map.131), calls=%async_computation.1 | async-start | bytes 786432 | tf_op jit(solution)/shard_map/all_to_all | solution.py:423
  60.4 0.7 constant_dynamic-slice_fusion.inv_ref
  61.1 0.7 dynamic-slice_bitcast_fusion.ey_ref
  61.8 8.5 %all-to-all-done.1.g_ref = f32[32,24,128]{2,1,0:T(8,128)S(1)} async-done(((f32[32,24,128]{2,1,0:T(8,128)}), f32[32,24,128]{2,1,0:T(8,128)S(1)}, u32[]{:S(2)}, u32[]{:S(2)}) %all-to-all-start.1) | async-done | bytes 393248 | tf_op jit(solution)/shard_map/all_to_all | solution.py:423
  70.3 1.3 %shard_map.133 = f32[16,8,128]{2,1,0:T(8,128)} custom-call(f32[32,24,128]{2,1,0:T(8,128)S(1)} %all-to-all-done.1.g_ref, f32[1,128]{1,0:T(1,128)S(1)} %constant_dynamic-slice_fusion.inv_ref, f32[256,256]{1,0:T(8,128)S(1)} %copy-done.1, f32[128,128]{1,0:T(8,128)S(1)} %copy-done.3), custom_call_target="tpu_custom_call" | custom-call | tf_op jit(solution)/shard_map/pallas_call | solution.py:347
  71.6 15.6 %all-to-all-start.2 = ((f32[16,8,128]{2,1,0:T(8,128)}), f32[16,8,128]{2,1,0:T(8,128)S(1)}, u32[]{:S(2)}, u32[]{:S(2)}) async-start(f32[16,8,128]{2,1,0:T(8,128)} %shard_map.133), calls=%async_computation.2 | async-start | bytes 131072 | tf_op jit(solution)/shard_map/all_to_all | solution.py:427
  87.2 0.7 dynamic-slice_bitcast_fusion.1.ez_ref
  87.9 1.1 %shard_map.132.f_ref = f32[384,1024]{1,0:T(8,128)S(1)} custom-call(f32[32,24,128]{2,1,0:T(8,128)S(1)} %all-to-all-done.1.g_ref, f32[8,128]{1,0:T(8,128)S(1)} %dynamic-slice_bitcast_fusion.1.ez_ref, f32[16,128]{1,0:T(8,128)S(1)} %dynamic-slice_bitcast_fusion.ey_ref, f32[1,128]{1,0:T(1,128)S(1)} %constant_dynamic-slice_fusion.inv_ref, f32[256,1024]{1,0:T(8,128)S(1)} %copy-done.7), custom_call_target="tpu_custom_call" | custom-call | flops 2147483648 | bytes 1048576 | tf_op jit(solution)/shard_map/pallas_call | solution.py:347
  89.0 1.3 %all-to-all-done.2.p_ref = f32[16,8,128]{2,1,0:T(8,128)S(1)} async-done(((f32[16,8,128]{2,1,0:T(8,128)}), f32[16,8,128]{2,1,0:T(8,128)S(1)}, u32[]{:S(2)}, u32[]{:S(2)}) %all-to-all-start.2) | async-done | bytes 65568 | tf_op jit(solution)/shard_map/all_to_all | solution.py:427
  90.3 1.8 %shard_map.134 = f32[384,1024]{1,0:T(8,128)} custom-call(f32[384,1024]{1,0:T(8,128)S(1)} %shard_map.132.f_ref, f32[16,8,128]{2,1,0:T(8,128)S(1)} %all-to-all-done.2.p_ref), custom_call_target="tpu_custom_call" | custom-call | tf_op jit(solution)/shard_map/pallas_call | solution.py:347
  (16 shorter events, 0.0 us)
Async XLA Ops:
  31.4 5.9 %collective-permute-start = (f32[2,2,40,128]{3,2,1,0:T(8,128)S(1)}, f32[2,2,40,128]{3,2,1,0:T(8,128)S(1)}, u32[]{:S(2)}, u32[]{:S(2)}) collective-permute-start(f32[2,2,40,128]{3,2,1,0:T(8,128)S(1)} %get-tuple-element.7), channel_id=1, source_target_pairs={{0,4},{4,8},{8,12},{12,16},{16,20},{20,24},{24,28},{28,32},{32,36}... | collective-permute-start | bytes 245768 | tf_op jit(solution)/shard_map/ppermute | solution.py:385
  33.8 5.5 %copy-start = (f32[4,128,128]{2,1,0:T(8,128)S(1)}, f32[4,128,128]{2,1,0:T(8,128)}, u32[]{:S(2)}) copy-start(f32[4,128,128]{2,1,0:T(8,128)} %constant.64.clone.place_ref) | copy-start | bytes 786436
  33.8 5.5 %copy-start.2 = (f32[96,384]{1,0:T(8,128)S(1)}, f32[96,384]{1,0:T(8,128)}, u32[]{:S(2)}) copy-start(f32[96,384]{1,0:T(8,128)} %constant.63.clone.fx_ref) | copy-start | bytes 442372
  33.8 5.5 %copy-start.4 = (bf16[64,256]{1,0:T(8,128)(2,1)S(1)}, bf16[64,256]{1,0:T(8,128)(2,1)}, u32[]{:S(2)}) copy-start(bf16[64,256]{1,0:T(8,128)(2,1)} %constant.62.clone.fz_ref) | copy-start | bytes 98308
  33.8 5.5 %collective-permute-start.1 = (f32[2,2,40,128]{3,2,1,0:T(8,128)S(1)}, f32[2,2,40,128]{3,2,1,0:T(8,128)S(1)}, u32[]{:S(2)}, u32[]{:S(2)}) collective-permute-start(f32[2,2,40,128]{3,2,1,0:T(8,128)S(1)} %get-tuple-element.8), channel_id=1, source_target_pairs={{4,0},{8,4},{12,8},{16,12},{20,16},{24,20},{28,24},{32,28},{36,32}... | collective-permute-start | bytes 245768 | tf_op jit(solution)/shard_map/ppermute | solution.py:386
  37.3 16.1 %copy-start.5 = (f32[1,128]{1,0:T(1,128)S(1)}, f32[1,128]{1,0:T(1,128)}, u32[]{:S(2)}) copy-start(f32[1,128]{1,0:T(1,128)} %constant.65.clone.low_ref) | copy-start | bytes 1540
  37.3 16.1 %copy-start.6 = (f32[1,128]{1,0:T(1,128)S(1)}, f32[1,128]{1,0:T(1,128)}, u32[]{:S(2)}) copy-start(f32[1,128]{1,0:T(1,128)} %constant.66.clone.high_ref) | copy-start | bytes 1540
  37.3 33.0 %copy-start.1 = (f32[256,256]{1,0:T(8,128)S(1)}, f32[256,256]{1,0:T(8,128)}, u32[]{:S(2)}) copy-start(f32[256,256]{1,0:T(8,128)} %constant.67.clone.gx_ref) | copy-start | bytes 786436
  37.3 33.0 %copy-start.3 = (f32[128,128]{1,0:T(8,128)S(1)}, f32[128,128]{1,0:T(8,128)}, u32[]{:S(2)}) copy-start(f32[128,128]{1,0:T(8,128)} %constant.68.clone.gzy_ref) | copy-start | bytes 196612
  43.5 44.4 %copy-start.7 = (f32[256,1024]{1,0:T(8,128)S(1)}, f32[256,1024]{1,0:T(8,128)}, u32[]{:S(2)}) copy-start(f32[256,1024]{1,0:T(8,128)} %constant.69.clone.w_ref) | copy-start | bytes 3145732
  43.5 5.0 %collective-permute-start.2 = (f32[24,128]{1,0:T(8,128)S(1)}, f32[24,128]{1,0:T(8,128)S(1)}, u32[]{:S(2)}, u32[]{:S(2)}) collective-permute-start(f32[24,128]{1,0:T(8,128)S(1)} %shard_map.130.p_ref), channel_id=1, source_target_pairs={{0,4},{4,8},{8,12},{12,16},{16,20},{20,24},{24,28},{28,32},{32,36}... | collective-permute-start | bytes 36872 | tf_op jit(solution)/shard_map/ppermute | solution.py:412
  47.2 6.1 %collective-permute-start.3 = (f32[24,128]{1,0:T(8,128)S(1)}, f32[24,128]{1,0:T(8,128)S(1)}, u32[]{:S(2)}, u32[]{:S(2)}) collective-permute-start(f32[24,128]{1,0:T(8,128)S(1)} %shard_map.130.p_ref), channel_id=1, source_target_pairs={{4,0},{8,4},{12,8},{16,12},{20,16},{24,20},{28,24},{32,28},{36,32}... | collective-permute-start | bytes 36872 | tf_op jit(solution)/shard_map/ppermute | solution.py:413
  54.2 16.1 %all-to-all-start.1 = ((f32[32,24,128]{2,1,0:T(8,128)}), f32[32,24,128]{2,1,0:T(8,128)S(1)}, u32[]{:S(2)}, u32[]{:S(2)}) async-start(f32[32,24,128]{2,1,0:T(8,128)} %shard_map.131), calls=%async_computation.1 | async-start | bytes 786432 | tf_op jit(solution)/shard_map/all_to_all | solution.py:423
  71.6 18.8 %all-to-all-start.2 = ((f32[16,8,128]{2,1,0:T(8,128)}), f32[16,8,128]{2,1,0:T(8,128)S(1)}, u32[]{:S(2)}, u32[]{:S(2)}) async-start(f32[16,8,128]{2,1,0:T(8,128)} %shard_map.133), calls=%async_computation.2 | async-start | bytes 131072 | tf_op jit(solution)/shard_map/all_to_all | solution.py:427

commit v4 on v3

--- a/solution.py
+++ b/solution.py
@@ -31,6 +31,7 @@
 FROM_MIDDLE = sorted(range(STACKS), key=lambda i: abs(2 * i - STACKS))
 WIDE = COLS + 2 * RADIUS
 LANES = 128
+PARTS = 6
 KZ = SLABS + 3
 KY = STRIPS * ROWS // SPACING + 3
 F32 = jnp.float32
@@ -75,7 +76,7 @@
         for a in range(KZ):
             for b in range(5):
                 place[q, a, b, KY * a + 2 * q + b] = 1.0
-    place = place.reshape(STRIPS, LANES, LANES)
+    place = place.reshape(STRIPS * LANES, LANES)
     knots_x = WIDTH // SPACING + 3
     mass_x = np_mass(knots_x, WIDTH)
     full_x = np_basis(np.arange(WIDTH)[None, :], np.arange(knots_x)[:, None]) / mass_x[:, None]
@@ -109,7 +110,7 @@
     low_zy = (fit_zy - high_zy.astype(np.float32)).astype(jnp.bfloat16)
     fit_zy = np.block([[high_zy, high_zy], [low_zy, np.zeros_like(low_zy)]])
     return dict(
-        fit_zy=fit_zy, place=f(place), fit_x=f(fit_x), wide_x=f(wide_x), gram_x=f(gram_x), gram_zy=f(gram_zy),
+        fit_zy=fit_zy, place=np.asarray(place, jnp.bfloat16), fit_x=f(fit_x), wide_x=f(wide_x), gram_x=f(gram_x), gram_zy=f(gram_zy),
         inverse=f(inverse), ez=f(ez_l), ey=f(ey_l), low=f(low), high=f(high),
     )
 
@@ -291,10 +292,10 @@
         for a in range(4):
             acc[g + a] += part[8 * a : 8 * a + 8] + part[32 + 8 * a : 40 + 8 * a]
     wide = dot(fx_ref[...], acc[...].reshape(LANES, 3 * LANES), NT)
-    total = dot(wide[0:24], place_ref[0], NN)
-    for q in range(1, STRIPS):
-        total += dot(wide[24 * q : 24 * q + 24], place_ref[q], NN)
-    o_ref[...] = total
+    wide = jnp.concatenate([wide[24 * q : 24 * q + 24] for q in range(STRIPS)], axis=1)
+    mm = lambda u: lax.dot_general(u, place_ref[...], (NN, ((), ())), preferred_element_type=F32)
+    hi, lo = split(wide)
+    o_ref[...] = mm(hi) + mm(lo)
 
 
 def fold_kernel(p_ref, below_ref, above_ref, low_ref, high_ref, o_ref):
@@ -310,13 +311,20 @@
 
 
 def power_kernel(g_ref, inv_ref, gx_ref, gzy_ref, o_ref):
-    parts = [gathered(g_ref, k) * inv_ref[...] for k in range(3)]
-    t = dot(gx_ref[...], jnp.concatenate(parts, axis=1), NN)
-    u = dot(jnp.concatenate(parts, axis=0), gzy_ref[...], NN)
+    inverse = inv_ref[pl.ds(lax.axis_index("xy_0"), 1), :]
+    parts = [gathered(g_ref, k) * inverse for k in range(3)]
+    mm = lambda u, v: lax.dot_general(u, v, (NN, ((), ())), preferred_element_type=F32)
+    halves = [split(part) for part in parts]
+    high = jnp.concatenate([h for h, _ in halves], axis=1)
+    low = jnp.concatenate([l for _, l in halves], axis=1)
+    gh, gl = split(gx_ref[...])
+    t = mm(gh, high) + mm(gh, low) + mm(gl, high)
+    zh, zl = split(gzy_ref[...])
+    zz = jnp.concatenate([zh, zh], axis=0)
     total = jnp.zeros((8, LANES), F32)
-    size = 8 * MEMBERS
-    for k in range(3):
-        product = t[:, k * LANES : (k + 1) * LANES] * u[k * size : (k + 1) * size]
+    for k, (h, l) in enumerate(halves):
+        u = mm(jnp.concatenate([h, l], axis=1), zz) + mm(h, zl)
+        product = t[:, k * LANES : (k + 1) * LANES] * u
         total += jnp.sum(product.reshape(MEMBERS, 8, LANES), axis=0)
     total = jnp.full((8, LANES), jnp.sum(total), F32)
     for stack in range(STACKS):
@@ -324,21 +332,30 @@
 
 
 def field_kernel(g_ref, ez_ref, ey_ref, inv_ref, w_ref, o_ref):
-    ey = ey_ref[...]
-    rows = [ez_ref[z : z + 1] * ey for z in range(DEPTH)]
-    e = jnp.concatenate(rows, axis=0) * inv_ref[...]
+    ez = ez_ref[2 * lax.axis_index("gz_0") + lax.axis_index("gz_1")]
+    ey = ey_ref[2 * lax.axis_index("xy_1") + lax.axis_index("xy_2")]
+    rows = [ez[z : z + 1] * ey for z in range(DEPTH)]
+    e = jnp.concatenate(rows, axis=0) * inv_ref[pl.ds(lax.axis_index("xy_0"), 1), :]
     h = dot(e, jnp.concatenate([gathered(g_ref, k) for k in range(3)], axis=0), NT)
     size = 8 * MEMBERS
     h = jnp.concatenate([h[:, k * size : (k + 1) * size] for k in range(3)], axis=0)
     o_ref[...] = dot(h, w_ref[...], NN)
 
 
-def scale_kernel(size, f_ref, p_ref, o_ref):
+def scale_kernel(size, f_ref, p_ref, o_ref, s_ref, sem):
     power = p_ref[0]
     for stack in range(1, STACKS):
         power = power + p_ref[stack]
-    scale = 1.0 / (jnp.sqrt(power / size) + 1e-6)
-    o_ref[...] = f_ref[...] * scale[0:1, 0:1]
+    scale = (1.0 / (jnp.sqrt(power / size) + 1e-6))[0:1, 0:1]
+    part = 3 * LANES // PARTS
+    copies = []
+    for i in range(PARTS):
+        at = pl.ds(i * part, part)
+        s_ref[at] = f_ref[at] * scale
+        copies.append(pltpu.make_async_copy(s_ref.at[at], o_ref.at[at], sem.at[i]))
+        copies[-1].start()
+    for copy in copies:
+        copy.wait()
 
 
 def call(kernel, shapes, *args, scratch=(), flops=0, **kw):
@@ -356,15 +373,8 @@
 def shards(fixed, moving):
     tab = tables()
     sds = lambda *shape: jax.ShapeDtypeStruct(shape, F32)
-    stack = lax.axis_index("xy_0")
-    slab = lax.axis_index(GZ)
-    strip = lax.axis_index(("xy_1", "xy_2"))
     upward = [(i, i + 1) for i in range(STACKS - 1)]
     downward = [(i + 1, i) for i in range(STACKS - 1)]
-
-    inverse = lax.dynamic_slice_in_dim(tab["inverse"], stack, 1, 0)
-    ez = lax.dynamic_index_in_dim(tab["ez"], slab, 0, keepdims=False)
-    ey = lax.dynamic_index_in_dim(tab["ey"], strip, 0, keepdims=False)
 
     flat = (DEPTH * ROWS, WIDTH)
     chunks = call(
@@ -422,7 +432,7 @@
     )
     numer = lax.all_to_all(copies, PLANE, 0, 0)
     power = call(
-        power_kernel, sds(STACKS, 8, LANES), numer, inverse, tab["gram_x"], tab["gram_zy"]
+        power_kernel, sds(STACKS, 8, LANES), numer, tab["inverse"], tab["gram_x"], tab["gram_zy"]
     )
     powers = lax.all_to_all(power, "xy_0", 0, 0, axis_index_groups=[FROM_MIDDLE])
     size = float(3 * SLABS * DEPTH * STACKS * STRIPS * ROWS * WIDTH)
@@ -430,24 +440,19 @@
         field_kernel,
         sds(3 * LANES, WIDTH),
         numer,
-        ez,
-        ey,
-        inverse,
+        tab["ez"],
+        tab["ey"],
+        tab["inverse"],
         tab["wide_x"],
         flops=1 << 31,
     )
-    block = (LANES, WIDTH)
     field = call(
         functools.partial(scale_kernel, size),
         sds(3 * LANES, WIDTH),
         field,
         powers,
-        grid=(3,),
-        in_specs=[
-            pl.BlockSpec(block, lambda i: (i, 0)),
-            pl.BlockSpec((STACKS, 8, LANES), lambda i: (0, 0, 0)),
-        ],
-        out_specs=pl.BlockSpec(block, lambda i: (i, 0)),
+        scratch=[pltpu.VMEM((3 * LANES, WIDTH), F32), pltpu.SemaphoreType.DMA((PARTS,))],
+        out_specs=pl.BlockSpec(memory_space=pltpu.HBM),
     )
     return field.reshape(3, DEPTH, ROWS, WIDTH)
 

time: 92.7 us -> 93 us (level)
  blocking collectives: 29.5 us -> 45.6 us
  waiting for transfers between devices: 16.6 us -> 4.77 us
  local copies, waits for them, and re-layouts: 2.14 us -> 0.08 us
  Pallas kernels: 13.1 us -> 11.7 us
    all_to_all x0 -> x1, blocking collectives: none -> 16.1 us  [shards(): numer = lax.all_to_all(copies, PLANE, 0, 0)]
    all_to_all x1 -> x0, waiting for transfers between devices: 8.48 us -> none  [shards(): numer = lax.all_to_all(copies, PLANE, 0, 0)]
    all_to_all x1 -> x0, starting transfers between devices: 6.18 us -> none  [shards(): numer = lax.all_to_all(copies, PLANE, 0, 0)]
    all_to_all x1, starting transfers between devices: 15.6 us -> 20.9 us  [shards(): lax.all_to_all(power, 'xy_0', 0, 0, axis_index_groups=[FROM_MIDDLE])]
    ppermute x1, waiting for transfers between devices: 4.84 us -> 0.01 us  [shards(): above = lax.ppermute(part, 'xy_0', downward)]
    pallas_call x8, Pallas kernels: 13.1 us -> 11.7 us  [call(): pl.pallas_call(kernel, out_shape=shapes, scratch_shapes=list(scratch), co...]
    squeeze x2 -> x0, local copies, waits for them, and re-layouts: 1.38 us -> none  [the longest x1 0.7 us: shards(): ey = lax.dynamic_index_in_dim(tab['ey'], strip, 0, keepdims=False)]
  transfers between devices with their start and end apart: 6 -> 5, of which waited for: 4 -> 3; matrix products, arithmetic and copies ran while one was open for 2% -> 0% of each run, Pallas kernels for 3% -> 3%
where the time goes in v4:
time: 93 us; the launch traced here: 92.6 us
  blocking collectives  45.6 us (49%)
  starting transfers between devices  30.3 us (33%)
  Pallas kernels  11.7 us (13%)
  waiting for transfers between devices  4.77 us (5%)
    all_to_all x1, blocking collectives, shards(): blocks = lax.all_to_all(chunks, PLANE, 0, 0)  29.5 us
    all_to_all x1, starting transfers between devices, shards(): lax.all_to_all(power, 'xy_0', 0, 0, axis_index_groups=[FROM_MIDDLE])  20.9 us
    all_to_all x1, blocking collectives, shards(): numer = lax.all_to_all(copies, PLANE, 0, 0)  16.1 us
    pallas_call x8, Pallas kernels, call(): pl.pallas_call(kernel, out_shape=shapes, scratch_shapes=list(scratch), co...  11.7 us
    ppermute x1, starting transfers between devices, shards(): below = lax.ppermute(part, 'xy_0', upward)  4.17 us
    ppermute x1, starting transfers between devices, shards(): below = lax.ppermute(up, 'xy_0', upward)  2.33 us
    all_to_all x1, waiting for transfers between devices, shards(): lax.all_to_all(power, 'xy_0', 0, 0, axis_index_groups=[FROM_MIDDLE])  2 us
    ppermute x1, waiting for transfers between devices, shards(): above = lax.ppermute(down, 'xy_0', downward)  1.96 us
  transfers between devices with their start and end apart: 5, of which 3 were waited for; matrix products, arithmetic and copies ran while one was open for 0% of the time, Pallas kernels for 3%

profile of v4, /device:TPU:1, one launch (start us, length us, event | category | flops | bytes accessed | tf_op | source)
XLA Modules:
  0.0 92.6 jit_solution(11464887380890818791)
XLA Ops:
  0.0 1.7 %shard_map.127 = f32[32,2,40,128]{3,2,1,0:T(8,128)S(1)} custom-call(f32[128,1024]{1,0:T(8,128)} %bitcast.3, f32[128,1024]{1,0:T(8,128)} %bitcast.4), custom_call_target="tpu_custom_call" | custom-call | tf_op jit(solution)/shard_map/pallas_call | solution.py:364
  1.7 29.5 %all_to_all.15.r_ref = f32[32,2,40,128]{3,2,1,0:T(8,128)S(1)} all-to-all(f32[32,2,40,128]{3,2,1,0:T(8,128)S(1)} %shard_map.127), channel_id=1, replica_groups=mesh['gz_0'=4,'gz_1'=2,'xy_0'=16,'xy_1'=2,'xy_2'=2] {'gz_0','gz_1','xy_1..., dimensions={0} | all-to-all | bytes 2621440 | tf_op jit(solution)/shard_map/all_to_all | solution.py:393
  31.2 0.2 shard_map.129
  31.4 2.3 %collective-permute-start = (f32[2,2,40,128]{3,2,1,0:T(8,128)S(1)}, f32[2,2,40,128]{3,2,1,0:T(8,128)S(1)}, u32[]{:S(2)}, u32[]{:S(2)}) collective-permute-start(f32[2,2,40,128]{3,2,1,0:T(8,128)S(1)} %get-tuple-element.7), channel_id=1, source_target_pairs={{0,4},{4,8},{8,12},{12,16},{16,20},{20,24},{24,28},{28,32},{32,36}... | collective-permute-start | bytes 245768 | tf_op jit(solution)/shard_map/ppermute | solution.py:395
  33.8 0.0 copy-start.1
  33.8 0.0 copy-start.4
  33.8 1.4 %collective-permute-start.1 = (f32[2,2,40,128]{3,2,1,0:T(8,128)S(1)}, f32[2,2,40,128]{3,2,1,0:T(8,128)S(1)}, u32[]{:S(2)}, u32[]{:S(2)}) collective-permute-start(f32[2,2,40,128]{3,2,1,0:T(8,128)S(1)} %get-tuple-element.8), channel_id=1, source_target_pairs={{4,0},{8,4},{12,8},{16,12},{20,16},{24,20},{28,24},{32,28},{36,32}... | collective-permute-start | bytes 245768 | tf_op jit(solution)/shard_map/ppermute | solution.py:396
  35.2 2.0 %shard_map.128.turned = f32[8,8,128,128]{3,2,1,0:T(8,128)S(1)} custom-call(f32[32,2,40,128]{3,2,1,0:T(8,128)S(1)} %all_to_all.15.r_ref), custom_call_target="tpu_custom_call" | custom-call | flops 2147483648 | bytes 1048576 | tf_op jit(solution)/shard_map/pallas_call | solution.py:364
  37.3 0.0 copy-start.6
  37.3 0.0 copy-start.7
  37.3 0.0 copy-start
  37.3 0.0 copy-start.5
  37.3 2.0 %collective-permute-done.1.above_ref = f32[2,2,40,128]{3,2,1,0:T(8,128)S(1)} collective-permute-done((f32[2,2,40,128]{3,2,1,0:T(8,128)S(1)}, f32[2,2,40,128]{3,2,1,0:T(8,128)S(1)}, u32[]{:S(2)}, u32[]{:S(2)}) %collective-permute-start.1) | collective-permute-done | bytes 81952 | tf_op jit(solution)/shard_map/ppermute | solution.py:396
  39.3 4.0 %shard_map.130.p_ref = f32[24,128]{1,0:T(8,128)S(1)} custom-call(f32[8,8,128,128]{3,2,1,0:T(8,128)S(1)} %shard_map.128.turned, f32[2,2,40,128]{3,2,1,0:T(8,128)S(1)} %collective-permute-done.below_ref, f32[2,2,40,128]{3,2,1,0:T(8,128)S(1)} %collective-permute-done.1.above_ref, bf16[64,256]{1,0:T(8,128)(2,1)S(1)} %copy-done.4, f32[96,384]{1,0:T(8,128)S(1)} %copy-done.1, ...), custom_call_target="tpu_custom_call" | custom-call | tf_op jit(solution)/shard_map/pallas_call | solution.py:364
  43.4 1.4 %collective-permute-start.3 = (f32[24,128]{1,0:T(8,128)S(1)}, f32[24,128]{1,0:T(8,128)S(1)}, u32[]{:S(2)}, u32[]{:S(2)}) collective-permute-start(f32[24,128]{1,0:T(8,128)S(1)} %shard_map.130.p_ref), channel_id=1, source_target_pairs={{4,0},{8,4},{12,8},{16,12},{20,16},{24,20},{28,24},{32,28},{36,32}... | collective-permute-start | bytes 36872 | tf_op jit(solution)/shard_map/ppermute | solution.py:423
  44.8 4.2 %collective-permute-start.2 = (f32[24,128]{1,0:T(8,128)S(1)}, f32[24,128]{1,0:T(8,128)S(1)}, u32[]{:S(2)}, u32[]{:S(2)}) collective-permute-start(f32[24,128]{1,0:T(8,128)S(1)} %shard_map.130.p_ref), channel_id=1, source_target_pairs={{0,4},{4,8},{8,12},{12,16},{16,20},{20,24},{24,28},{28,32},{32,36}... | collective-permute-start | bytes 36872 | tf_op jit(solution)/shard_map/ppermute | solution.py:422
  49.0 0.8 collective-permute-done.2.below_ref
  49.8 0.1 shard_map.131
  49.9 16.1 %all_to_all.16.g_ref = f32[32,24,128]{2,1,0:T(8,128)S(1)} all-to-all(f32[32,24,128]{2,1,0:T(8,128)S(1)} %shard_map.131), channel_id=1, replica_groups=mesh['gz_0'=4,'gz_1'=2,'xy_0'=16,'xy_1'=2,'xy_2'=2] {'gz_0','gz_1','xy_1..., dimensions={0} | all-to-all | bytes 786432 | tf_op jit(solution)/shard_map/all_to_all | solution.py:433
  66.0 1.3 %shard_map.133 = f32[16,8,128]{2,1,0:T(8,128)} custom-call(f32[32,24,128]{2,1,0:T(8,128)S(1)} %all_to_all.16.g_ref, f32[16,128]{1,0:T(8,128)S(1)} %copy-done.5, f32[256,256]{1,0:T(8,128)S(1)} %copy-done, f32[128,128]{1,0:T(8,128)S(1)} %copy-done.3), custom_call_target="tpu_custom_call" | custom-call | tf_op jit(solution)/shard_map/pallas_call | solution.py:364
  67.3 20.9 %all-to-all-start.2 = ((f32[16,8,128]{2,1,0:T(8,128)}), f32[16,8,128]{2,1,0:T(8,128)S(1)}, u32[]{:S(2)}, u32[]{:S(2)}) async-start(f32[16,8,128]{2,1,0:T(8,128)} %shard_map.133), calls=%async_computation.2 | async-start | bytes 131072 | tf_op jit(solution)/shard_map/all_to_all | solution.py:437
  88.2 1.1 %shard_map.132.f_ref = f32[384,1024]{1,0:T(8,128)S(1)} custom-call(f32[32,24,128]{2,1,0:T(8,128)S(1)} %all_to_all.16.g_ref, f32[8,8,128]{2,1,0:T(8,128)S(1)} %copy-done.10, f32[4,16,128]{2,1,0:T(8,128)S(1)} %copy-done.9, f32[16,128]{1,0:T(8,128)S(1)} %copy-done.5, f32[256,1024]{1,0:T(8,128)S(1)} %copy-done.8), custom_call_target="tpu_custom_call" | custom-call | flops 2147483648 | bytes 1048576 | tf_op jit(solution)/shard_map/pallas_call | solution.py:364
  89.4 2.0 %all-to-all-done.2.p_ref = f32[16,8,128]{2,1,0:T(8,128)S(1)} async-done(((f32[16,8,128]{2,1,0:T(8,128)}), f32[16,8,128]{2,1,0:T(8,128)S(1)}, u32[]{:S(2)}, u32[]{:S(2)}) %all-to-all-start.2) | async-done | bytes 65568 | tf_op jit(solution)/shard_map/all_to_all | solution.py:437
  91.4 1.3 %shard_map.134 = f32[384,1024]{1,0:T(8,128)} custom-call(f32[384,1024]{1,0:T(8,128)S(1)} %shard_map.132.f_ref, f32[16,8,128]{2,1,0:T(8,128)S(1)} %all-to-all-done.2.p_ref), custom_call_target="tpu_custom_call" | custom-call | tf_op jit(solution)/shard_map/pallas_call | solution.py:364
  (18 shorter events, 0.1 us)
Async XLA Ops:
  31.4 5.9 %collective-permute-start = (f32[2,2,40,128]{3,2,1,0:T(8,128)S(1)}, f32[2,2,40,128]{3,2,1,0:T(8,128)S(1)}, u32[]{:S(2)}, u32[]{:S(2)}) collective-permute-start(f32[2,2,40,128]{3,2,1,0:T(8,128)S(1)} %get-tuple-element.7), channel_id=1, source_target_pairs={{0,4},{4,8},{8,12},{12,16},{16,20},{20,24},{24,28},{28,32},{32,36}... | collective-permute-start | bytes 245768 | tf_op jit(solution)/shard_map/ppermute | solution.py:395
  33.8 5.5 %copy-start.1 = (f32[96,384]{1,0:T(8,128)S(1)}, f32[96,384]{1,0:T(8,128)}, u32[]{:S(2)}) copy-start(f32[96,384]{1,0:T(8,128)} %constant.23.clone.fx_ref) | copy-start | bytes 442372
  33.8 5.5 %copy-start.2 = (bf16[512,128]{1,0:T(8,128)(2,1)S(1)}, bf16[512,128]{1,0:T(8,128)(2,1)}, u32[]{:S(2)}) copy-start(bf16[512,128]{1,0:T(8,128)(2,1)} %constant.24.clone.place_ref) | copy-start | bytes 393220
  33.8 5.5 %copy-start.4 = (bf16[64,256]{1,0:T(8,128)(2,1)S(1)}, bf16[64,256]{1,0:T(8,128)(2,1)}, u32[]{:S(2)}) copy-start(bf16[64,256]{1,0:T(8,128)(2,1)} %constant.22.clone.fz_ref) | copy-start | bytes 98308
  33.8 5.5 %collective-permute-start.1 = (f32[2,2,40,128]{3,2,1,0:T(8,128)S(1)}, f32[2,2,40,128]{3,2,1,0:T(8,128)S(1)}, u32[]{:S(2)}, u32[]{:S(2)}) collective-permute-start(f32[2,2,40,128]{3,2,1,0:T(8,128)S(1)} %get-tuple-element.8), channel_id=1, source_target_pairs={{4,0},{8,4},{12,8},{16,12},{20,16},{24,20},{28,24},{32,28},{36,32}... | collective-permute-start | bytes 245768 | tf_op jit(solution)/shard_map/ppermute | solution.py:396
  37.3 12.5 %copy-start.6 = (f32[1,128]{1,0:T(1,128)S(1)}, f32[1,128]{1,0:T(1,128)}, u32[]{:S(2)}) copy-start(f32[1,128]{1,0:T(1,128)} %constant.26.clone.high_ref) | copy-start | bytes 1540
  37.3 12.5 %copy-start.7 = (f32[1,128]{1,0:T(1,128)S(1)}, f32[1,128]{1,0:T(1,128)}, u32[]{:S(2)}) copy-start(f32[1,128]{1,0:T(1,128)} %constant.25.clone.low_ref) | copy-start | bytes 1540
  37.3 28.7 %copy-start = (f32[256,256]{1,0:T(8,128)S(1)}, f32[256,256]{1,0:T(8,128)}, u32[]{:S(2)}) copy-start(f32[256,256]{1,0:T(8,128)} %constant.28.clone.gx_ref) | copy-start | bytes 786436
  37.3 28.7 %copy-start.3 = (f32[128,128]{1,0:T(8,128)S(1)}, f32[128,128]{1,0:T(8,128)}, u32[]{:S(2)}) copy-start(f32[128,128]{1,0:T(8,128)} %constant.29.clone.gzy_ref) | copy-start | bytes 196612
  37.3 28.7 %copy-start.5 = (f32[16,128]{1,0:T(8,128)S(1)}, f32[16,128]{1,0:T(8,128)}, u32[]{:S(2)}) copy-start(f32[16,128]{1,0:T(8,128)} %constant.27.clone.inv_ref) | copy-start | bytes 24580
  43.3 44.9 %copy-start.8 = (f32[256,1024]{1,0:T(8,128)S(1)}, f32[256,1024]{1,0:T(8,128)}, u32[]{:S(2)}) copy-start(f32[256,1024]{1,0:T(8,128)} %constant.32.clone.w_ref) | copy-start | bytes 3145732
  43.3 44.9 %copy-start.9 = (f32[4,16,128]{2,1,0:T(8,128)S(1)}, f32[4,16,128]{2,1,0:T(8,128)}, u32[]{:S(2)}) copy-start(f32[4,16,128]{2,1,0:T(8,128)} %constant.31.clone.ey_ref) | copy-start | bytes 98308
  43.4 44.9 %copy-start.10 = (f32[8,8,128]{2,1,0:T(8,128)S(1)}, f32[8,8,128]{2,1,0:T(8,128)}, u32[]{:S(2)}) copy-start(f32[8,8,128]{2,1,0:T(8,128)} %constant.30.clone.ez_ref) | copy-start | bytes 98308
  43.4 5.6 %collective-permute-start.3 = (f32[24,128]{1,0:T(8,128)S(1)}, f32[24,128]{1,0:T(8,128)S(1)}, u32[]{:S(2)}, u32[]{:S(2)}) collective-permute-start(f32[24,128]{1,0:T(8,128)S(1)} %shard_map.130.p_ref), channel_id=1, source_target_pairs={{4,0},{8,4},{12,8},{16,12},{20,16},{24,20},{28,24},{32,28},{36,32}... | collective-permute-start | bytes 36872 | tf_op jit(solution)/shard_map/ppermute | solution.py:423
  44.8 5.0 %collective-permute-start.2 = (f32[24,128]{1,0:T(8,128)S(1)}, f32[24,128]{1,0:T(8,128)S(1)}, u32[]{:S(2)}, u32[]{:S(2)}) collective-permute-start(f32[24,128]{1,0:T(8,128)S(1)} %shard_map.130.p_ref), channel_id=1, source_target_pairs={{0,4},{4,8},{8,12},{12,16},{16,20},{20,24},{24,28},{28,32},{32,36}... | collective-permute-start | bytes 36872 | tf_op jit(solution)/shard_map/ppermute | solution.py:422
  67.3 24.1 %all-to-all-start.2 = ((f32[16,8,128]{2,1,0:T(8,128)}), f32[16,8,128]{2,1,0:T(8,128)S(1)}, u32[]{:S(2)}, u32[]{:S(2)}) async-start(f32[16,8,128]{2,1,0:T(8,128)} %shard_map.133), calls=%async_computation.2 | async-start | bytes 131072 | tf_op jit(solution)/shard_map/all_to_all | solution.py:437

commit v5 on v4

--- a/solution.py
+++ b/solution.py
@@ -9,6 +9,7 @@
 from jax.sharding import Mesh
 from jax.sharding import PartitionSpec as P
 
+
 RADIUS = 4
 SPACING = 8
 EPS = 1e-05
@@ -31,7 +32,6 @@
 FROM_MIDDLE = sorted(range(STACKS), key=lambda i: abs(2 * i - STACKS))
 WIDE = COLS + 2 * RADIUS
 LANES = 128
-PARTS = 6
 KZ = SLABS + 3
 KY = STRIPS * ROWS // SPACING + 3
 F32 = jnp.float32
@@ -331,28 +331,22 @@
         o_ref[stack] = total
 
 
-def field_kernel(g_ref, ez_ref, ey_ref, inv_ref, w_ref, o_ref):
+def field_kernel(size, g_ref, ez_ref, ey_ref, inv_ref, w_ref, p_ref, o_ref, s_ref, sem):
     ez = ez_ref[2 * lax.axis_index("gz_0") + lax.axis_index("gz_1")]
     ey = ey_ref[2 * lax.axis_index("xy_1") + lax.axis_index("xy_2")]
     rows = [ez[z : z + 1] * ey for z in range(DEPTH)]
     e = jnp.concatenate(rows, axis=0) * inv_ref[pl.ds(lax.axis_index("xy_0"), 1), :]
-    h = dot(e, jnp.concatenate([gathered(g_ref, k) for k in range(3)], axis=0), NT)
-    size = 8 * MEMBERS
-    h = jnp.concatenate([h[:, k * size : (k + 1) * size] for k in range(3)], axis=0)
-    o_ref[...] = dot(h, w_ref[...], NN)
-
-
-def scale_kernel(size, f_ref, p_ref, o_ref, s_ref, sem):
     power = p_ref[0]
     for stack in range(1, STACKS):
         power = power + p_ref[stack]
-    scale = (1.0 / (jnp.sqrt(power / size) + 1e-6))[0:1, 0:1]
-    part = 3 * LANES // PARTS
+    e = e * (1.0 / (jnp.sqrt(power / size) + 1e-6))[0:1, 0:1]
+    h = dot(e, jnp.concatenate([gathered(g_ref, k) for k in range(3)], axis=0), NT)
+    wide = 8 * MEMBERS
     copies = []
-    for i in range(PARTS):
-        at = pl.ds(i * part, part)
-        s_ref[at] = f_ref[at] * scale
-        copies.append(pltpu.make_async_copy(s_ref.at[at], o_ref.at[at], sem.at[i]))
+    for k in range(3):
+        at = pl.ds(k * LANES, LANES)
+        s_ref[at] = dot(h[:, k * wide : (k + 1) * wide], w_ref[...], NN)
+        copies.append(pltpu.make_async_copy(s_ref.at[at], o_ref.at[at], sem.at[k]))
         copies[-1].start()
     for copy in copies:
         copy.wait()
@@ -370,7 +364,7 @@
     )(*args)
 
 
-def shards(fixed, moving):
+def body(fixed, moving):
     tab = tables()
     sds = lambda *shape: jax.ShapeDtypeStruct(shape, F32)
     upward = [(i, i + 1) for i in range(STACKS - 1)]
@@ -437,21 +431,15 @@
     powers = lax.all_to_all(power, "xy_0", 0, 0, axis_index_groups=[FROM_MIDDLE])
     size = float(3 * SLABS * DEPTH * STACKS * STRIPS * ROWS * WIDTH)
     field = call(
-        field_kernel,
+        functools.partial(field_kernel, size),
         sds(3 * LANES, WIDTH),
         numer,
         tab["ez"],
         tab["ey"],
         tab["inverse"],
         tab["wide_x"],
-        flops=1 << 31,
-    )
-    field = call(
-        functools.partial(scale_kernel, size),
-        sds(3 * LANES, WIDTH),
-        field,
         powers,
-        scratch=[pltpu.VMEM((3 * LANES, WIDTH), F32), pltpu.SemaphoreType.DMA((PARTS,))],
+        scratch=[pltpu.VMEM((3 * LANES, WIDTH), F32), pltpu.SemaphoreType.DMA((3,))],
         out_specs=pl.BlockSpec(memory_space=pltpu.HBM),
     )
     return field.reshape(3, DEPTH, ROWS, WIDTH)
@@ -461,5 +449,5 @@
     torus = Mesh(mesh.devices.reshape(4, 2, 16, 2, 2), ("gz_0", "gz_1", "xy_0", "xy_1", "xy_2"))
     placed = (P(GZ, XY, None), P(GZ, XY, None))
     return jax.shard_map(
-        shards, mesh=torus, in_specs=placed, out_specs=P(None, GZ, XY, None), check_vma=False
-    )
+        body, mesh=torus, in_specs=placed, out_specs=P(None, GZ, XY, None), check_vma=False
+    )

time: 93 us -> 92.9 us (level)
  blocking collectives: 45.6 us -> 69.5 us
  starting transfers between devices: 30.3 us -> 9.35 us
  waiting for transfers between devices: 4.77 us -> 2.77 us
  Pallas kernels: 11.7 us -> 10.7 us
    all_to_all x2 -> x3, blocking collectives: 45.6 us -> 69.5 us  [the longest x1 29.5 us: body(): blocks = lax.all_to_all(chunks, PLANE, 0, 0)]
    all_to_all x1 -> x0, starting transfers between devices: 20.9 us -> none  [shards(): lax.all_to_all(power, 'xy_0', 0, 0, axis_index_groups=[FROM_MIDDLE])]
    all_to_all x1 -> x0, waiting for transfers between devices: 2 us -> none  [shards(): lax.all_to_all(power, 'xy_0', 0, 0, axis_index_groups=[FROM_MIDDLE])]
    pallas_call x8 -> x7, Pallas kernels: 11.7 us -> 10.7 us  [call(): pl.pallas_call(kernel, out_shape=shapes, scratch_shapes=list(scratch), co...]
  transfers between devices with their start and end apart: 5 -> 4, of which waited for: 3 -> 2; matrix products, arithmetic and copies ran while one was open for 0% -> 0% of each run, Pallas kernels for 3% -> 2%
where the time goes in v5:
time: 92.9 us; the launch traced here: 92.6 us
  blocking collectives  69.5 us (75%)
  Pallas kernels  10.7 us (12%)
  starting transfers between devices  9.35 us (10%)
  waiting for transfers between devices  2.77 us (3%)
    all_to_all x1, blocking collectives, body(): blocks = lax.all_to_all(chunks, PLANE, 0, 0)  29.5 us
    all_to_all x1, blocking collectives, body(): lax.all_to_all(power, 'xy_0', 0, 0, axis_index_groups=[FROM_MIDDLE])  23.9 us
    all_to_all x1, blocking collectives, body(): numer = lax.all_to_all(copies, PLANE, 0, 0)  16.1 us
    pallas_call x7, Pallas kernels, call(): pl.pallas_call(kernel, out_shape=shapes, scratch_shapes=list(scratch), co...  10.7 us
    ppermute x1, starting transfers between devices, body(): below = lax.ppermute(part, 'xy_0', upward)  4.17 us
    ppermute x1, starting transfers between devices, body(): below = lax.ppermute(up, 'xy_0', upward)  2.33 us
    ppermute x1, waiting for transfers between devices, body(): above = lax.ppermute(down, 'xy_0', downward)  1.96 us
  transfers between devices with their start and end apart: 4, of which 2 were waited for; matrix products, arithmetic and copies ran while one was open for 0% of the time, Pallas kernels for 2%

profile of v5, /device:TPU:1, one launch (start us, length us, event | category | flops | bytes accessed | tf_op | source)
XLA Modules:
  0.0 92.6 jit_solution(12201257987317611585)
XLA Ops:
  0.0 1.7 %shard_map.127 = f32[32,2,40,128]{3,2,1,0:T(8,128)S(1)} custom-call(f32[128,1024]{1,0:T(8,128)} %bitcast.3, f32[128,1024]{1,0:T(8,128)} %bitcast.4), custom_call_target="tpu_custom_call" | custom-call | tf_op jit(solution)/shard_map/pallas_call | solution.py:358
  1.7 29.5 %all_to_all.15.r_ref = f32[32,2,40,128]{3,2,1,0:T(8,128)S(1)} all-to-all(f32[32,2,40,128]{3,2,1,0:T(8,128)S(1)} %shard_map.127), channel_id=1, replica_groups=mesh['gz_0'=4,'gz_1'=2,'xy_0'=16,'xy_1'=2,'xy_2'=2] {'gz_0','gz_1','xy_1..., dimensions={0} | all-to-all | bytes 2621440 | tf_op jit(solution)/shard_map/all_to_all | solution.py:387
  31.2 0.2 shard_map.129
  31.4 2.3 %collective-permute-start = (f32[2,2,40,128]{3,2,1,0:T(8,128)S(1)}, f32[2,2,40,128]{3,2,1,0:T(8,128)S(1)}, u32[]{:S(2)}, u32[]{:S(2)}) collective-permute-start(f32[2,2,40,128]{3,2,1,0:T(8,128)S(1)} %get-tuple-element.7), channel_id=1, source_target_pairs={{0,4},{4,8},{8,12},{12,16},{16,20},{20,24},{24,28},{28,32},{32,36}... | collective-permute-start | bytes 245768 | tf_op jit(solution)/shard_map/ppermute | solution.py:389
  33.8 0.0 copy-start.2
  33.8 0.0 copy-start.3
  33.8 0.0 copy-start.7
  33.8 1.4 %collective-permute-start.1 = (f32[2,2,40,128]{3,2,1,0:T(8,128)S(1)}, f32[2,2,40,128]{3,2,1,0:T(8,128)S(1)}, u32[]{:S(2)}, u32[]{:S(2)}) collective-permute-start(f32[2,2,40,128]{3,2,1,0:T(8,128)S(1)} %get-tuple-element.8), channel_id=1, source_target_pairs={{4,0},{8,4},{12,8},{16,12},{20,16},{24,20},{28,24},{32,28},{36,32}... | collective-permute-start | bytes 245768 | tf_op jit(solution)/shard_map/ppermute | solution.py:390
  35.2 2.0 %shard_map.128.turned = f32[8,8,128,128]{3,2,1,0:T(8,128)S(1)} custom-call(f32[32,2,40,128]{3,2,1,0:T(8,128)S(1)} %all_to_all.15.r_ref), custom_call_target="tpu_custom_call" | custom-call | flops 2147483648 | bytes 1048576 | tf_op jit(solution)/shard_map/pallas_call | solution.py:358
  37.3 0.0 copy-start.9
  37.3 0.0 copy-start.1
  37.3 0.0 copy-start.4
  37.3 0.0 copy-start.8
  37.3 2.0 %collective-permute-done.1.above_ref = f32[2,2,40,128]{3,2,1,0:T(8,128)S(1)} collective-permute-done((f32[2,2,40,128]{3,2,1,0:T(8,128)S(1)}, f32[2,2,40,128]{3,2,1,0:T(8,128)S(1)}, u32[]{:S(2)}, u32[]{:S(2)}) %collective-permute-start.1) | collective-permute-done | bytes 81952 | tf_op jit(solution)/shard_map/ppermute | solution.py:390
  39.3 4.0 %shard_map.130.p_ref = f32[24,128]{1,0:T(8,128)S(1)} custom-call(f32[8,8,128,128]{3,2,1,0:T(8,128)S(1)} %shard_map.128.turned, f32[2,2,40,128]{3,2,1,0:T(8,128)S(1)} %collective-permute-done.below_ref, f32[2,2,40,128]{3,2,1,0:T(8,128)S(1)} %collective-permute-done.1.above_ref, bf16[64,256]{1,0:T(8,128)(2,1)S(1)} %copy-done.7, f32[96,384]{1,0:T(8,128)S(1)} %copy-done.2, ...), custom_call_target="tpu_custom_call" | custom-call | tf_op jit(solution)/shard_map/pallas_call | solution.py:358
  43.3 0.0 copy-start
  43.4 1.4 %collective-permute-start.3 = (f32[24,128]{1,0:T(8,128)S(1)}, f32[24,128]{1,0:T(8,128)S(1)}, u32[]{:S(2)}, u32[]{:S(2)}) collective-permute-start(f32[24,128]{1,0:T(8,128)S(1)} %shard_map.130.p_ref), channel_id=1, source_target_pairs={{4,0},{8,4},{12,8},{16,12},{20,16},{24,20},{28,24},{32,28},{36,32}... | collective-permute-start | bytes 36872 | tf_op jit(solution)/shard_map/ppermute | solution.py:417
  44.8 4.2 %collective-permute-start.2 = (f32[24,128]{1,0:T(8,128)S(1)}, f32[24,128]{1,0:T(8,128)S(1)}, u32[]{:S(2)}, u32[]{:S(2)}) collective-permute-start(f32[24,128]{1,0:T(8,128)S(1)} %shard_map.130.p_ref), channel_id=1, source_target_pairs={{0,4},{4,8},{8,12},{12,16},{16,20},{20,24},{24,28},{28,32},{32,36}... | collective-permute-start | bytes 36872 | tf_op jit(solution)/shard_map/ppermute | solution.py:416
  49.0 0.8 collective-permute-done.2.below_ref
  49.8 0.1 shard_map.131
  49.9 16.1 %all_to_all.16.g_ref = f32[32,24,128]{2,1,0:T(8,128)S(1)} all-to-all(f32[32,24,128]{2,1,0:T(8,128)S(1)} %shard_map.131), channel_id=1, replica_groups=mesh['gz_0'=4,'gz_1'=2,'xy_0'=16,'xy_1'=2,'xy_2'=2] {'gz_0','gz_1','xy_1..., dimensions={0} | all-to-all | bytes 786432 | tf_op jit(solution)/shard_map/all_to_all | solution.py:427
  66.0 0.7 shard_map.132
  66.7 23.9 %all_to_all.17.p_ref = f32[16,8,128]{2,1,0:T(8,128)S(1)} all-to-all(f32[16,8,128]{2,1,0:T(8,128)S(1)} %shard_map.132), channel_id=1, replica_groups={{32,28,36,24,40,20,44,16,48,12,52,8,56,4,60,0},{33,29,37,25,41,21,45,17..., dimensions={0} | all-to-all | bytes 131072 | tf_op jit(solution)/shard_map/all_to_all | solution.py:431
  90.5 2.1 %shard_map.133 = f32[384,1024]{1,0:T(8,128)} custom-call(f32[32,24,128]{2,1,0:T(8,128)S(1)} %all_to_all.16.g_ref, f32[8,8,128]{2,1,0:T(8,128)S(1)} %copy-done.6, f32[4,16,128]{2,1,0:T(8,128)S(1)} %copy-done.5, f32[16,128]{1,0:T(8,128)S(1)} %copy-done.8, f32[256,1024]{1,0:T(8,128)S(1)} %copy-done, f32[16,8,128]{2,1,0:T(8,128)S(1)} %all_to_all.17.p_ref), custom_call_target="tpu_custom_call" | custom-call | tf_op jit(solution)/shard_map/pallas_call | solution.py:358
  (16 shorter events, 0.0 us)
Async XLA Ops:
  31.4 5.9 %collective-permute-start = (f32[2,2,40,128]{3,2,1,0:T(8,128)S(1)}, f32[2,2,40,128]{3,2,1,0:T(8,128)S(1)}, u32[]{:S(2)}, u32[]{:S(2)}) collective-permute-start(f32[2,2,40,128]{3,2,1,0:T(8,128)S(1)} %get-tuple-element.7), channel_id=1, source_target_pairs={{0,4},{4,8},{8,12},{12,16},{16,20},{20,24},{24,28},{28,32},{32,36}... | collective-permute-start | bytes 245768 | tf_op jit(solution)/shard_map/ppermute | solution.py:389
  33.8 5.5 %copy-start.2 = (f32[96,384]{1,0:T(8,128)S(1)}, f32[96,384]{1,0:T(8,128)}, u32[]{:S(2)}) copy-start(f32[96,384]{1,0:T(8,128)} %constant.23.clone.fx_ref) | copy-start | bytes 442372
  33.8 5.5 %copy-start.3 = (bf16[512,128]{1,0:T(8,128)(2,1)S(1)}, bf16[512,128]{1,0:T(8,128)(2,1)}, u32[]{:S(2)}) copy-start(bf16[512,128]{1,0:T(8,128)(2,1)} %constant.24.clone.place_ref) | copy-start | bytes 393220
  33.8 5.5 %copy-start.7 = (bf16[64,256]{1,0:T(8,128)(2,1)S(1)}, bf16[64,256]{1,0:T(8,128)(2,1)}, u32[]{:S(2)}) copy-start(bf16[64,256]{1,0:T(8,128)(2,1)} %constant.22.clone.fz_ref) | copy-start | bytes 98308
  33.8 5.5 %collective-permute-start.1 = (f32[2,2,40,128]{3,2,1,0:T(8,128)S(1)}, f32[2,2,40,128]{3,2,1,0:T(8,128)S(1)}, u32[]{:S(2)}, u32[]{:S(2)}) collective-permute-start(f32[2,2,40,128]{3,2,1,0:T(8,128)S(1)} %get-tuple-element.8), channel_id=1, source_target_pairs={{4,0},{8,4},{12,8},{16,12},{20,16},{24,20},{28,24},{32,28},{36,32}... | collective-permute-start | bytes 245768 | tf_op jit(solution)/shard_map/ppermute | solution.py:390
  37.3 12.5 %copy-start.9 = (f32[1,128]{1,0:T(1,128)S(1)}, f32[1,128]{1,0:T(1,128)}, u32[]{:S(2)}) copy-start(f32[1,128]{1,0:T(1,128)} %constant.26.clone.high_ref) | copy-start | bytes 1540
  37.3 12.5 %copy-start.10 = (f32[1,128]{1,0:T(1,128)S(1)}, f32[1,128]{1,0:T(1,128)}, u32[]{:S(2)}) copy-start(f32[1,128]{1,0:T(1,128)} %constant.25.clone.low_ref) | copy-start | bytes 1540
  37.3 28.7 %copy-start.1 = (f32[256,256]{1,0:T(8,128)S(1)}, f32[256,256]{1,0:T(8,128)}, u32[]{:S(2)}) copy-start(f32[256,256]{1,0:T(8,128)} %constant.28.clone.gx_ref) | copy-start | bytes 786436
  37.3 28.7 %copy-start.4 = (f32[128,128]{1,0:T(8,128)S(1)}, f32[128,128]{1,0:T(8,128)}, u32[]{:S(2)}) copy-start(f32[128,128]{1,0:T(8,128)} %constant.29.clone.gzy_ref) | copy-start | bytes 196612
  37.3 28.7 %copy-start.8 = (f32[16,128]{1,0:T(8,128)S(1)}, f32[16,128]{1,0:T(8,128)}, u32[]{:S(2)}) copy-start(f32[16,128]{1,0:T(8,128)} %constant.27.clone.inv_ref) | copy-start | bytes 24580
  43.3 47.2 %copy-start = (f32[256,1024]{1,0:T(8,128)S(1)}, f32[256,1024]{1,0:T(8,128)}, u32[]{:S(2)}) copy-start(f32[256,1024]{1,0:T(8,128)} %constant.32.clone.w_ref) | copy-start | bytes 3145732
  43.3 47.2 %copy-start.5 = (f32[4,16,128]{2,1,0:T(8,128)S(1)}, f32[4,16,128]{2,1,0:T(8,128)}, u32[]{:S(2)}) copy-start(f32[4,16,128]{2,1,0:T(8,128)} %constant.31.clone.ey_ref) | copy-start | bytes 98308
  43.4 47.2 %copy-start.6 = (f32[8,8,128]{2,1,0:T(8,128)S(1)}, f32[8,8,128]{2,1,0:T(8,128)}, u32[]{:S(2)}) copy-start(f32[8,8,128]{2,1,0:T(8,128)} %constant.30.clone.ez_ref) | copy-start | bytes 98308
  43.4 5.6 %collective-permute-start.3 = (f32[24,128]{1,0:T(8,128)S(1)}, f32[24,128]{1,0:T(8,128)S(1)}, u32[]{:S(2)}, u32[]{:S(2)}) collective-permute-start(f32[24,128]{1,0:T(8,128)S(1)} %shard_map.130.p_ref), channel_id=1, source_target_pairs={{4,0},{8,4},{12,8},{16,12},{20,16},{24,20},{28,24},{32,28},{36,32}... | collective-permute-start | bytes 36872 | tf_op jit(solution)/shard_map/ppermute | solution.py:417
  44.8 5.0 %collective-permute-start.2 = (f32[24,128]{1,0:T(8,128)S(1)}, f32[24,128]{1,0:T(8,128)S(1)}, u32[]{:S(2)}, u32[]{:S(2)}) collective-permute-start(f32[24,128]{1,0:T(8,128)S(1)} %shard_map.130.p_ref), channel_id=1, source_target_pairs={{0,4},{4,8},{8,12},{12,16},{16,20},{20,24},{24,28},{28,32},{32,36}... | collective-permute-start | bytes 36872 | tf_op jit(solution)/shard_map/ppermute | solution.py:416

commit v6 on v4

--- a/solution.py
+++ b/solution.py
@@ -8,6 +8,7 @@
 from jax.experimental.pallas import tpu as pltpu
 from jax.sharding import Mesh
 from jax.sharding import PartitionSpec as P
+
 
 RADIUS = 4
 SPACING = 8
@@ -106,11 +107,16 @@
     ez_l[..., : KZ * KY] = np.repeat(ez, KY, axis=2)
     ey_l[..., : KZ * KY] = np.tile(ey, (1, 1, KZ))
     f = lambda v: np.asarray(v, np.float32)
+
+    def pair(v):
+        high = f(v).astype(jnp.bfloat16)
+        return np.stack([high, (f(v) - high.astype(np.float32)).astype(jnp.bfloat16)])
+
     high_zy = fit_zy.astype(jnp.bfloat16)
     low_zy = (fit_zy - high_zy.astype(np.float32)).astype(jnp.bfloat16)
     fit_zy = np.block([[high_zy, high_zy], [low_zy, np.zeros_like(low_zy)]])
     return dict(
-        fit_zy=fit_zy, place=np.asarray(place, jnp.bfloat16), fit_x=f(fit_x), wide_x=f(wide_x), gram_x=f(gram_x), gram_zy=f(gram_zy),
+        fit_zy=fit_zy, place=np.asarray(place, jnp.bfloat16), fit_x=f(fit_x), wide_x=pair(wide_x), gram_x=pair(gram_x), gram_zy=pair(gram_zy),
         inverse=f(inverse), ez=f(ez_l), ey=f(ey_l), low=f(low), high=f(high),
     )
 
@@ -317,9 +323,9 @@
     halves = [split(part) for part in parts]
     high = jnp.concatenate([h for h, _ in halves], axis=1)
     low = jnp.concatenate([l for _, l in halves], axis=1)
-    gh, gl = split(gx_ref[...])
+    gh, gl = gx_ref[0], gx_ref[1]
     t = mm(gh, high) + mm(gh, low) + mm(gl, high)
-    zh, zl = split(gzy_ref[...])
+    zh, zl = gzy_ref[0], gzy_ref[1]
     zz = jnp.concatenate([zh, zh], axis=0)
     total = jnp.zeros((8, LANES), F32)
     for k, (h, l) in enumerate(halves):
@@ -339,7 +345,9 @@
     h = dot(e, jnp.concatenate([gathered(g_ref, k) for k in range(3)], axis=0), NT)
     size = 8 * MEMBERS
     h = jnp.concatenate([h[:, k * size : (k + 1) * size] for k in range(3)], axis=0)
-    o_ref[...] = dot(h, w_ref[...], NN)
+    hi, lo = split(h)
+    mm = lambda u, v: lax.dot_general(u, v, (NN, ((), ())), preferred_element_type=F32)
+    o_ref[...] = mm(hi, w_ref[0]) + mm(hi, w_ref[1]) + mm(lo, w_ref[0])
 
 
 def scale_kernel(size, f_ref, p_ref, o_ref, s_ref, sem):
@@ -370,7 +378,7 @@
     )(*args)
 
 
-def shards(fixed, moving):
+def body(fixed, moving):
     tab = tables()
     sds = lambda *shape: jax.ShapeDtypeStruct(shape, F32)
     upward = [(i, i + 1) for i in range(STACKS - 1)]
@@ -461,5 +469,5 @@
     torus = Mesh(mesh.devices.reshape(4, 2, 16, 2, 2), ("gz_0", "gz_1", "xy_0", "xy_1", "xy_2"))
     placed = (P(GZ, XY, None), P(GZ, XY, None))
     return jax.shard_map(
-        shards, mesh=torus, in_specs=placed, out_specs=P(None, GZ, XY, None), check_vma=False
-    )
+        body, mesh=torus, in_specs=placed, out_specs=P(None, GZ, XY, None), check_vma=False
+    )

time: 93 us -> 93 us (level)
  no operation moved by 1% of the time
where the time goes in v6:
time: 93 us; the launch traced here: 92.6 us
  blocking collectives  45.6 us (49%)
  starting transfers between devices  30.3 us (33%)
  Pallas kernels  11.7 us (13%)
  waiting for transfers between devices  4.78 us (5%)
    all_to_all x1, blocking collectives, body(): blocks = lax.all_to_all(chunks, PLANE, 0, 0)  29.5 us
    all_to_all x1, starting transfers between devices, body(): lax.all_to_all(power, 'xy_0', 0, 0, axis_index_groups=[FROM_MIDDLE])  20.9 us
    all_to_all x1, blocking collectives, body(): numer = lax.all_to_all(copies, PLANE, 0, 0)  16.1 us
    pallas_call x8, Pallas kernels, call(): pl.pallas_call(kernel, out_shape=shapes, scratch_shapes=list(scratch), co...  11.7 us
    ppermute x1, starting transfers between devices, body(): below = lax.ppermute(part, 'xy_0', upward)  4.17 us
    ppermute x1, starting transfers between devices, body(): below = lax.ppermute(up, 'xy_0', upward)  2.33 us
    all_to_all x1, waiting for transfers between devices, body(): lax.all_to_all(power, 'xy_0', 0, 0, axis_index_groups=[FROM_MIDDLE])  2.01 us
    ppermute x1, waiting for transfers between devices, body(): above = lax.ppermute(down, 'xy_0', downward)  1.96 us
  transfers between devices with their start and end apart: 5, of which 3 were waited for; matrix products, arithmetic and copies ran while one was open for 0% of the time, Pallas kernels for 3%

profile of v6, /device:TPU:1, one launch (start us, length us, event | category | flops | bytes accessed | tf_op | source)
XLA Modules:
  0.0 92.6 jit_solution(6038142182454244245)
XLA Ops:
  0.0 1.7 %shard_map.127 = f32[32,2,40,128]{3,2,1,0:T(8,128)S(1)} custom-call(f32[128,1024]{1,0:T(8,128)} %bitcast.3, f32[128,1024]{1,0:T(8,128)} %bitcast.4), custom_call_target="tpu_custom_call" | custom-call | tf_op jit(solution)/shard_map/pallas_call | solution.py:372
  1.7 29.5 %all_to_all.15.r_ref = f32[32,2,40,128]{3,2,1,0:T(8,128)S(1)} all-to-all(f32[32,2,40,128]{3,2,1,0:T(8,128)S(1)} %shard_map.127), channel_id=1, replica_groups=mesh['gz_0'=4,'gz_1'=2,'xy_0'=16,'xy_1'=2,'xy_2'=2] {'gz_0','gz_1','xy_1..., dimensions={0} | all-to-all | bytes 2621440 | tf_op jit(solution)/shard_map/all_to_all | solution.py:401
  31.2 0.2 shard_map.129
  31.4 2.3 %collective-permute-start = (f32[2,2,40,128]{3,2,1,0:T(8,128)S(1)}, f32[2,2,40,128]{3,2,1,0:T(8,128)S(1)}, u32[]{:S(2)}, u32[]{:S(2)}) collective-permute-start(f32[2,2,40,128]{3,2,1,0:T(8,128)S(1)} %get-tuple-element.7), channel_id=1, source_target_pairs={{0,4},{4,8},{8,12},{12,16},{16,20},{20,24},{24,28},{28,32},{32,36}... | collective-permute-start | bytes 245768 | tf_op jit(solution)/shard_map/ppermute | solution.py:403
  33.8 0.0 copy-start.1
  33.8 0.0 copy-start.2
  33.8 0.0 copy-start.4
  33.8 1.4 %collective-permute-start.1 = (f32[2,2,40,128]{3,2,1,0:T(8,128)S(1)}, f32[2,2,40,128]{3,2,1,0:T(8,128)S(1)}, u32[]{:S(2)}, u32[]{:S(2)}) collective-permute-start(f32[2,2,40,128]{3,2,1,0:T(8,128)S(1)} %get-tuple-element.8), channel_id=1, source_target_pairs={{4,0},{8,4},{12,8},{16,12},{20,16},{24,20},{28,24},{32,28},{36,32}... | collective-permute-start | bytes 245768 | tf_op jit(solution)/shard_map/ppermute | solution.py:404
  35.2 2.0 %shard_map.128.turned = f32[8,8,128,128]{3,2,1,0:T(8,128)S(1)} custom-call(f32[32,2,40,128]{3,2,1,0:T(8,128)S(1)} %all_to_all.15.r_ref), custom_call_target="tpu_custom_call" | custom-call | flops 2147483648 | bytes 1048576 | tf_op jit(solution)/shard_map/pallas_call | solution.py:372
  37.3 0.0 copy-start.6
  37.3 0.0 copy-start
  37.3 0.0 copy-start.3
  37.3 2.0 %collective-permute-done.1.above_ref = f32[2,2,40,128]{3,2,1,0:T(8,128)S(1)} collective-permute-done((f32[2,2,40,128]{3,2,1,0:T(8,128)S(1)}, f32[2,2,40,128]{3,2,1,0:T(8,128)S(1)}, u32[]{:S(2)}, u32[]{:S(2)}) %collective-permute-start.1) | collective-permute-done | bytes 81952 | tf_op jit(solution)/shard_map/ppermute | solution.py:404
  39.3 4.0 %shard_map.130.p_ref = f32[24,128]{1,0:T(8,128)S(1)} custom-call(f32[8,8,128,128]{3,2,1,0:T(8,128)S(1)} %shard_map.128.turned, f32[2,2,40,128]{3,2,1,0:T(8,128)S(1)} %collective-permute-done.below_ref, f32[2,2,40,128]{3,2,1,0:T(8,128)S(1)} %collective-permute-done.1.above_ref, bf16[64,256]{1,0:T(8,128)(2,1)S(1)} %copy-done.4, f32[96,384]{1,0:T(8,128)S(1)} %copy-done.1, ...), custom_call_target="tpu_custom_call" | custom-call | tf_op jit(solution)/shard_map/pallas_call | solution.py:372
  43.4 1.4 %collective-permute-start.3 = (f32[24,128]{1,0:T(8,128)S(1)}, f32[24,128]{1,0:T(8,128)S(1)}, u32[]{:S(2)}, u32[]{:S(2)}) collective-permute-start(f32[24,128]{1,0:T(8,128)S(1)} %shard_map.130.p_ref), channel_id=1, source_target_pairs={{4,0},{8,4},{12,8},{16,12},{20,16},{24,20},{28,24},{32,28},{36,32}... | collective-permute-start | bytes 36872 | tf_op jit(solution)/shard_map/ppermute | solution.py:431
  44.8 4.2 %collective-permute-start.2 = (f32[24,128]{1,0:T(8,128)S(1)}, f32[24,128]{1,0:T(8,128)S(1)}, u32[]{:S(2)}, u32[]{:S(2)}) collective-permute-start(f32[24,128]{1,0:T(8,128)S(1)} %shard_map.130.p_ref), channel_id=1, source_target_pairs={{0,4},{4,8},{8,12},{12,16},{16,20},{20,24},{24,28},{28,32},{32,36}... | collective-permute-start | bytes 36872 | tf_op jit(solution)/shard_map/ppermute | solution.py:430
  49.0 0.8 collective-permute-done.2.below_ref
  49.8 0.1 shard_map.131
  49.9 16.1 %all_to_all.16.g_ref = f32[32,24,128]{2,1,0:T(8,128)S(1)} all-to-all(f32[32,24,128]{2,1,0:T(8,128)S(1)} %shard_map.131), channel_id=1, replica_groups=mesh['gz_0'=4,'gz_1'=2,'xy_0'=16,'xy_1'=2,'xy_2'=2] {'gz_0','gz_1','xy_1..., dimensions={0} | all-to-all | bytes 786432 | tf_op jit(solution)/shard_map/all_to_all | solution.py:441
  66.0 1.3 %shard_map.133 = f32[16,8,128]{2,1,0:T(8,128)} custom-call(f32[32,24,128]{2,1,0:T(8,128)S(1)} %all_to_all.16.g_ref, f32[16,128]{1,0:T(8,128)S(1)} %copy-done.5, bf16[2,256,256]{2,1,0:T(8,128)(2,1)S(1)} %copy-done, bf16[2,128,128]{2,1,0:T(8,128)(2,1)S(1)} %copy-done.3), custom_call_target="tpu_custom_call" | custom-call | tf_op jit(solution)/shard_map/pallas_call | solution.py:372
  67.3 20.9 %all-to-all-start.2 = ((f32[16,8,128]{2,1,0:T(8,128)}), f32[16,8,128]{2,1,0:T(8,128)S(1)}, u32[]{:S(2)}, u32[]{:S(2)}) async-start(f32[16,8,128]{2,1,0:T(8,128)} %shard_map.133), calls=%async_computation.2 | async-start | bytes 131072 | tf_op jit(solution)/shard_map/all_to_all | solution.py:445
  88.2 1.1 %shard_map.132.f_ref = f32[384,1024]{1,0:T(8,128)S(1)} custom-call(f32[32,24,128]{2,1,0:T(8,128)S(1)} %all_to_all.16.g_ref, f32[8,8,128]{2,1,0:T(8,128)S(1)} %copy-done.10, f32[4,16,128]{2,1,0:T(8,128)S(1)} %copy-done.9, f32[16,128]{1,0:T(8,128)S(1)} %copy-done.5, bf16[2,256,1024]{2,1,0:T(8,128)(2,1)S(1)} %copy-done.8), custom_call_target="tpu_custom_call" | custom-call | flops 2147483648 | bytes 1048576 | tf_op jit(solution)/shard_map/pallas_call | solution.py:372
  89.4 2.0 %all-to-all-done.2.p_ref = f32[16,8,128]{2,1,0:T(8,128)S(1)} async-done(((f32[16,8,128]{2,1,0:T(8,128)}), f32[16,8,128]{2,1,0:T(8,128)S(1)}, u32[]{:S(2)}, u32[]{:S(2)}) %all-to-all-start.2) | async-done | bytes 65568 | tf_op jit(solution)/shard_map/all_to_all | solution.py:445
  91.4 1.3 %shard_map.134 = f32[384,1024]{1,0:T(8,128)} custom-call(f32[384,1024]{1,0:T(8,128)S(1)} %shard_map.132.f_ref, f32[16,8,128]{2,1,0:T(8,128)S(1)} %all-to-all-done.2.p_ref), custom_call_target="tpu_custom_call" | custom-call | tf_op jit(solution)/shard_map/pallas_call | solution.py:372
  (18 shorter events, 0.1 us)
Async XLA Ops:
  31.4 5.9 %collective-permute-start = (f32[2,2,40,128]{3,2,1,0:T(8,128)S(1)}, f32[2,2,40,128]{3,2,1,0:T(8,128)S(1)}, u32[]{:S(2)}, u32[]{:S(2)}) collective-permute-start(f32[2,2,40,128]{3,2,1,0:T(8,128)S(1)} %get-tuple-element.7), channel_id=1, source_target_pairs={{0,4},{4,8},{8,12},{12,16},{16,20},{20,24},{24,28},{28,32},{32,36}... | collective-permute-start | bytes 245768 | tf_op jit(solution)/shard_map/ppermute | solution.py:403
  33.8 5.5 %copy-start.1 = (f32[96,384]{1,0:T(8,128)S(1)}, f32[96,384]{1,0:T(8,128)}, u32[]{:S(2)}) copy-start(f32[96,384]{1,0:T(8,128)} %constant.23.clone.fx_ref) | copy-start | bytes 442372
  33.8 5.5 %copy-start.2 = (bf16[512,128]{1,0:T(8,128)(2,1)S(1)}, bf16[512,128]{1,0:T(8,128)(2,1)}, u32[]{:S(2)}) copy-start(bf16[512,128]{1,0:T(8,128)(2,1)} %constant.24.clone.place_ref) | copy-start | bytes 393220
  33.8 5.5 %copy-start.4 = (bf16[64,256]{1,0:T(8,128)(2,1)S(1)}, bf16[64,256]{1,0:T(8,128)(2,1)}, u32[]{:S(2)}) copy-start(bf16[64,256]{1,0:T(8,128)(2,1)} %constant.22.clone.fz_ref) | copy-start | bytes 98308
  33.8 5.5 %collective-permute-start.1 = (f32[2,2,40,128]{3,2,1,0:T(8,128)S(1)}, f32[2,2,40,128]{3,2,1,0:T(8,128)S(1)}, u32[]{:S(2)}, u32[]{:S(2)}) collective-permute-start(f32[2,2,40,128]{3,2,1,0:T(8,128)S(1)} %get-tuple-element.8), channel_id=1, source_target_pairs={{4,0},{8,4},{12,8},{16,12},{20,16},{24,20},{28,24},{32,28},{36,32}... | collective-permute-start | bytes 245768 | tf_op jit(solution)/shard_map/ppermute | solution.py:404
  37.3 12.5 %copy-start.6 = (f32[1,128]{1,0:T(1,128)S(1)}, f32[1,128]{1,0:T(1,128)}, u32[]{:S(2)}) copy-start(f32[1,128]{1,0:T(1,128)} %constant.26.clone.high_ref) | copy-start | bytes 1540
  37.3 12.5 %copy-start.7 = (f32[1,128]{1,0:T(1,128)S(1)}, f32[1,128]{1,0:T(1,128)}, u32[]{:S(2)}) copy-start(f32[1,128]{1,0:T(1,128)} %constant.25.clone.low_ref) | copy-start | bytes 1540
  37.3 28.7 %copy-start = (bf16[2,256,256]{2,1,0:T(8,128)(2,1)S(1)}, bf16[2,256,256]{2,1,0:T(8,128)(2,1)}, u32[]{:S(2)}) copy-start(bf16[2,256,256]{2,1,0:T(8,128)(2,1)} %constant.28.clone.gx_ref) | copy-start | bytes 786436
  37.3 28.7 %copy-start.3 = (bf16[2,128,128]{2,1,0:T(8,128)(2,1)S(1)}, bf16[2,128,128]{2,1,0:T(8,128)(2,1)}, u32[]{:S(2)}) copy-start(bf16[2,128,128]{2,1,0:T(8,128)(2,1)} %constant.29.clone.gzy_ref) | copy-start | bytes 196612
  37.3 28.7 %copy-start.5 = (f32[16,128]{1,0:T(8,128)S(1)}, f32[16,128]{1,0:T(8,128)}, u32[]{:S(2)}) copy-start(f32[16,128]{1,0:T(8,128)} %constant.27.clone.inv_ref) | copy-start | bytes 24580
  43.3 44.9 %copy-start.8 = (bf16[2,256,1024]{2,1,0:T(8,128)(2,1)S(1)}, bf16[2,256,1024]{2,1,0:T(8,128)(2,1)}, u32[]{:S(2)}) copy-start(bf16[2,256,1024]{2,1,0:T(8,128)(2,1)} %constant.32.clone.w_ref) | copy-start | bytes 3145732
  43.3 44.9 %copy-start.9 = (f32[4,16,128]{2,1,0:T(8,128)S(1)}, f32[4,16,128]{2,1,0:T(8,128)}, u32[]{:S(2)}) copy-start(f32[4,16,128]{2,1,0:T(8,128)} %constant.31.clone.ey_ref) | copy-start | bytes 98308
  43.4 44.9 %copy-start.10 = (f32[8,8,128]{2,1,0:T(8,128)S(1)}, f32[8,8,128]{2,1,0:T(8,128)}, u32[]{:S(2)}) copy-start(f32[8,8,128]{2,1,0:T(8,128)} %constant.30.clone.ez_ref) | copy-start | bytes 98308
  43.4 5.6 %collective-permute-start.3 = (f32[24,128]{1,0:T(8,128)S(1)}, f32[24,128]{1,0:T(8,128)S(1)}, u32[]{:S(2)}, u32[]{:S(2)}) collective-permute-start(f32[24,128]{1,0:T(8,128)S(1)} %shard_map.130.p_ref), channel_id=1, source_target_pairs={{4,0},{8,4},{12,8},{16,12},{20,16},{24,20},{28,24},{32,28},{36,32}... | collective-permute-start | bytes 36872 | tf_op jit(solution)/shard_map/ppermute | solution.py:431
  44.8 5.0 %collective-permute-start.2 = (f32[24,128]{1,0:T(8,128)S(1)}, f32[24,128]{1,0:T(8,128)S(1)}, u32[]{:S(2)}, u32[]{:S(2)}) collective-permute-start(f32[24,128]{1,0:T(8,128)S(1)} %shard_map.130.p_ref), channel_id=1, source_target_pairs={{0,4},{4,8},{8,12},{12,16},{16,20},{20,24},{24,28},{28,32},{32,36}... | collective-permute-start | bytes 36872 | tf_op jit(solution)/shard_map/ppermute | solution.py:430
  67.3 24.1 %all-to-all-start.2 = ((f32[16,8,128]{2,1,0:T(8,128)}), f32[16,8,128]{2,1,0:T(8,128)S(1)}, u32[]{:S(2)}, u32[]{:S(2)}) async-start(f32[16,8,128]{2,1,0:T(8,128)} %shard_map.133), calls=%async_computation.2 | async-start | bytes 131072 | tf_op jit(solution)/shard_map/all_to_all | solution.py:445
